TPU v7x, 256 devices: a whole 4x4x8 slice. The times are simulated.
256 devices in a mesh: prow: 16 (over y, x), pcol: 16 (over z, core).
Axes of the slice: x: 4, y: 4, z: 8, core: 2. Of those that a mesh axis runs over, the one named last changes fastest.
Arguments:
- blocked: float32 [16384, 16384], P('prow', 'pcol'), may hold values from -6 to 6, as said below
Outputs:
- factored: float32 [16384, 16384], P('prow', 'pcol')
Inputs may be any that keep to these rules, and one draw needn't show every extreme that they name: blocked is the block-cyclic storage of a symmetric positive definite matrix whose diagonal is at least 1 plus a nonnegative Gram diagonal and whose condition number is below about 40.
All inputs are finite; a program needn't handle non-finite values.
Results may differ from a plain program's by a relative error of at most 0.0003.
Values sent between devices are 32-bit elements.
No kernel may reach another device: no remote copies, remote signals or barrier semaphores. Data moves between devices by JAX's collectives and lax.ppermute only.
A program may use at most 128 MiB of HBM per device.

v0:
```python
import functools

import jax
import jax.numpy as jnp
from jax import lax
from jax.experimental import pallas as pl
from jax.experimental.pallas import tpu as pltpu
from jax.sharding import PartitionSpec as P


BLOCK = 128
STEPS = 8
WIDTH = STEPS * BLOCK
HALF = WIDTH // 2
SIDE = 4
NB = 32
GROUP = 16
CHUNK = 256


bf16 = jnp.bfloat16
f32 = jnp.float32


def split(x):
    hi = x.astype(bf16)
    return hi, (x - hi.astype(f32)).astype(bf16)


def dot(a, b, dims=((1,), (0,))):
    return lax.dot_general(a, b, (dims, ((), ())), preferred_element_type=f32)


def dot_split(a, b, dims=((1,), (0,))):
    return dot(a[0], b[0], dims) + dot(a[1], b[0], dims) + dot(a[0], b[1], dims)


def dot_split_128(a, b):
    (ah, al), (bh, bl) = a, b
    return dot(jnp.concatenate([ah, al], 1), jnp.concatenate([bh, bh], 0)) + dot(ah, bl)


def other_half(k):
    return 14 - k + 2 * (k % 2)


def spread(row):
    return jnp.broadcast_to(row, (8, row.shape[1]))


def factor_tile(work_ref):
    tiles = NB // 8
    sub = lax.broadcasted_iota(jnp.int32, (8, 128), 0)
    for base in range(0, BLOCK, NB):
        rows = [
            [work_ref[base + 8 * t : base + 8 * t + 8, h * 128 : h * 128 + 128] for h in range(2)]
            for t in range(tiles)
        ]
        scale = [None] * tiles
        for first in range(0, NB, GROUP):
            last = first + GROUP
            cols = {
                (j, t): jnp.broadcast_to(rows[t][0][:, base + j : base + j + 1], (8, 128))
                for j in range(first, last)
                for t in range(j // 8, tiles)
            }
            for k in range(first, last, 2):
                tk, rk = divmod(k, 8)
                a = spread(cols[k, tk][rk : rk + 1])
                b = spread(cols[k, tk][rk + 1 : rk + 2])
                c = spread(cols[k + 1, tk][rk + 1 : rk + 2])
                det = a * c - b * b
                inv, ra = 1.0 / det, 1.0 / a
                ai, bi, ci = a * inv, b * inv, c * inv
                r0, r1 = lax.rsqrt(a), lax.rsqrt(det * ra)
                scale[tk] = r0 if rk == 0 else jnp.where(sub == rk, r0, scale[tk])
                scale[tk] = jnp.where(sub == rk + 1, r1, scale[tk])
                p, q = {}, {}
                for t in range(tk + (rk == 6), tiles):
                    p[t] = ci * cols[k, t] - bi * cols[k + 1, t]
                    q[t] = ai * cols[k + 1, t] - bi * cols[k, t]
                    if t == tk:
                        p[t] = jnp.where(sub > rk + 1, p[t], 0.0)
                        q[t] = jnp.where(sub > rk + 1, q[t], 0.0)
                for j in range(k + 2, last):
                    tj, rj = divmod(j, 8)
                    c0 = spread(cols[k, tj][rj : rj + 1])
                    c1 = spread(cols[k + 1, tj][rj : rj + 1])
                    for t in range(tj, tiles):
                        cols[j, t] = cols[j, t] - (p[t] * c0 + q[t] * c1)
                second = jnp.where(sub == rk + 1, b * ra, 0.0)
                for h in range(2):
                    s0 = spread(rows[tk][h][rk : rk + 1])
                    s1 = spread(rows[tk][h][rk + 1 : rk + 2])
                    rows[tk][h] = rows[tk][h] - second * s0
                    for t in p:
                        rows[t][h] = rows[t][h] - (p[t] * s0 + q[t] * s1)
                yield
        done = jnp.concatenate(
            [jnp.concatenate([rows[t][h] * scale[t] for h in range(2)], 1) for t in range(tiles)], 0
        )
        end = base + NB
        work_ref[base:end, :] = done
        if end < BLOCK:
            lh, ll = split(jnp.transpose(done[:, :128])[end:])
            uh, ul = split(done)
            left = jnp.concatenate([lh, lh, ll], 1)
            right = jnp.concatenate([uh, ul, uh], 0)
            work_ref[end:, :] = work_ref[end:, :] - dot(left, right)


def factor_kernel(
    place_ref, w_ref, mh_out, ml_out, corner_ref,
    x_ref, d_ref, mh_ref, ml_ref, work_ref, inv_ref, left_ref, right_ref, rest_ref, sems, out_sems,
):
    copies = []
    for j in range(STEPS):
        for h, slot in enumerate((j, other_half(j))):
            dst = x_ref.at[h * HALF : (h + 1) * HALF, j * BLOCK : (j + 1) * BLOCK]
            copies.append(pltpu.make_async_copy(w_ref.at[slot], dst, sems.at[slot]))
    for copy in copies:
        copy.start()
    for copy in copies:
        copy.wait()
    r = lax.broadcasted_iota(jnp.int32, (BLOCK, BLOCK), 0)
    c = lax.broadcasted_iota(jnp.int32, (BLOCK, BLOCK), 1)
    inv_ref[...] = jnp.zeros_like(inv_ref)
    work_ref[:, :BLOCK] = x_ref[:BLOCK, :BLOCK]

    def finish_row(k, live, b):
        here, at = pl.ds(pl.multiple_of(k * BLOCK, BLOCK), BLOCK), slice(b * BLOCK, (b + 1) * BLOCK)
        old, inverse = x_ref[here, at], inv_ref[...]
        new = jnp.where(k == b, inverse, dot_split_128(split(inverse), split(old)))
        new = jnp.where(live, new, old)
        x_ref[here, at] = new
        hi, lo = split(new)
        right_ref[:BLOCK, at], rest_ref[:, at] = hi, lo
        mh_ref[here, at] = jnp.where(b <= k, hi, jnp.zeros_like(hi))
        ml_ref[here, at] = jnp.where(b <= k, lo, jnp.zeros_like(lo))
        right_ref[BLOCK:, at] = hi
        left_ref[at, :BLOCK], left_ref[at, BLOCK:] = split(jnp.where(live & (b > k), jnp.transpose(new), 0.0))

    def send_row(k):
        here = pl.ds(pl.multiple_of(k * BLOCK, BLOCK), BLOCK)
        return [
            pltpu.make_async_copy(ref.at[here], out.at[here], out_sems.at[part, k])
            for part, (ref, out) in enumerate(((mh_ref, mh_out), (ml_ref, ml_out)))
        ]

    def clear(k, live):
        here = pl.ds(pl.multiple_of(k * BLOCK, BLOCK), BLOCK)
        block = lax.broadcasted_iota(jnp.int32, (WIDTH, BLOCK), 0) // BLOCK
        x_ref[:, here] = jnp.where(live & (block > k), 0.0, x_ref[:, here])

    def trail(m, n):
        at, to = slice(m * BLOCK, (m + 1) * BLOCK), slice(n * 2 * BLOCK, (n + 1) * 2 * BLOCK)
        product = dot(left_ref[at, :], right_ref[:, to]) + dot(left_ref[at, :BLOCK], rest_ref[:, to])
        x_ref[at, to] = x_ref[at, to] - product

    def step(k, _):
        here = pl.ds(pl.multiple_of(k * BLOCK, BLOCK), BLOCK)
        after = pl.ds(pl.multiple_of(jnp.minimum(k + 1, STEPS - 1) * BLOCK, BLOCK), BLOCK)
        work_ref[:, BLOCK:] = jnp.where(r == c, 1.0, 0.0).astype(f32)
        before, live = jnp.maximum(k - 1, 0), k > 0
        others = [functools.partial(finish_row, before, live, b) for b in range(STEPS)]
        others += [functools.partial(clear, before, live)]
        others += [functools.partial(trail, m, n) for n in range(STEPS // 2) for m in range(STEPS)]
        places = BLOCK // 2
        emitted = 0
        for place, _ in enumerate(factor_tile(work_ref)):
            until = -(-len(others) * (place + 1) // places)
            for other in others[emitted:until]:
                other()
            emitted = until

        @pl.when(live)
        def _():
            for copy in send_row(before):
                copy.start()

        d_ref[here, :] = jnp.where(r <= c, work_ref[:, :BLOCK], 0.0)
        inverse = work_ref[:, BLOCK:]
        inv_ref[...] = inverse
        u = dot_split_128(split(inverse), split(x_ref[here, after]))
        work_ref[:, :BLOCK] = x_ref[after, after] - dot_split_128(split(jnp.transpose(u)), split(u))
        return 0

    lax.fori_loop(0, STEPS, step, 0)
    end = slice(WIDTH - BLOCK, WIDTH)
    x_ref[end, :] = dot_split_128(split(inv_ref[...]), split(x_ref[end, :]))
    x_ref[end, end] = inv_ref[...]
    mh_ref[end, :], ml_ref[end, :] = split(x_ref[end, :])
    for copy in send_row(STEPS - 1):
        copy.start()
    row, col = place_ref[0], place_ref[1]
    mine = pl.ds(pl.multiple_of(jnp.minimum(row, STEPS - 1) * BLOCK, BLOCK), BLOCK)
    other = pl.ds(pl.multiple_of(jnp.minimum(col, STEPS - 1) * BLOCK, BLOCK), BLOCK)
    block = jnp.where(row == col, d_ref[mine, :], x_ref[other, mine])
    corner_ref[...] = jnp.where(row >= col, jnp.transpose(block), 0.0)
    for k in range(STEPS):
        for copy in send_row(k):
            copy.wait()


def factor(place, gathered):
    square = lambda dtype: pltpu.VMEM((WIDTH, WIDTH), dtype)
    hbm = pl.BlockSpec(memory_space=pltpu.HBM)
    return pl.pallas_call(
        factor_kernel,
        in_specs=[pl.BlockSpec(memory_space=pltpu.SMEM), hbm],
        out_specs=(hbm, hbm, pl.BlockSpec(memory_space=pltpu.VMEM)),
        out_shape=(
            pltpu.HBM((WIDTH, WIDTH), bf16),
            pltpu.HBM((WIDTH, WIDTH), bf16),
            jax.ShapeDtypeStruct((BLOCK, BLOCK), f32),
        ),
        scratch_shapes=[
            square(f32),
            pltpu.VMEM((WIDTH, BLOCK), f32),
            square(bf16),
            square(bf16),
            pltpu.VMEM((BLOCK, 2 * BLOCK), f32),
            pltpu.VMEM((BLOCK, BLOCK), f32),
            pltpu.VMEM((WIDTH, 2 * BLOCK), bf16),
            pltpu.VMEM((2 * BLOCK, WIDTH), bf16),
            pltpu.VMEM((BLOCK, WIDTH), bf16),
            pltpu.SemaphoreType.DMA((2 * STEPS,)),
            pltpu.SemaphoreType.DMA((2, STEPS)),
        ],
        compiler_params=pltpu.CompilerParams(vmem_limit_bytes=24 * 2**20),
        cost_estimate=pl.CostEstimate(flops=40_000_000_000, bytes_accessed=2**23, transcendentals=0),
        name="factor",
    )(place, gathered)


def apply_kernel(place_ref, mh_hbm, ml_hbm, *refs):
    v_hbm, (ch_hbm, cl_hbm, mh, ml, vh, vl, ch, cl, v_ref, sems) = refs[:SIDE], refs[SIDE:]
    pairs = [(v, v_ref.at[d]) for d, v in enumerate(v_hbm)] + [(mh_hbm, mh), (ml_hbm, ml)]
    copies = [pltpu.make_async_copy(src, dst, sems.at[n]) for n, (src, dst) in enumerate(pairs)]
    for copy in copies:
        copy.start()
    row = place_ref[0]
    my_y, my_x = row // SIDE, row % SIDE
    swapped = jnp.where((my_y == 1) | (my_y == 2), 1, 0)
    for d in range(SIDE):
        copies[d].wait()
        for e in range(2):
            block = SIDE * (e + swapped - 2 * e * swapped) + (my_x + d) % SIDE
            at = pl.ds(pl.multiple_of(block * BLOCK, BLOCK), BLOCK)
            vh[at], vl[at] = split(v_ref[d, e * BLOCK : (e + 1) * BLOCK])
    for copy in copies[SIDE:]:
        copy.wait()
    sent = []
    for n, k in enumerate(range(0, WIDTH, CHUNK)):
        at, upto = slice(k, k + CHUNK), slice(0, k + CHUNK)
        ch[at], cl[at] = split(dot_split((mh[at, upto], ml[at, upto]), (vh[upto], vl[upto])))
        for m, (src, dst) in enumerate(((ch, ch_hbm), (cl, cl_hbm))):
            sent.append(pltpu.make_async_copy(src.at[at], dst.at[at], sems.at[SIDE + 2 + 2 * n + m]))
            sent[-1].start()
    for copy in sent:
        copy.wait()


def apply(place, mh, ml, across):
    hbm = pl.BlockSpec(memory_space=pltpu.HBM)
    square = pltpu.VMEM((WIDTH, WIDTH), bf16)
    return pl.pallas_call(
        apply_kernel,
        in_specs=[pl.BlockSpec(memory_space=pltpu.SMEM)] + [hbm] * (2 + SIDE),
        out_specs=(hbm, hbm),
        out_shape=(pltpu.HBM((WIDTH, WIDTH), bf16), pltpu.HBM((WIDTH, WIDTH), bf16)),
        scratch_shapes=[square] * 6
        + [
            pltpu.VMEM((SIDE, 2 * BLOCK, WIDTH), f32),
            pltpu.SemaphoreType.DMA((SIDE + 2 + 2 * (WIDTH // CHUNK),)),
        ],
        compiler_params=pltpu.CompilerParams(vmem_limit_bytes=28 * 2**20),
        cost_estimate=pl.CostEstimate(flops=6_000_000_000, bytes_accessed=2**23, transcendentals=0),
        name="apply",
    )(place, mh, ml, *across)


def update_kernel(place_ref, a_ref, u_ref, corner_ref, mh_hbm, ml_hbm, ch_hbm, cl_hbm, out_ref, mh, ml, ch, cl, r_ref, sems):
    row, col, step = place_ref[0], place_ref[1], pl.program_id(0)
    pairs = ((mh_hbm, mh), (ml_hbm, ml), (ch_hbm, ch), (cl_hbm, cl))
    copies = [pltpu.make_async_copy(src, dst, sems.at[n]) for n, (src, dst) in enumerate(pairs)]

    @pl.when(step == 0)
    def _():
        for copy in copies:
            copy.start()
        for copy in copies[:2]:
            copy.wait()

    slots = [jnp.where(step < HALF // CHUNK, j, other_half(j) - STEPS) for j in range(STEPS)]
    uh, ul = split(jnp.concatenate([u_ref[s] for s in slots], 1))
    for k in range(0, WIDTH, CHUNK):
        at, upto = slice(k, k + CHUNK), slice(0, k + CHUNK)
        r_ref[:, at] = dot_split((uh[:, upto], ul[:, upto]), (mh[at, upto], ml[at, upto]), ((1,), (1,)))

    @pl.when(step == 0)
    def _():
        for copy in copies[2:]:
            copy.wait()

    out_ref[...] = a_ref[...] - dot_split(split(r_ref[...]), (ch[...], cl[...]))

    @pl.when(col < STEPS)
    def _():
        out_ref[:, :BLOCK] = r_ref[:, pl.ds(pl.multiple_of(col * BLOCK, BLOCK), BLOCK)]

    @pl.when((step == 0) & (row < STEPS))
    def _():
        out_ref[:BLOCK, :] = jnp.zeros((BLOCK, WIDTH), f32)

        @pl.when(col < STEPS)
        def _():
            out_ref[:BLOCK, :BLOCK] = corner_ref[...]


def update(place, blocked, gathered, corner, mh, ml, ch, cl):
    per_half = HALF // CHUNK
    square = pltpu.VMEM((WIDTH, WIDTH), bf16)
    return pl.pallas_call(
        update_kernel,
        grid=(WIDTH // CHUNK,),
        in_specs=[
            pl.BlockSpec(memory_space=pltpu.SMEM),
            pl.BlockSpec((CHUNK, WIDTH), lambda i: (i, 0)),
            pl.BlockSpec((STEPS, CHUNK, BLOCK), lambda i: (i // per_half, i % per_half, 0)),
            pl.BlockSpec((BLOCK, BLOCK), lambda i: (0, 0)),
        ]
        + [pl.BlockSpec(memory_space=pltpu.HBM)] * 4,
        out_specs=pl.BlockSpec((CHUNK, WIDTH), lambda i: (i, 0)),
        out_shape=jax.ShapeDtypeStruct((WIDTH, WIDTH), f32),
        scratch_shapes=[square] * 4 + [pltpu.VMEM((CHUNK, WIDTH), f32), pltpu.SemaphoreType.DMA((4,))],
        compiler_params=pltpu.CompilerParams(vmem_limit_bytes=32 * 2**20),
        name="update",
    )(place, blocked, gathered, corner, mh, ml, ch, cl)


def per_device(blocked):
    rows, cols = lax.axis_size("prow"), lax.axis_size("pcol")
    row, col = lax.axis_index("prow"), lax.axis_index("pcol")
    span = range(STEPS)
    in_hbm = lambda a: pltpu.with_memory_space_constraint(a, pltpu.HBM)

    quarter = BLOCK // 4
    parts = []
    for g in range(4):
        pairs = [
            (i * cols + k, (4 * (i % 4) + g) * cols + (k if i < 4 else other_half(k))) for i in span for k in span
        ]
        parts.append(lax.ppermute(blocked[g * quarter : (g + 1) * quarter, :BLOCK], ("prow", "pcol"), pairs))
    part = (parts[0] + parts[1]) + (parts[2] + parts[3])
    lower = lax.ppermute(blocked[HALF:, :BLOCK], "pcol", [(k, other_half(k)) for k in span])
    strip = lax.all_to_all(jnp.broadcast_to(part, (rows, quarter, BLOCK)), "prow", 0, 0)
    window = lax.all_gather(strip.reshape(HALF, BLOCK), "pcol", axis=0)
    payload = jnp.where(col < STEPS, blocked[:HALF, :BLOCK], lower)

    own = blocked[:BLOCK]
    moves = ([(0, 1), (1, 0)], [(0, 3), (1, 2)], [(0, 2), (1, 3)])
    got = [
        lax.ppermute(own, "prow", [(a * SIDE + x, b * SIDE + x) for a, b in move for x in range(SIDE)])
        for move in moves
    ]
    source = row < 2 * SIDE
    pair = jnp.concatenate([jnp.where(source, own, got[1]), jnp.where(source, got[0], got[2])], 0)
    payload, window, _ = lax.optimization_barrier((payload, window, pair))
    panels = lax.all_gather(payload, "pcol", axis=0)
    across = [pair]
    for d in range(1, SIDE):
        across.append(lax.ppermute(pair, "prow", [(r // SIDE * SIDE + (r + d) % SIDE, r) for r in range(rows)]))

    place = jnp.stack([row, col])
    mh, ml, corner, *across = (in_hbm(v) for v in (*factor(place, in_hbm(window)), *across))
    ch, cl = (in_hbm(v) for v in apply(place, mh, ml, across))
    return update(place, in_hbm(blocked), in_hbm(panels), corner, mh, ml, ch, cl)


def solution(mesh):
    return jax.shard_map(
        per_device,
        mesh=mesh,
        in_specs=(P("prow", "pcol"),),
        out_specs=P("prow", "pcol"),
        check_vma=False,
    )
```

profile of v0, /device:TPU:1, one launch (start us, length us, event | category | flops | bytes accessed | tf_op | source)
XLA Modules:
  0.0 174.0 jit_solution(12606091536638886965)
XLA Ops:
  6.5 0.8 fusion
  7.3 0.7 collective-permute-start.1
  8.0 6.4 %collective-permute-start.2 = (f32[32,128]{1,0:T(8,128)S(1)}, f32[32,128]{1,0:T(8,128)S(1)}, u32[]{:S(2)}, u32[]{:S(2)}) collective-permute-start(f32[32,128]{1,0:T(8,128)S(1)} %get-tuple-element.19), channel_id=1, source_target_pairs={{0,16},{1,17},{2,18},{3,19},{4,20},{5,21},{6,22},{7,23},{16,80},{1... | collective-permute-start | bytes 49160 | tf_op jit(solution)/shard_map/ppermute | solution.py:354
  14.4 4.4 %collective-permute-start.3 = (f32[32,128]{1,0:T(8,128)S(1)}, f32[32,128]{1,0:T(8,128)S(1)}, u32[]{:S(2)}, u32[]{:S(2)}) collective-permute-start(f32[32,128]{1,0:T(8,128)S(1)} %get-tuple-element.21), channel_id=1, source_target_pairs={{0,32},{1,33},{2,34},{3,35},{4,36},{5,37},{6,38},{7,39},{16,96},{1... | collective-permute-start | bytes 49160 | tf_op jit(solution)/shard_map/ppermute | solution.py:354
  18.8 1.3 collective-permute-start.4
  20.2 0.8 collective-permute-done.4
  21.0 18.4 %all_to_all.5 = f32[16,32,128]{2,1,0:T(8,128)} all-to-all(f32[16,32,128]{2,1,0:T(8,128)S(1)} %broadcast_in_dim.3), channel_id=1, replica_groups=mesh['prow'=16,'pcol'=16] {'prow'}, dimensions={0} | all-to-all | bytes 524288 | tf_op jit(solution)/shard_map/all_to_all | solution.py:357
  39.4 0.0 all-gather.6.cloned.1.call-start
  39.5 1.1 slice.27
  40.5 2.5 %collective-permute-start.5 = (f32[128,1024]{1,0:T(8,128)S(1)}, f32[128,1024]{1,0:T(8,128)S(1)}, u32[]{:S(2)}, u32[]{:S(2)}) collective-permute-start(f32[128,1024]{1,0:T(8,128)S(1)} %slice.27), channel_id=1, source_target_pairs={{0,192},{16,208},{32,224},{48,240},{64,128},{80,144},{96,160},{112... | collective-permute-start | bytes 1572872 | tf_op jit(solution)/shard_map/ppermute | solution.py:364
  43.1 1.0 slice.22
  44.0 2.9 %collective-permute-start = (f32[512,128]{1,0:T(8,128)S(1)}, f32[512,128]{1,0:T(8,128)S(1)}, u32[]{:S(2)}, u32[]{:S(2)}) collective-permute-start(f32[512,128]{1,0:T(8,128)S(1)} %slice.22), channel_id=1, source_target_pairs={{0,14},{1,15},{2,12},{3,13},{4,10},{5,11},{6,8},{7,9},{16,30},{17,... | collective-permute-start | bytes 786440 | tf_op jit(solution)/shard_map/ppermute | solution.py:356
  47.0 1.9 %collective-permute-start.6 = (f32[128,1024]{1,0:T(8,128)S(1)}, f32[128,1024]{1,0:T(8,128)S(1)}, u32[]{:S(2)}, u32[]{:S(2)}) collective-permute-start(f32[128,1024]{1,0:T(8,128)S(1)} %slice.27), channel_id=1, source_target_pairs={{0,64},{16,80},{32,96},{48,112},{64,0},{80,16},{96,32},{112,48},{1... | collective-permute-start | bytes 1572872 | tf_op jit(solution)/shard_map/ppermute | solution.py:364
  48.9 1.3 collective-permute-start.7
  50.3 2.8 %collective-permute-done = f32[512,128]{1,0:T(8,128)S(1)} collective-permute-done((f32[512,128]{1,0:T(8,128)S(1)}, f32[512,128]{1,0:T(8,128)S(1)}, u32[]{:S(2)}, u32[]{:S(2)}) %collective-permute-start) | collective-permute-done | bytes 262176 | tf_op jit(solution)/shard_map/ppermute | solution.py:356
  53.1 1.7 slice_select_fusion
  54.8 1.1 broadcast_select_fusion.1
  55.9 2.9 %collective-permute-done.6 = f32[128,1024]{1,0:T(8,128)S(1)} collective-permute-done((f32[128,1024]{1,0:T(8,128)S(1)}, f32[128,1024]{1,0:T(8,128)S(1)}, u32[]{:S(2)}, u32[]{:S(2)}) %collective-permute-start.6) | collective-permute-done | bytes 524320 | tf_op jit(solution)/shard_map/ppermute | solution.py:364
  58.8 9.2 %collective-permute-done.7 = f32[128,1024]{1,0:T(8,128)S(1)} collective-permute-done((f32[128,1024]{1,0:T(8,128)S(1)}, f32[128,1024]{1,0:T(8,128)S(1)}, u32[]{:S(2)}, u32[]{:S(2)}) %collective-permute-start.7) | collective-permute-done | bytes 524320 | tf_op jit(solution)/shard_map/ppermute | solution.py:364
  68.0 0.1 broadcast_select_fusion
  68.0 0.1 pad_maximum_fusion.refs_0_
  68.2 17.4 %all-gather.4.cloned.1.call-done.w_ref = f32[16,512,128]{2,1,0:T(8,128)} async-done(((f32[1,512,128]{2,1,0:T(8,128)}), f32[16,512,128]{2,1,0:T(8,128)}) %all-gather.4.cloned.1.call-update) | async-done | bytes 4194320 | tf_op jit(solution)/shard_map/all_gather | solution.py:358
  85.6 0.1 pad_add_fusion.place_ref
  85.7 0.6 collective-permute-start.10
  86.3 2.1 %collective-permute-start.8 = (f32[256,1024]{1,0:T(8,128)S(1)}, f32[256,1024]{1,0:T(8,128)S(1)}, u32[]{:S(2)}, u32[]{:S(2)}) collective-permute-start(f32[256,1024]{1,0:T(8,128)S(1)} %pad_maximum_fusion.refs_0_), channel_id=1, source_target_pairs={{16,0},{32,16},{48,32},{0,48},{80,64},{96,80},{112,96},{64,112},{1... | collective-permute-start | bytes 3145736 | tf_op jit(solution)/shard_map/ppermute | solution.py:373
  88.4 0.0 collective-permute-start.9
  88.4 37.9 %factor.1 = (bf16[1024,1024]{1,0:T(8,128)(2,1)}, bf16[1024,1024]{1,0:T(8,128)(2,1)}, f32[128,128]{1,0:T(8,128)S(1)}) custom-call(s32[2]{0:T(128)S(1)} %pad_add_fusion.place_ref, f32[16,512,128]{2,1,0:T(8,128)} %all-gather.4.cloned.1.call-done.w_ref), custom_call_target="tpu_custom_call" | custom-call | flops 40000000000 | bytes 8388608 | tf_op jit(solution)/shard_map/factor/pallas_call | solution.py:208
  126.3 0.6 copy-done
  127.0 6.1 %collective-permute-done.9.refs_2_ = f32[256,1024]{1,0:T(8,128)S(1)} collective-permute-done((f32[256,1024]{1,0:T(8,128)S(1)}, f32[256,1024]{1,0:T(8,128)S(1)}, u32[]{:S(2)}, u32[]{:S(2)}) %collective-permute-start.9) | collective-permute-done | bytes 1048608 | tf_op jit(solution)/shard_map/ppermute | solution.py:373
  133.1 1.0 copy-done.4
  134.1 9.4 %apply.1 = (bf16[1024,1024]{1,0:T(8,128)(2,1)}, bf16[1024,1024]{1,0:T(8,128)(2,1)}) custom-call(s32[2]{0:T(128)S(1)} %pad_add_fusion.place_ref, bf16[1024,1024]{1,0:T(8,128)(2,1)} %get-tuple-element.15.mh_hbm, bf16[1024,1024]{1,0:T(8,128)(2,1)} %get-tuple-element.16.ml_hbm, f32[256,1024]{1,0:T(8,128)} %copy-done.1, f32[256,1024]{1,0:T(8,128)} %copy-done.3, ...), custom_call_target="tpu_custom_call" | custom-call | flops 6000000000 | bytes 8388608 | tf_op jit(solution)/shard_map/apply/pallas_call | solution.py:267
  143.5 23.6 %update.1 = f32[1024,1024]{1,0:T(8,128)} custom-call(s32[2]{0:T(128)S(1)} %pad_add_fusion.place_ref, f32[1024,1024]{1,0:T(8,128)} %a_ref.1, f32[16,512,128]{2,1,0:T(8,128)} %bitcast.4, f32[128,128]{1,0:T(8,128)} %copy-done, bf16[1024,1024]{1,0:T(8,128)(2,1)} %get-tuple-element.15.mh_hbm, bf16[1024,1024]{1,0:T(8,128)(2,1)} %get-tuple-element.16.ml_hbm, ...), custom_call_target="tpu_custom_call" | custom-call | tf_op jit(solution)/shard_map/update/pallas_call | solution.py:324
  (20 shorter events, 0.1 us)
Async XLA Ops:
  6.5 79.1 %all-gather.4.cloned.1.call-start = ((), (), s32[]{:S(2)}) async-start(), calls=%async_computation.1 | async-start | bytes 4456448 | tf_op jit(solution)/shard_map/all_gather | solution.py:358
  7.3 12.8 %collective-permute-start.1 = (f32[32,128]{1,0:T(8,128)S(1)}, f32[32,128]{1,0:T(8,128)S(1)}, u32[]{:S(2)}, u32[]{:S(2)}) collective-permute-start(f32[32,128]{1,0:T(8,128)S(1)} %get-tuple-element.22), channel_id=1, source_target_pairs={{0,0},{1,1},{2,2},{3,3},{4,4},{5,5},{6,6},{7,7},{16,64},{17,65},{1... | collective-permute-start | bytes 49160 | tf_op jit(solution)/shard_map/ppermute | solution.py:354
  8.0 12.2 %collective-permute-start.2 = (f32[32,128]{1,0:T(8,128)S(1)}, f32[32,128]{1,0:T(8,128)S(1)}, u32[]{:S(2)}, u32[]{:S(2)}) collective-permute-start(f32[32,128]{1,0:T(8,128)S(1)} %get-tuple-element.19), channel_id=1, source_target_pairs={{0,16},{1,17},{2,18},{3,19},{4,20},{5,21},{6,22},{7,23},{16,80},{1... | collective-permute-start | bytes 49160 | tf_op jit(solution)/shard_map/ppermute | solution.py:354
  14.4 5.7 %collective-permute-start.3 = (f32[32,128]{1,0:T(8,128)S(1)}, f32[32,128]{1,0:T(8,128)S(1)}, u32[]{:S(2)}, u32[]{:S(2)}) collective-permute-start(f32[32,128]{1,0:T(8,128)S(1)} %get-tuple-element.21), channel_id=1, source_target_pairs={{0,32},{1,33},{2,34},{3,35},{4,36},{5,37},{6,38},{7,39},{16,96},{1... | collective-permute-start | bytes 49160 | tf_op jit(solution)/shard_map/ppermute | solution.py:354
  18.8 2.1 %collective-permute-start.4 = (f32[32,128]{1,0:T(8,128)S(1)}, f32[32,128]{1,0:T(8,128)S(1)}, u32[]{:S(2)}, u32[]{:S(2)}) collective-permute-start(f32[32,128]{1,0:T(8,128)S(1)} %get-tuple-element.20), channel_id=1, source_target_pairs={{0,48},{1,49},{2,50},{3,51},{4,52},{5,53},{6,54},{7,55},{16,112},{... | collective-permute-start | bytes 49160 | tf_op jit(solution)/shard_map/ppermute | solution.py:354
  39.4 104.1 %all-gather.6.cloned.1.call-start = ((), (), s32[]{:S(2)}) async-start(), calls=%async_computation.2 | async-start | bytes 4456448 | tf_op jit(solution)/shard_map/all_gather | solution.py:370
  40.5 14.2 %collective-permute-start.5 = (f32[128,1024]{1,0:T(8,128)S(1)}, f32[128,1024]{1,0:T(8,128)S(1)}, u32[]{:S(2)}, u32[]{:S(2)}) collective-permute-start(f32[128,1024]{1,0:T(8,128)S(1)} %slice.27), channel_id=1, source_target_pairs={{0,192},{16,208},{32,224},{48,240},{64,128},{80,144},{96,160},{112... | collective-permute-start | bytes 1572872 | tf_op jit(solution)/shard_map/ppermute | solution.py:364
  44.0 9.0 %collective-permute-start = (f32[512,128]{1,0:T(8,128)S(1)}, f32[512,128]{1,0:T(8,128)S(1)}, u32[]{:S(2)}, u32[]{:S(2)}) collective-permute-start(f32[512,128]{1,0:T(8,128)S(1)} %slice.22), channel_id=1, source_target_pairs={{0,14},{1,15},{2,12},{3,13},{4,10},{5,11},{6,8},{7,9},{16,30},{17,... | collective-permute-start | bytes 786440 | tf_op jit(solution)/shard_map/ppermute | solution.py:356
  47.0 11.8 %collective-permute-start.6 = (f32[128,1024]{1,0:T(8,128)S(1)}, f32[128,1024]{1,0:T(8,128)S(1)}, u32[]{:S(2)}, u32[]{:S(2)}) collective-permute-start(f32[128,1024]{1,0:T(8,128)S(1)} %slice.27), channel_id=1, source_target_pairs={{0,64},{16,80},{32,96},{48,112},{64,0},{80,16},{96,32},{112,48},{1... | collective-permute-start | bytes 1572872 | tf_op jit(solution)/shard_map/ppermute | solution.py:364
  48.9 19.1 %collective-permute-start.7 = (f32[128,1024]{1,0:T(8,128)S(1)}, f32[128,1024]{1,0:T(8,128)S(1)}, u32[]{:S(2)}, u32[]{:S(2)}) collective-permute-start(f32[128,1024]{1,0:T(8,128)S(1)} %slice.27), channel_id=1, source_target_pairs={{0,128},{16,144},{32,160},{48,176},{64,192},{80,208},{96,224},{112... | collective-permute-start | bytes 1572872 | tf_op jit(solution)/shard_map/ppermute | solution.py:364
  68.2 58.2 %copy-start.1 = (f32[256,1024]{1,0:T(8,128)}, f32[256,1024]{1,0:T(8,128)S(1)}, u32[]{:S(2)}) copy-start(f32[256,1024]{1,0:T(8,128)S(1)} %pad_maximum_fusion.refs_0_) | copy-start | bytes 3145732
  85.7 41.3 %collective-permute-start.10 = (f32[256,1024]{1,0:T(8,128)S(1)}, f32[256,1024]{1,0:T(8,128)S(1)}, u32[]{:S(2)}, u32[]{:S(2)}) collective-permute-start(f32[256,1024]{1,0:T(8,128)S(1)} %pad_maximum_fusion.refs_0_), channel_id=1, source_target_pairs={{48,0},{0,16},{16,32},{32,48},{112,64},{64,80},{80,96},{96,112},{1... | collective-permute-start | bytes 3145736 | tf_op jit(solution)/shard_map/ppermute | solution.py:373
  86.3 40.7 %collective-permute-start.8 = (f32[256,1024]{1,0:T(8,128)S(1)}, f32[256,1024]{1,0:T(8,128)S(1)}, u32[]{:S(2)}, u32[]{:S(2)}) collective-permute-start(f32[256,1024]{1,0:T(8,128)S(1)} %pad_maximum_fusion.refs_0_), channel_id=1, source_target_pairs={{16,0},{32,16},{48,32},{0,48},{80,64},{96,80},{112,96},{64,112},{1... | collective-permute-start | bytes 3145736 | tf_op jit(solution)/shard_map/ppermute | solution.py:373
  88.4 44.7 %collective-permute-start.9 = (f32[256,1024]{1,0:T(8,128)S(1)}, f32[256,1024]{1,0:T(8,128)S(1)}, u32[]{:S(2)}, u32[]{:S(2)}) collective-permute-start(f32[256,1024]{1,0:T(8,128)S(1)} %pad_maximum_fusion.refs_0_), channel_id=1, source_target_pairs={{32,0},{48,16},{0,32},{16,48},{96,64},{112,80},{64,96},{80,112},{1... | collective-permute-start | bytes 3145736 | tf_op jit(solution)/shard_map/ppermute | solution.py:373
  126.3 0.7 copy-start
  127.0 6.1 %copy-start.2 = (f32[256,1024]{1,0:T(8,128)}, f32[256,1024]{1,0:T(8,128)S(1)}, u32[]{:S(2)}) copy-start(f32[256,1024]{1,0:T(8,128)S(1)} %collective-permute-done.10.refs_3_) | copy-start | bytes 3145732
  127.0 6.1 %copy-start.3 = (f32[256,1024]{1,0:T(8,128)}, f32[256,1024]{1,0:T(8,128)S(1)}, u32[]{:S(2)}) copy-start(f32[256,1024]{1,0:T(8,128)S(1)} %collective-permute-done.8.refs_1_) | copy-start | bytes 3145732
  133.1 1.0 copy-start.4
Sparse Core Ops, SparseCore 0:
  39.5 46.0 all-gather.3
  87.4 36.9 all-gather.5
where the time goes:
time: 175 us; the launch traced here: 174 us
  Pallas kernels  70.9 us (41%)
  waiting for transfers between devices  39.3 us (22%)
  starting transfers between devices  24.3 us (14%)
  blocking collectives  18.4 us (11%)
  between operations  13.6 us (8%)
  local copies, waits for them, and re-layouts  4.49 us (3%)
  other arithmetic  3.02 us (2%)
    pallas_call x1, Pallas kernels, factor(): pl.pallas_call(factor_kernel, in_specs=[pl.BlockSpec(memory_space=pltpu.S...  37.9 us
    pallas_call x1, Pallas kernels, update(): pl.pallas_call(update_kernel, grid=(WIDTH // CHUNK,), in_specs=[pl.BlockS...  23.6 us
    all_to_all x1, blocking collectives, per_device(): lax.all_to_all(jnp.broadcast_to(part, (rows, quarter, BLOCK)), 'prow', 0, 0)  18.4 us
    all_gather x1, waiting for transfers between devices, per_device(): window = lax.all_gather(strip.reshape(HALF, BLOCK), 'pcol', axis=0)  17.4 us
    ppermute x4, starting transfers between devices, per_device(): lax.ppermute(blocked[g * quarter:(g + 1) * quarter, :BLOCK], ('prow', 'pc...  12.8 us
    ppermute x3, waiting for transfers between devices, per_device(): lax.ppermute(own, 'prow', [(a * SIDE + x, b * SIDE + x) for a, b in move...  12.1 us
    pallas_call x1, Pallas kernels, apply(): pl.pallas_call(apply_kernel, in_specs=[pl.BlockSpec(memory_space=pltpu.SM...  9.43 us
    ppermute x3, waiting for transfers between devices, per_device(): lax.ppermute(pair, 'prow', [(r // SIDE * SIDE + (r + d) % SIDE, r) for r...  6.08 us
  transfers between devices with their start and end apart: 13, of which 6 were waited for; matrix products, arithmetic and copies ran while one was open for 3% of the time, Pallas kernels for 27%

commit v1 on v0

--- a/solution.py
+++ b/solution.py
@@ -110,8 +110,8 @@
 
 
 def factor_kernel(
-    place_ref, w_ref, mh_out, ml_out, corner_ref,
-    x_ref, d_ref, mh_ref, ml_ref, work_ref, inv_ref, left_ref, right_ref, rest_ref, sems, out_sems,
+    place_ref, w_ref, mh_ref, ml_ref, corner_hbm,
+    x_ref, d_ref, corner_ref, work_ref, inv_ref, left_ref, right_ref, rest_ref, sems,
 ):
     copies = []
     for j in range(STEPS):
@@ -139,13 +139,6 @@
         ml_ref[here, at] = jnp.where(b <= k, lo, jnp.zeros_like(lo))
         right_ref[BLOCK:, at] = hi
         left_ref[at, :BLOCK], left_ref[at, BLOCK:] = split(jnp.where(live & (b > k), jnp.transpose(new), 0.0))
-
-    def send_row(k):
-        here = pl.ds(pl.multiple_of(k * BLOCK, BLOCK), BLOCK)
-        return [
-            pltpu.make_async_copy(ref.at[here], out.at[here], out_sems.at[part, k])
-            for part, (ref, out) in enumerate(((mh_ref, mh_out), (ml_ref, ml_out)))
-        ]
 
     def clear(k, live):
         here = pl.ds(pl.multiple_of(k * BLOCK, BLOCK), BLOCK)
@@ -173,11 +166,6 @@
                 other()
             emitted = until
 
-        @pl.when(live)
-        def _():
-            for copy in send_row(before):
-                copy.start()
-
         d_ref[here, :] = jnp.where(r <= c, work_ref[:, :BLOCK], 0.0)
         inverse = work_ref[:, BLOCK:]
         inv_ref[...] = inverse
@@ -190,42 +178,37 @@
     x_ref[end, :] = dot_split_128(split(inv_ref[...]), split(x_ref[end, :]))
     x_ref[end, end] = inv_ref[...]
     mh_ref[end, :], ml_ref[end, :] = split(x_ref[end, :])
-    for copy in send_row(STEPS - 1):
-        copy.start()
     row, col = place_ref[0], place_ref[1]
     mine = pl.ds(pl.multiple_of(jnp.minimum(row, STEPS - 1) * BLOCK, BLOCK), BLOCK)
     other = pl.ds(pl.multiple_of(jnp.minimum(col, STEPS - 1) * BLOCK, BLOCK), BLOCK)
     block = jnp.where(row == col, d_ref[mine, :], x_ref[other, mine])
     corner_ref[...] = jnp.where(row >= col, jnp.transpose(block), 0.0)
-    for k in range(STEPS):
-        for copy in send_row(k):
-            copy.wait()
+    copy = pltpu.make_async_copy(corner_ref, corner_hbm, sems.at[2 * STEPS])
+    copy.start()
+    copy.wait()
 
 
 def factor(place, gathered):
-    square = lambda dtype: pltpu.VMEM((WIDTH, WIDTH), dtype)
-    hbm = pl.BlockSpec(memory_space=pltpu.HBM)
+    vmem, hbm = pl.BlockSpec(memory_space=pltpu.VMEM), pl.BlockSpec(memory_space=pltpu.HBM)
     return pl.pallas_call(
         factor_kernel,
         in_specs=[pl.BlockSpec(memory_space=pltpu.SMEM), hbm],
-        out_specs=(hbm, hbm, pl.BlockSpec(memory_space=pltpu.VMEM)),
+        out_specs=(vmem, vmem, hbm),
         out_shape=(
-            pltpu.HBM((WIDTH, WIDTH), bf16),
-            pltpu.HBM((WIDTH, WIDTH), bf16),
-            jax.ShapeDtypeStruct((BLOCK, BLOCK), f32),
+            jax.ShapeDtypeStruct((WIDTH, WIDTH), bf16),
+            jax.ShapeDtypeStruct((WIDTH, WIDTH), bf16),
+            pltpu.HBM((BLOCK, BLOCK), f32),
         ),
         scratch_shapes=[
-            square(f32),
+            pltpu.VMEM((WIDTH, WIDTH), f32),
             pltpu.VMEM((WIDTH, BLOCK), f32),
-            square(bf16),
-            square(bf16),
+            pltpu.VMEM((BLOCK, BLOCK), f32),
             pltpu.VMEM((BLOCK, 2 * BLOCK), f32),
             pltpu.VMEM((BLOCK, BLOCK), f32),
             pltpu.VMEM((WIDTH, 2 * BLOCK), bf16),
             pltpu.VMEM((2 * BLOCK, WIDTH), bf16),
             pltpu.VMEM((BLOCK, WIDTH), bf16),
-            pltpu.SemaphoreType.DMA((2 * STEPS,)),
-            pltpu.SemaphoreType.DMA((2, STEPS)),
+            pltpu.SemaphoreType.DMA((2 * STEPS + 1,)),
         ],
         compiler_params=pltpu.CompilerParams(vmem_limit_bytes=24 * 2**20),
         cost_estimate=pl.CostEstimate(flops=40_000_000_000, bytes_accessed=2**23, transcendentals=0),
@@ -233,81 +216,67 @@
     )(place, gathered)
 
 
-def apply_kernel(place_ref, mh_hbm, ml_hbm, *refs):
-    v_hbm, (ch_hbm, cl_hbm, mh, ml, vh, vl, ch, cl, v_ref, sems) = refs[:SIDE], refs[SIDE:]
-    pairs = [(v, v_ref.at[d]) for d, v in enumerate(v_hbm)] + [(mh_hbm, mh), (ml_hbm, ml)]
-    copies = [pltpu.make_async_copy(src, dst, sems.at[n]) for n, (src, dst) in enumerate(pairs)]
-    for copy in copies:
-        copy.start()
-    row = place_ref[0]
+def apply_kernel(place_ref, mh, ml, *refs):
+    v_hbm, outs, (vh, vl, v_ref, sems) = refs[:SIDE], refs[SIDE : SIDE + 4], refs[SIDE + 4 :]
+    count = iter(range(sems.shape[0]))
+    copy = lambda src, dst: pltpu.make_async_copy(src, dst, sems.at[next(count)])
+    arriving = [copy(v, v_ref.at[d]) for d, v in enumerate(v_hbm)]
+    for c in arriving:
+        c.start()
+    row, col = place_ref[0], place_ref[1]
+    other = pl.ds(pl.multiple_of(jnp.minimum(col, STEPS - 1) * BLOCK, BLOCK), BLOCK)
+    sent = [copy(m.at[other], out) for m, out in zip((mh, ml), outs[2:])]
+    for c in sent:
+        c.start()
     my_y, my_x = row // SIDE, row % SIDE
     swapped = jnp.where((my_y == 1) | (my_y == 2), 1, 0)
     for d in range(SIDE):
-        copies[d].wait()
+        arriving[d].wait()
         for e in range(2):
             block = SIDE * (e + swapped - 2 * e * swapped) + (my_x + d) % SIDE
             at = pl.ds(pl.multiple_of(block * BLOCK, BLOCK), BLOCK)
             vh[at], vl[at] = split(v_ref[d, e * BLOCK : (e + 1) * BLOCK])
-    for copy in copies[SIDE:]:
-        copy.wait()
-    sent = []
-    for n, k in enumerate(range(0, WIDTH, CHUNK)):
+    for k in reversed(range(0, WIDTH, CHUNK)):
         at, upto = slice(k, k + CHUNK), slice(0, k + CHUNK)
-        ch[at], cl[at] = split(dot_split((mh[at, upto], ml[at, upto]), (vh[upto], vl[upto])))
-        for m, (src, dst) in enumerate(((ch, ch_hbm), (cl, cl_hbm))):
-            sent.append(pltpu.make_async_copy(src.at[at], dst.at[at], sems.at[SIDE + 2 + 2 * n + m]))
+        vh[at], vl[at] = split(dot_split((mh[at, upto], ml[at, upto]), (vh[upto], vl[upto])))
+    for k in range(0, WIDTH, CHUNK):
+        at, on = slice(k, k + CHUNK), slice(k, WIDTH)
+        vh[at], vl[at] = split(dot_split((mh[on, at], ml[on, at]), (vh[on], vl[on]), ((0,), (0,))))
+        for v, out in zip((vh, vl), outs):
+            sent.append(copy(v.at[at], out.at[at]))
             sent[-1].start()
-    for copy in sent:
-        copy.wait()
+    for c in sent:
+        c.wait()
 
 
 def apply(place, mh, ml, across):
-    hbm = pl.BlockSpec(memory_space=pltpu.HBM)
+    vmem, hbm = pl.BlockSpec(memory_space=pltpu.VMEM), pl.BlockSpec(memory_space=pltpu.HBM)
     square = pltpu.VMEM((WIDTH, WIDTH), bf16)
     return pl.pallas_call(
         apply_kernel,
-        in_specs=[pl.BlockSpec(memory_space=pltpu.SMEM)] + [hbm] * (2 + SIDE),
-        out_specs=(hbm, hbm),
-        out_shape=(pltpu.HBM((WIDTH, WIDTH), bf16), pltpu.HBM((WIDTH, WIDTH), bf16)),
-        scratch_shapes=[square] * 6
+        in_specs=[pl.BlockSpec(memory_space=pltpu.SMEM), vmem, vmem] + [hbm] * SIDE,
+        out_specs=(hbm,) * 4,
+        out_shape=tuple(pltpu.HBM((rows, WIDTH), bf16) for rows in (WIDTH, WIDTH, BLOCK, BLOCK)),
+        scratch_shapes=[square, square]
         + [
             pltpu.VMEM((SIDE, 2 * BLOCK, WIDTH), f32),
             pltpu.SemaphoreType.DMA((SIDE + 2 + 2 * (WIDTH // CHUNK),)),
         ],
-        compiler_params=pltpu.CompilerParams(vmem_limit_bytes=28 * 2**20),
-        cost_estimate=pl.CostEstimate(flops=6_000_000_000, bytes_accessed=2**23, transcendentals=0),
+        compiler_params=pltpu.CompilerParams(vmem_limit_bytes=20 * 2**20),
+        cost_estimate=pl.CostEstimate(flops=10_000_000_000, bytes_accessed=2**23, transcendentals=0),
         name="apply",
     )(place, mh, ml, *across)
 
 
-def update_kernel(place_ref, a_ref, u_ref, corner_ref, mh_hbm, ml_hbm, ch_hbm, cl_hbm, out_ref, mh, ml, ch, cl, r_ref, sems):
+def update_kernel(place_ref, a_ref, u_ref, corner_ref, yh_ref, yl_ref, ph_ref, pl_ref, out_ref):
     row, col, step = place_ref[0], place_ref[1], pl.program_id(0)
-    pairs = ((mh_hbm, mh), (ml_hbm, ml), (ch_hbm, ch), (cl_hbm, cl))
-    copies = [pltpu.make_async_copy(src, dst, sems.at[n]) for n, (src, dst) in enumerate(pairs)]
-
-    @pl.when(step == 0)
-    def _():
-        for copy in copies:
-            copy.start()
-        for copy in copies[:2]:
-            copy.wait()
-
     slots = [jnp.where(step < HALF // CHUNK, j, other_half(j) - STEPS) for j in range(STEPS)]
-    uh, ul = split(jnp.concatenate([u_ref[s] for s in slots], 1))
-    for k in range(0, WIDTH, CHUNK):
-        at, upto = slice(k, k + CHUNK), slice(0, k + CHUNK)
-        r_ref[:, at] = dot_split((uh[:, upto], ul[:, upto]), (mh[at, upto], ml[at, upto]), ((1,), (1,)))
-
-    @pl.when(step == 0)
-    def _():
-        for copy in copies[2:]:
-            copy.wait()
-
-    out_ref[...] = a_ref[...] - dot_split(split(r_ref[...]), (ch[...], cl[...]))
+    u = split(jnp.concatenate([u_ref[s] for s in slots], 1))
+    out_ref[...] = a_ref[...] - dot_split(u, (yh_ref[...], yl_ref[...]))
 
     @pl.when(col < STEPS)
     def _():
-        out_ref[:, :BLOCK] = r_ref[:, pl.ds(pl.multiple_of(col * BLOCK, BLOCK), BLOCK)]
+        out_ref[:, :BLOCK] = dot_split(u, (ph_ref[...], pl_ref[...]), ((1,), (1,)))
 
     @pl.when((step == 0) & (row < STEPS))
     def _():
@@ -318,9 +287,9 @@
             out_ref[:BLOCK, :BLOCK] = corner_ref[...]
 
 
-def update(place, blocked, gathered, corner, mh, ml, ch, cl):
+def update(place, blocked, gathered, corner, yh, yl, ph, pl_):
     per_half = HALF // CHUNK
-    square = pltpu.VMEM((WIDTH, WIDTH), bf16)
+    whole = lambda *shape: pl.BlockSpec(shape, lambda i: (0, 0))
     return pl.pallas_call(
         update_kernel,
         grid=(WIDTH // CHUNK,),
@@ -328,15 +297,17 @@
             pl.BlockSpec(memory_space=pltpu.SMEM),
             pl.BlockSpec((CHUNK, WIDTH), lambda i: (i, 0)),
             pl.BlockSpec((STEPS, CHUNK, BLOCK), lambda i: (i // per_half, i % per_half, 0)),
-            pl.BlockSpec((BLOCK, BLOCK), lambda i: (0, 0)),
-        ]
-        + [pl.BlockSpec(memory_space=pltpu.HBM)] * 4,
+            whole(BLOCK, BLOCK),
+            whole(WIDTH, WIDTH),
+            whole(WIDTH, WIDTH),
+            whole(BLOCK, WIDTH),
+            whole(BLOCK, WIDTH),
+        ],
         out_specs=pl.BlockSpec((CHUNK, WIDTH), lambda i: (i, 0)),
         out_shape=jax.ShapeDtypeStruct((WIDTH, WIDTH), f32),
-        scratch_shapes=[square] * 4 + [pltpu.VMEM((CHUNK, WIDTH), f32), pltpu.SemaphoreType.DMA((4,))],
-        compiler_params=pltpu.CompilerParams(vmem_limit_bytes=32 * 2**20),
+        compiler_params=pltpu.CompilerParams(vmem_limit_bytes=28 * 2**20),
         name="update",
-    )(place, blocked, gathered, corner, mh, ml, ch, cl)
+    )(place, blocked, gathered, corner, yh, yl, ph, pl_)
 
 
 def per_device(blocked):
@@ -373,9 +344,9 @@
         across.append(lax.ppermute(pair, "prow", [(r // SIDE * SIDE + (r + d) % SIDE, r) for r in range(rows)]))
 
     place = jnp.stack([row, col])
-    mh, ml, corner, *across = (in_hbm(v) for v in (*factor(place, in_hbm(window)), *across))
-    ch, cl = (in_hbm(v) for v in apply(place, mh, ml, across))
-    return update(place, in_hbm(blocked), in_hbm(panels), corner, mh, ml, ch, cl)
+    mh, ml, corner = factor(place, in_hbm(window))
+    applied = apply(place, mh, ml, [in_hbm(v) for v in across])
+    return update(place, *(in_hbm(v) for v in (blocked, panels, corner, *applied)))
 
 
 def solution(mesh):

time: 175 us -> 169 us (0.966)
  Pallas kernels: 70.9 us -> 64 us
    pallas_call x1, Pallas kernels: 23.6 us -> 13.7 us  [update(): pl.pallas_call(update_kernel, grid=(WIDTH // CHUNK,), in_specs=[pl.BlockS...]
    pallas_call x1, Pallas kernels: 9.43 us -> 12.6 us  [apply(): pl.pallas_call(apply_kernel, in_specs=[pl.BlockSpec(memory_space=pltpu.SM...]
  transfers between devices with their start and end apart: 13 -> 13, of which waited for: 6 -> 6; matrix products, arithmetic and copies ran while one was open for 3% -> 3% of each run, Pallas kernels for 27% -> 30%
where the time goes in v1:
time: 169 us; the launch traced here: 167 us
  Pallas kernels  64 us (38%)
  waiting for transfers between devices  40.2 us (24%)
  starting transfers between devices  24.3 us (14%)
  blocking collectives  18.4 us (11%)
  between operations  13.6 us (8%)
  local copies, waits for them, and re-layouts  3.85 us (2%)
  other arithmetic  3.02 us (2%)
    pallas_call x1, Pallas kernels, factor(): pl.pallas_call(factor_kernel, in_specs=[pl.BlockSpec(memory_space=pltpu.S...  37.7 us
    all_to_all x1, blocking collectives, per_device(): lax.all_to_all(jnp.broadcast_to(part, (rows, quarter, BLOCK)), 'prow', 0, 0)  18.4 us
    all_gather x1, waiting for transfers between devices, per_device(): window = lax.all_gather(strip.reshape(HALF, BLOCK), 'pcol', axis=0)  17.4 us
    pallas_call x1, Pallas kernels, update(): pl.pallas_call(update_kernel, grid=(WIDTH // CHUNK,), in_specs=[pl.BlockS...  13.7 us
    ppermute x4, starting transfers between devices, per_device(): lax.ppermute(blocked[g * quarter:(g + 1) * quarter, :BLOCK], ('prow', 'pc...  12.8 us
    pallas_call x1, Pallas kernels, apply(): pl.pallas_call(apply_kernel, in_specs=[pl.BlockSpec(memory_space=pltpu.SM...  12.6 us
    ppermute x3, waiting for transfers between devices, per_device(): lax.ppermute(own, 'prow', [(a * SIDE + x, b * SIDE + x) for a, b in move...  12.1 us
    ppermute x3, waiting for transfers between devices, per_device(): lax.ppermute(pair, 'prow', [(r // SIDE * SIDE + (r + d) % SIDE, r) for r...  6.9 us
  transfers between devices with their start and end apart: 13, of which 6 were waited for; matrix products, arithmetic and copies ran while one was open for 3% of the time, Pallas kernels for 30%

profile of v1, /device:TPU:1, one launch (start us, length us, event | category | flops | bytes accessed | tf_op | source)
XLA Modules:
  0.0 167.3 jit_solution(1536909411782705436)
XLA Ops:
  6.5 0.8 fusion
  7.3 0.7 collective-permute-start.1
  8.0 6.4 %collective-permute-start.2 = (f32[32,128]{1,0:T(8,128)S(1)}, f32[32,128]{1,0:T(8,128)S(1)}, u32[]{:S(2)}, u32[]{:S(2)}) collective-permute-start(f32[32,128]{1,0:T(8,128)S(1)} %get-tuple-element.23), channel_id=1, source_target_pairs={{0,16},{1,17},{2,18},{3,19},{4,20},{5,21},{6,22},{7,23},{16,80},{1... | collective-permute-start | bytes 49160 | tf_op jit(solution)/shard_map/ppermute | solution.py:325
  14.4 4.4 %collective-permute-start.3 = (f32[32,128]{1,0:T(8,128)S(1)}, f32[32,128]{1,0:T(8,128)S(1)}, u32[]{:S(2)}, u32[]{:S(2)}) collective-permute-start(f32[32,128]{1,0:T(8,128)S(1)} %get-tuple-element.25), channel_id=1, source_target_pairs={{0,32},{1,33},{2,34},{3,35},{4,36},{5,37},{6,38},{7,39},{16,96},{1... | collective-permute-start | bytes 49160 | tf_op jit(solution)/shard_map/ppermute | solution.py:325
  18.8 1.3 collective-permute-start.4
  20.2 0.8 collective-permute-done.4
  21.0 18.4 %all_to_all.5 = f32[16,32,128]{2,1,0:T(8,128)} all-to-all(f32[16,32,128]{2,1,0:T(8,128)S(1)} %broadcast_in_dim.3), channel_id=1, replica_groups=mesh['prow'=16,'pcol'=16] {'prow'}, dimensions={0} | all-to-all | bytes 524288 | tf_op jit(solution)/shard_map/all_to_all | solution.py:328
  39.4 0.0 all-gather.6.cloned.1.call-start
  39.5 1.1 slice.27
  40.5 2.5 %collective-permute-start.5 = (f32[128,1024]{1,0:T(8,128)S(1)}, f32[128,1024]{1,0:T(8,128)S(1)}, u32[]{:S(2)}, u32[]{:S(2)}) collective-permute-start(f32[128,1024]{1,0:T(8,128)S(1)} %slice.27), channel_id=1, source_target_pairs={{0,192},{16,208},{32,224},{48,240},{64,128},{80,144},{96,160},{112... | collective-permute-start | bytes 1572872 | tf_op jit(solution)/shard_map/ppermute | solution.py:335
  43.1 1.0 slice.22
  44.0 2.9 %collective-permute-start = (f32[512,128]{1,0:T(8,128)S(1)}, f32[512,128]{1,0:T(8,128)S(1)}, u32[]{:S(2)}, u32[]{:S(2)}) collective-permute-start(f32[512,128]{1,0:T(8,128)S(1)} %slice.22), channel_id=1, source_target_pairs={{0,14},{1,15},{2,12},{3,13},{4,10},{5,11},{6,8},{7,9},{16,30},{17,... | collective-permute-start | bytes 786440 | tf_op jit(solution)/shard_map/ppermute | solution.py:327
  47.0 1.9 %collective-permute-start.6 = (f32[128,1024]{1,0:T(8,128)S(1)}, f32[128,1024]{1,0:T(8,128)S(1)}, u32[]{:S(2)}, u32[]{:S(2)}) collective-permute-start(f32[128,1024]{1,0:T(8,128)S(1)} %slice.27), channel_id=1, source_target_pairs={{0,64},{16,80},{32,96},{48,112},{64,0},{80,16},{96,32},{112,48},{1... | collective-permute-start | bytes 1572872 | tf_op jit(solution)/shard_map/ppermute | solution.py:335
  48.9 1.3 collective-permute-start.7
  50.3 2.8 %collective-permute-done = f32[512,128]{1,0:T(8,128)S(1)} collective-permute-done((f32[512,128]{1,0:T(8,128)S(1)}, f32[512,128]{1,0:T(8,128)S(1)}, u32[]{:S(2)}, u32[]{:S(2)}) %collective-permute-start) | collective-permute-done | bytes 262176 | tf_op jit(solution)/shard_map/ppermute | solution.py:327
  53.1 1.7 slice_select_fusion
  54.8 1.1 broadcast_select_fusion.1
  55.9 2.9 %collective-permute-done.6 = f32[128,1024]{1,0:T(8,128)S(1)} collective-permute-done((f32[128,1024]{1,0:T(8,128)S(1)}, f32[128,1024]{1,0:T(8,128)S(1)}, u32[]{:S(2)}, u32[]{:S(2)}) %collective-permute-start.6) | collective-permute-done | bytes 524320 | tf_op jit(solution)/shard_map/ppermute | solution.py:335
  58.8 9.2 %collective-permute-done.7 = f32[128,1024]{1,0:T(8,128)S(1)} collective-permute-done((f32[128,1024]{1,0:T(8,128)S(1)}, f32[128,1024]{1,0:T(8,128)S(1)}, u32[]{:S(2)}, u32[]{:S(2)}) %collective-permute-start.7) | collective-permute-done | bytes 524320 | tf_op jit(solution)/shard_map/ppermute | solution.py:335
  68.0 0.1 broadcast_select_fusion
  68.0 0.1 pad_maximum_fusion.refs_0_
  68.2 17.4 %all-gather.4.cloned.1.call-done.w_ref = f32[16,512,128]{2,1,0:T(8,128)} async-done(((f32[1,512,128]{2,1,0:T(8,128)}), f32[16,512,128]{2,1,0:T(8,128)}) %all-gather.4.cloned.1.call-update) | async-done | bytes 4194320 | tf_op jit(solution)/shard_map/all_gather | solution.py:329
  85.6 0.1 pad_add_fusion.place_ref
  85.7 0.6 collective-permute-start.10
  86.3 2.1 %collective-permute-start.8 = (f32[256,1024]{1,0:T(8,128)S(1)}, f32[256,1024]{1,0:T(8,128)S(1)}, u32[]{:S(2)}, u32[]{:S(2)}) collective-permute-start(f32[256,1024]{1,0:T(8,128)S(1)} %pad_maximum_fusion.refs_0_), channel_id=1, source_target_pairs={{16,0},{32,16},{48,32},{0,48},{80,64},{96,80},{112,96},{64,112},{1... | collective-permute-start | bytes 3145736 | tf_op jit(solution)/shard_map/ppermute | solution.py:344
  88.4 0.0 collective-permute-start.9
  88.4 37.7 %factor.1 = (bf16[1024,1024]{1,0:T(8,128)(2,1)S(1)}, bf16[1024,1024]{1,0:T(8,128)(2,1)S(1)}, f32[128,128]{1,0:T(8,128)}) custom-call(s32[2]{0:T(128)S(1)} %pad_add_fusion.place_ref, f32[16,512,128]{2,1,0:T(8,128)} %all-gather.4.cloned.1.call-done.w_ref), custom_call_target="tpu_custom_call" | custom-call | flops 40000000000 | bytes 8388608 | tf_op jit(solution)/shard_map/factor/pallas_call | solution.py:193
  126.2 6.9 %collective-permute-done.9.refs_2_ = f32[256,1024]{1,0:T(8,128)S(1)} collective-permute-done((f32[256,1024]{1,0:T(8,128)S(1)}, f32[256,1024]{1,0:T(8,128)S(1)}, u32[]{:S(2)}, u32[]{:S(2)}) %collective-permute-start.9) | collective-permute-done | bytes 1048608 | tf_op jit(solution)/shard_map/ppermute | solution.py:344
  133.1 1.0 copy-done.3
  134.1 12.6 %apply.1 = (bf16[1024,1024]{1,0:T(8,128)(2,1)}, bf16[1024,1024]{1,0:T(8,128)(2,1)}, bf16[128,1024]{1,0:T(8,128)(2,1)}, bf16[128,1024]{1,0:T(8,128)(2,1)}) custom-call(s32[2]{0:T(128)S(1)} %pad_add_fusion.place_ref, bf16[1024,1024]{1,0:T(8,128)(2,1)S(1)} %get-tuple-element.17.mh, bf16[1024,1024]{1,0:T(8,128)(2,1)S(1)} %get-tuple-element.18.ml, ...), custom_call_target="tpu_custom_call" | custom-call | flops 10000000000 | bytes 8388608 | tf_op jit(solution)/shard_map/apply/pallas_call | solution.py:255
  146.7 0.0 all-gather.6.cloned.1.call-done
  146.7 13.7 %update.1 = f32[1024,1024]{1,0:T(8,128)} custom-call(s32[2]{0:T(128)S(1)} %pad_add_fusion.place_ref, f32[1024,1024]{1,0:T(8,128)} %a_ref.1, f32[16,512,128]{2,1,0:T(8,128)} %bitcast.4, f32[128,128]{1,0:T(8,128)} %get-tuple-element.16.corner_ref, bf16[1024,1024]{1,0:T(8,128)(2,1)} %get-tuple-element.19.yh_ref, bf16[1024,1024]{1,0:T(8,128)(2,1)} %get-tuple-element.20.yl_ref, ...), custom_call_target="tpu_custom_call" | custom-call | tf_op jit(solution)/shard_map/update/pallas_call | solution.py:293
  (18 shorter events, 0.1 us)
Async XLA Ops:
  6.5 79.1 %all-gather.4.cloned.1.call-start = ((), (), s32[]{:S(2)}) async-start(), calls=%async_computation.1 | async-start | bytes 4456448 | tf_op jit(solution)/shard_map/all_gather | solution.py:329
  7.3 12.8 %collective-permute-start.1 = (f32[32,128]{1,0:T(8,128)S(1)}, f32[32,128]{1,0:T(8,128)S(1)}, u32[]{:S(2)}, u32[]{:S(2)}) collective-permute-start(f32[32,128]{1,0:T(8,128)S(1)} %get-tuple-element.26), channel_id=1, source_target_pairs={{0,0},{1,1},{2,2},{3,3},{4,4},{5,5},{6,6},{7,7},{16,64},{17,65},{1... | collective-permute-start | bytes 49160 | tf_op jit(solution)/shard_map/ppermute | solution.py:325
  8.0 12.2 %collective-permute-start.2 = (f32[32,128]{1,0:T(8,128)S(1)}, f32[32,128]{1,0:T(8,128)S(1)}, u32[]{:S(2)}, u32[]{:S(2)}) collective-permute-start(f32[32,128]{1,0:T(8,128)S(1)} %get-tuple-element.23), channel_id=1, source_target_pairs={{0,16},{1,17},{2,18},{3,19},{4,20},{5,21},{6,22},{7,23},{16,80},{1... | collective-permute-start | bytes 49160 | tf_op jit(solution)/shard_map/ppermute | solution.py:325
  14.4 5.7 %collective-permute-start.3 = (f32[32,128]{1,0:T(8,128)S(1)}, f32[32,128]{1,0:T(8,128)S(1)}, u32[]{:S(2)}, u32[]{:S(2)}) collective-permute-start(f32[32,128]{1,0:T(8,128)S(1)} %get-tuple-element.25), channel_id=1, source_target_pairs={{0,32},{1,33},{2,34},{3,35},{4,36},{5,37},{6,38},{7,39},{16,96},{1... | collective-permute-start | bytes 49160 | tf_op jit(solution)/shard_map/ppermute | solution.py:325
  18.8 2.1 %collective-permute-start.4 = (f32[32,128]{1,0:T(8,128)S(1)}, f32[32,128]{1,0:T(8,128)S(1)}, u32[]{:S(2)}, u32[]{:S(2)}) collective-permute-start(f32[32,128]{1,0:T(8,128)S(1)} %get-tuple-element.24), channel_id=1, source_target_pairs={{0,48},{1,49},{2,50},{3,51},{4,52},{5,53},{6,54},{7,55},{16,112},{... | collective-permute-start | bytes 49160 | tf_op jit(solution)/shard_map/ppermute | solution.py:325
  39.4 107.3 %all-gather.6.cloned.1.call-start = ((), (), s32[]{:S(2)}) async-start(), calls=%async_computation.2 | async-start | bytes 4456448 | tf_op jit(solution)/shard_map/all_gather | solution.py:341
  40.5 14.2 %collective-permute-start.5 = (f32[128,1024]{1,0:T(8,128)S(1)}, f32[128,1024]{1,0:T(8,128)S(1)}, u32[]{:S(2)}, u32[]{:S(2)}) collective-permute-start(f32[128,1024]{1,0:T(8,128)S(1)} %slice.27), channel_id=1, source_target_pairs={{0,192},{16,208},{32,224},{48,240},{64,128},{80,144},{96,160},{112... | collective-permute-start | bytes 1572872 | tf_op jit(solution)/shard_map/ppermute | solution.py:335
  44.0 9.0 %collective-permute-start = (f32[512,128]{1,0:T(8,128)S(1)}, f32[512,128]{1,0:T(8,128)S(1)}, u32[]{:S(2)}, u32[]{:S(2)}) collective-permute-start(f32[512,128]{1,0:T(8,128)S(1)} %slice.22), channel_id=1, source_target_pairs={{0,14},{1,15},{2,12},{3,13},{4,10},{5,11},{6,8},{7,9},{16,30},{17,... | collective-permute-start | bytes 786440 | tf_op jit(solution)/shard_map/ppermute | solution.py:327
  47.0 11.8 %collective-permute-start.6 = (f32[128,1024]{1,0:T(8,128)S(1)}, f32[128,1024]{1,0:T(8,128)S(1)}, u32[]{:S(2)}, u32[]{:S(2)}) collective-permute-start(f32[128,1024]{1,0:T(8,128)S(1)} %slice.27), channel_id=1, source_target_pairs={{0,64},{16,80},{32,96},{48,112},{64,0},{80,16},{96,32},{112,48},{1... | collective-permute-start | bytes 1572872 | tf_op jit(solution)/shard_map/ppermute | solution.py:335
  48.9 19.1 %collective-permute-start.7 = (f32[128,1024]{1,0:T(8,128)S(1)}, f32[128,1024]{1,0:T(8,128)S(1)}, u32[]{:S(2)}, u32[]{:S(2)}) collective-permute-start(f32[128,1024]{1,0:T(8,128)S(1)} %slice.27), channel_id=1, source_target_pairs={{0,128},{16,144},{32,160},{48,176},{64,192},{80,208},{96,224},{112... | collective-permute-start | bytes 1572872 | tf_op jit(solution)/shard_map/ppermute | solution.py:335
  68.2 58.0 %copy-start = (f32[256,1024]{1,0:T(8,128)}, f32[256,1024]{1,0:T(8,128)S(1)}, u32[]{:S(2)}) copy-start(f32[256,1024]{1,0:T(8,128)S(1)} %pad_maximum_fusion.refs_0_) | copy-start | bytes 3145732
  85.7 40.4 %collective-permute-start.10 = (f32[256,1024]{1,0:T(8,128)S(1)}, f32[256,1024]{1,0:T(8,128)S(1)}, u32[]{:S(2)}, u32[]{:S(2)}) collective-permute-start(f32[256,1024]{1,0:T(8,128)S(1)} %pad_maximum_fusion.refs_0_), channel_id=1, source_target_pairs={{48,0},{0,16},{16,32},{32,48},{112,64},{64,80},{80,96},{96,112},{1... | collective-permute-start | bytes 3145736 | tf_op jit(solution)/shard_map/ppermute | solution.py:344
  86.3 39.9 %collective-permute-start.8 = (f32[256,1024]{1,0:T(8,128)S(1)}, f32[256,1024]{1,0:T(8,128)S(1)}, u32[]{:S(2)}, u32[]{:S(2)}) collective-permute-start(f32[256,1024]{1,0:T(8,128)S(1)} %pad_maximum_fusion.refs_0_), channel_id=1, source_target_pairs={{16,0},{32,16},{48,32},{0,48},{80,64},{96,80},{112,96},{64,112},{1... | collective-permute-start | bytes 3145736 | tf_op jit(solution)/shard_map/ppermute | solution.py:344
  88.4 44.7 %collective-permute-start.9 = (f32[256,1024]{1,0:T(8,128)S(1)}, f32[256,1024]{1,0:T(8,128)S(1)}, u32[]{:S(2)}, u32[]{:S(2)}) collective-permute-start(f32[256,1024]{1,0:T(8,128)S(1)} %pad_maximum_fusion.refs_0_), channel_id=1, source_target_pairs={{32,0},{48,16},{0,32},{16,48},{96,64},{112,80},{64,96},{80,112},{1... | collective-permute-start | bytes 3145736 | tf_op jit(solution)/shard_map/ppermute | solution.py:344
  126.2 6.9 %copy-start.1 = (f32[256,1024]{1,0:T(8,128)}, f32[256,1024]{1,0:T(8,128)S(1)}, u32[]{:S(2)}) copy-start(f32[256,1024]{1,0:T(8,128)S(1)} %collective-permute-done.10.refs_3_) | copy-start | bytes 3145732
  126.2 6.9 %copy-start.2 = (f32[256,1024]{1,0:T(8,128)}, f32[256,1024]{1,0:T(8,128)S(1)}, u32[]{:S(2)}) copy-start(f32[256,1024]{1,0:T(8,128)S(1)} %collective-permute-done.8.refs_1_) | copy-start | bytes 3145732
  133.1 1.0 copy-start.3
Sparse Core Ops, SparseCore 0:
  39.5 46.0 all-gather.3
  87.4 37.0 all-gather.5

commit v2 on v1

--- a/solution.py
+++ b/solution.py
@@ -71,30 +71,32 @@
                 c = spread(cols[k + 1, tk][rk + 1 : rk + 2])
                 det = a * c - b * b
                 inv, ra = 1.0 / det, 1.0 / a
-                ai, bi, ci = a * inv, b * inv, c * inv
                 r0, r1 = lax.rsqrt(a), lax.rsqrt(det * ra)
                 scale[tk] = r0 if rk == 0 else jnp.where(sub == rk, r0, scale[tk])
                 scale[tk] = jnp.where(sub == rk + 1, r1, scale[tk])
                 p, q = {}, {}
                 for t in range(tk + (rk == 6), tiles):
-                    p[t] = ci * cols[k, t] - bi * cols[k + 1, t]
-                    q[t] = ai * cols[k + 1, t] - bi * cols[k, t]
-                    if t == tk:
-                        p[t] = jnp.where(sub > rk + 1, p[t], 0.0)
-                        q[t] = jnp.where(sub > rk + 1, q[t], 0.0)
+                    p[t] = c * cols[k, t] - b * cols[k + 1, t]
+                    q[t] = a * cols[k + 1, t] - b * cols[k, t]
+                pd, qd = {t: v * inv for t, v in p.items()}, {t: v * inv for t, v in q.items()}
                 for j in range(k + 2, last):
                     tj, rj = divmod(j, 8)
                     c0 = spread(cols[k, tj][rj : rj + 1])
                     c1 = spread(cols[k + 1, tj][rj : rj + 1])
                     for t in range(tj, tiles):
-                        cols[j, t] = cols[j, t] - (p[t] * c0 + q[t] * c1)
+                        if j < k + 4:
+                            cols[j, t] = cols[j, t] - (p[t] * c0 + q[t] * c1) * inv
+                        else:
+                            cols[j, t] = cols[j, t] - (pd[t] * c0 + qd[t] * c1)
+                if tk in pd:
+                    pd[tk], qd[tk] = (jnp.where(sub > rk + 1, v[tk], 0.0) for v in (pd, qd))
                 second = jnp.where(sub == rk + 1, b * ra, 0.0)
                 for h in range(2):
                     s0 = spread(rows[tk][h][rk : rk + 1])
                     s1 = spread(rows[tk][h][rk + 1 : rk + 2])
                     rows[tk][h] = rows[tk][h] - second * s0
-                    for t in p:
-                        rows[t][h] = rows[t][h] - (p[t] * s0 + q[t] * s1)
+                    for t in pd:
+                        rows[t][h] = rows[t][h] - (pd[t] * s0 + qd[t] * s1)
                 yield
         done = jnp.concatenate(
             [jnp.concatenate([rows[t][h] * scale[t] for h in range(2)], 1) for t in range(tiles)], 0
@@ -110,8 +112,8 @@
 
 
 def factor_kernel(
-    place_ref, w_ref, mh_ref, ml_ref, corner_hbm,
-    x_ref, d_ref, corner_ref, work_ref, inv_ref, left_ref, right_ref, rest_ref, sems,
+    place_ref, w_ref, mh_ref, ml_ref, corner_ref,
+    x_ref, d_ref, work_ref, inv_ref, left_ref, right_ref, rest_ref, sems,
 ):
     copies = []
     for j in range(STEPS):
@@ -120,60 +122,64 @@
             copies.append(pltpu.make_async_copy(w_ref.at[slot], dst, sems.at[slot]))
     for copy in copies:
         copy.start()
-    for copy in copies:
-        copy.wait()
+    copies[0].wait()
     r = lax.broadcasted_iota(jnp.int32, (BLOCK, BLOCK), 0)
     c = lax.broadcasted_iota(jnp.int32, (BLOCK, BLOCK), 1)
-    inv_ref[...] = jnp.zeros_like(inv_ref)
     work_ref[:, :BLOCK] = x_ref[:BLOCK, :BLOCK]
 
-    def finish_row(k, live, b):
+    def finish_row(k, b):
         here, at = pl.ds(pl.multiple_of(k * BLOCK, BLOCK), BLOCK), slice(b * BLOCK, (b + 1) * BLOCK)
         old, inverse = x_ref[here, at], inv_ref[...]
         new = jnp.where(k == b, inverse, dot_split_128(split(inverse), split(old)))
-        new = jnp.where(live, new, old)
         x_ref[here, at] = new
         hi, lo = split(new)
         right_ref[:BLOCK, at], rest_ref[:, at] = hi, lo
         mh_ref[here, at] = jnp.where(b <= k, hi, jnp.zeros_like(hi))
         ml_ref[here, at] = jnp.where(b <= k, lo, jnp.zeros_like(lo))
         right_ref[BLOCK:, at] = hi
-        left_ref[at, :BLOCK], left_ref[at, BLOCK:] = split(jnp.where(live & (b > k), jnp.transpose(new), 0.0))
-
-    def clear(k, live):
+        left_ref[at, :BLOCK], left_ref[at, BLOCK:] = split(jnp.where(b > k, jnp.transpose(new), 0.0))
+
+    def clear(k):
         here = pl.ds(pl.multiple_of(k * BLOCK, BLOCK), BLOCK)
         block = lax.broadcasted_iota(jnp.int32, (WIDTH, BLOCK), 0) // BLOCK
-        x_ref[:, here] = jnp.where(live & (block > k), 0.0, x_ref[:, here])
+        x_ref[:, here] = jnp.where(block > k, 0.0, x_ref[:, here])
 
     def trail(m, n):
         at, to = slice(m * BLOCK, (m + 1) * BLOCK), slice(n * 2 * BLOCK, (n + 1) * 2 * BLOCK)
         product = dot(left_ref[at, :], right_ref[:, to]) + dot(left_ref[at, :BLOCK], rest_ref[:, to])
         x_ref[at, to] = x_ref[at, to] - product
 
-    def step(k, _):
-        here = pl.ds(pl.multiple_of(k * BLOCK, BLOCK), BLOCK)
-        after = pl.ds(pl.multiple_of(jnp.minimum(k + 1, STEPS - 1) * BLOCK, BLOCK), BLOCK)
+    def factor_block(others):
         work_ref[:, BLOCK:] = jnp.where(r == c, 1.0, 0.0).astype(f32)
-        before, live = jnp.maximum(k - 1, 0), k > 0
-        others = [functools.partial(finish_row, before, live, b) for b in range(STEPS)]
-        others += [functools.partial(clear, before, live)]
-        others += [functools.partial(trail, m, n) for n in range(STEPS // 2) for m in range(STEPS)]
-        places = BLOCK // 2
         emitted = 0
         for place, _ in enumerate(factor_tile(work_ref)):
-            until = -(-len(others) * (place + 1) // places)
+            until = -(-len(others) * (place + 1) // (BLOCK // 2))
             for other in others[emitted:until]:
                 other()
             emitted = until
 
+    def prepare(k):
+        here = pl.ds(pl.multiple_of(k * BLOCK, BLOCK), BLOCK)
+        after = pl.ds(pl.multiple_of(jnp.minimum(k + 1, STEPS - 1) * BLOCK, BLOCK), BLOCK)
         d_ref[here, :] = jnp.where(r <= c, work_ref[:, :BLOCK], 0.0)
         inverse = work_ref[:, BLOCK:]
         inv_ref[...] = inverse
         u = dot_split_128(split(inverse), split(x_ref[here, after]))
         work_ref[:, :BLOCK] = x_ref[after, after] - dot_split_128(split(jnp.transpose(u)), split(u))
+
+    def step(k, _):
+        others = [functools.partial(finish_row, k - 1, b) for b in range(STEPS)]
+        others += [functools.partial(clear, k - 1)]
+        others += [functools.partial(trail, m, n) for n in range(STEPS // 2) for m in range(STEPS)]
+        factor_block(others)
+        prepare(k)
         return 0
 
-    lax.fori_loop(0, STEPS, step, 0)
+    factor_block([])
+    for copy in copies[1:]:
+        copy.wait()
+    prepare(0)
+    lax.fori_loop(1, STEPS, step, 0)
     end = slice(WIDTH - BLOCK, WIDTH)
     x_ref[end, :] = dot_split_128(split(inv_ref[...]), split(x_ref[end, :]))
     x_ref[end, end] = inv_ref[...]
@@ -183,9 +189,6 @@
     other = pl.ds(pl.multiple_of(jnp.minimum(col, STEPS - 1) * BLOCK, BLOCK), BLOCK)
     block = jnp.where(row == col, d_ref[mine, :], x_ref[other, mine])
     corner_ref[...] = jnp.where(row >= col, jnp.transpose(block), 0.0)
-    copy = pltpu.make_async_copy(corner_ref, corner_hbm, sems.at[2 * STEPS])
-    copy.start()
-    copy.wait()
 
 
 def factor(place, gathered):
@@ -193,22 +196,21 @@
     return pl.pallas_call(
         factor_kernel,
         in_specs=[pl.BlockSpec(memory_space=pltpu.SMEM), hbm],
-        out_specs=(vmem, vmem, hbm),
+        out_specs=(vmem, vmem, vmem),
         out_shape=(
             jax.ShapeDtypeStruct((WIDTH, WIDTH), bf16),
             jax.ShapeDtypeStruct((WIDTH, WIDTH), bf16),
-            pltpu.HBM((BLOCK, BLOCK), f32),
+            jax.ShapeDtypeStruct((BLOCK, BLOCK), f32),
         ),
         scratch_shapes=[
             pltpu.VMEM((WIDTH, WIDTH), f32),
             pltpu.VMEM((WIDTH, BLOCK), f32),
-            pltpu.VMEM((BLOCK, BLOCK), f32),
             pltpu.VMEM((BLOCK, 2 * BLOCK), f32),
             pltpu.VMEM((BLOCK, BLOCK), f32),
             pltpu.VMEM((WIDTH, 2 * BLOCK), bf16),
             pltpu.VMEM((2 * BLOCK, WIDTH), bf16),
             pltpu.VMEM((BLOCK, WIDTH), bf16),
-            pltpu.SemaphoreType.DMA((2 * STEPS + 1,)),
+            pltpu.SemaphoreType.DMA((2 * STEPS,)),
         ],
         compiler_params=pltpu.CompilerParams(vmem_limit_bytes=24 * 2**20),
         cost_estimate=pl.CostEstimate(flops=40_000_000_000, bytes_accessed=2**23, transcendentals=0),
@@ -216,8 +218,8 @@
     )(place, gathered)
 
 
-def apply_kernel(place_ref, mh, ml, *refs):
-    v_hbm, outs, (vh, vl, v_ref, sems) = refs[:SIDE], refs[SIDE : SIDE + 4], refs[SIDE + 4 :]
+def apply_kernel(place_ref, mh, ml, corner_ref, *refs):
+    v_hbm, outs, (vh, vl, v_ref, sems) = refs[:SIDE], refs[SIDE : SIDE + 3], refs[SIDE + 3 :]
     count = iter(range(sems.shape[0]))
     copy = lambda src, dst: pltpu.make_async_copy(src, dst, sems.at[next(count)])
     arriving = [copy(v, v_ref.at[d]) for d, v in enumerate(v_hbm)]
@@ -225,9 +227,8 @@
         c.start()
     row, col = place_ref[0], place_ref[1]
     other = pl.ds(pl.multiple_of(jnp.minimum(col, STEPS - 1) * BLOCK, BLOCK), BLOCK)
-    sent = [copy(m.at[other], out) for m, out in zip((mh, ml), outs[2:])]
-    for c in sent:
-        c.start()
+    sent = [copy(corner_ref, outs[2])]
+    sent[0].start()
     my_y, my_x = row // SIDE, row % SIDE
     swapped = jnp.where((my_y == 1) | (my_y == 2), 1, 0)
     for d in range(SIDE):
@@ -242,6 +243,9 @@
     for k in range(0, WIDTH, CHUNK):
         at, on = slice(k, k + CHUNK), slice(k, WIDTH)
         vh[at], vl[at] = split(dot_split((mh[on, at], ml[on, at]), (vh[on], vl[on]), ((0,), (0,))))
+        for v, m in ((vh, mh), (vl, ml)):
+            panel = jnp.transpose(m[other, at].astype(f32)).astype(bf16)
+            v[at, :BLOCK] = jnp.where(col < STEPS, panel, v[at, :BLOCK])
         for v, out in zip((vh, vl), outs):
             sent.append(copy(v.at[at], out.at[at]))
             sent[-1].start()
@@ -249,34 +253,32 @@
         c.wait()
 
 
-def apply(place, mh, ml, across):
+def apply(place, mh, ml, corner, across):
     vmem, hbm = pl.BlockSpec(memory_space=pltpu.VMEM), pl.BlockSpec(memory_space=pltpu.HBM)
     square = pltpu.VMEM((WIDTH, WIDTH), bf16)
     return pl.pallas_call(
         apply_kernel,
-        in_specs=[pl.BlockSpec(memory_space=pltpu.SMEM), vmem, vmem] + [hbm] * SIDE,
-        out_specs=(hbm,) * 4,
-        out_shape=tuple(pltpu.HBM((rows, WIDTH), bf16) for rows in (WIDTH, WIDTH, BLOCK, BLOCK)),
+        in_specs=[pl.BlockSpec(memory_space=pltpu.SMEM), vmem, vmem, vmem] + [hbm] * SIDE,
+        out_specs=(hbm,) * 3,
+        out_shape=(pltpu.HBM((WIDTH, WIDTH), bf16), pltpu.HBM((WIDTH, WIDTH), bf16), pltpu.HBM((BLOCK, BLOCK), f32)),
         scratch_shapes=[square, square]
         + [
             pltpu.VMEM((SIDE, 2 * BLOCK, WIDTH), f32),
-            pltpu.SemaphoreType.DMA((SIDE + 2 + 2 * (WIDTH // CHUNK),)),
+            pltpu.SemaphoreType.DMA((SIDE + 1 + 2 * (WIDTH // CHUNK),)),
         ],
         compiler_params=pltpu.CompilerParams(vmem_limit_bytes=20 * 2**20),
         cost_estimate=pl.CostEstimate(flops=10_000_000_000, bytes_accessed=2**23, transcendentals=0),
         name="apply",
-    )(place, mh, ml, *across)
-
-
-def update_kernel(place_ref, a_ref, u_ref, corner_ref, yh_ref, yl_ref, ph_ref, pl_ref, out_ref):
+    )(place, mh, ml, corner, *across)
+
+
+def update_kernel(place_ref, a_ref, u_ref, yh_ref, yl_ref, corner_ref, out_ref):
     row, col, step = place_ref[0], place_ref[1], pl.program_id(0)
     slots = [jnp.where(step < HALF // CHUNK, j, other_half(j) - STEPS) for j in range(STEPS)]
     u = split(jnp.concatenate([u_ref[s] for s in slots], 1))
-    out_ref[...] = a_ref[...] - dot_split(u, (yh_ref[...], yl_ref[...]))
-
-    @pl.when(col < STEPS)
-    def _():
-        out_ref[:, :BLOCK] = dot_split(u, (ph_ref[...], pl_ref[...]), ((1,), (1,)))
+    product = dot_split(u, (yh_ref[...], yl_ref[...]))
+    out_ref[:, :BLOCK] = jnp.where(col < STEPS, product[:, :BLOCK], a_ref[:, :BLOCK] - product[:, :BLOCK])
+    out_ref[:, BLOCK:] = a_ref[:, BLOCK:] - product[:, BLOCK:]
 
     @pl.when((step == 0) & (row < STEPS))
     def _():
@@ -287,7 +289,7 @@
             out_ref[:BLOCK, :BLOCK] = corner_ref[...]
 
 
-def update(place, blocked, gathered, corner, yh, yl, ph, pl_):
+def update(place, blocked, gathered, yh, yl, corner):
     per_half = HALF // CHUNK
     whole = lambda *shape: pl.BlockSpec(shape, lambda i: (0, 0))
     return pl.pallas_call(
@@ -297,17 +299,15 @@
             pl.BlockSpec(memory_space=pltpu.SMEM),
             pl.BlockSpec((CHUNK, WIDTH), lambda i: (i, 0)),
             pl.BlockSpec((STEPS, CHUNK, BLOCK), lambda i: (i // per_half, i % per_half, 0)),
-            whole(BLOCK, BLOCK),
             whole(WIDTH, WIDTH),
             whole(WIDTH, WIDTH),
-            whole(BLOCK, WIDTH),
-            whole(BLOCK, WIDTH),
+            whole(BLOCK, BLOCK),
         ],
         out_specs=pl.BlockSpec((CHUNK, WIDTH), lambda i: (i, 0)),
         out_shape=jax.ShapeDtypeStruct((WIDTH, WIDTH), f32),
         compiler_params=pltpu.CompilerParams(vmem_limit_bytes=28 * 2**20),
         name="update",
-    )(place, blocked, gathered, corner, yh, yl, ph, pl_)
+    )(place, blocked, gathered, yh, yl, corner)
 
 
 def per_device(blocked):
@@ -345,8 +345,8 @@
 
     place = jnp.stack([row, col])
     mh, ml, corner = factor(place, in_hbm(window))
-    applied = apply(place, mh, ml, [in_hbm(v) for v in across])
-    return update(place, *(in_hbm(v) for v in (blocked, panels, corner, *applied)))
+    applied = apply(place, mh, ml, corner, [in_hbm(v) for v in across])
+    return update(place, *(in_hbm(v) for v in (blocked, panels, *applied)))
 
 
 def solution(mesh):

time: 169 us -> 167 us (0.988)
  Pallas kernels: 64 us -> 58.4 us
  waiting for transfers between devices: 40.2 us -> 43.4 us
    ppermute x3, waiting for transfers between devices: 6.9 us -> 10.2 us  [per_device(): lax.ppermute(pair, 'prow', [(r // SIDE * SIDE + (r + d) % SIDE, r) for r...]
    pallas_call x1, Pallas kernels: 37.7 us -> 34.4 us  [factor(): pl.pallas_call(factor_kernel, in_specs=[pl.BlockSpec(memory_space=pltpu.S...]
    pallas_call x1, Pallas kernels: 13.7 us -> 11.3 us  [update(): pl.pallas_call(update_kernel, grid=(WIDTH // CHUNK,), in_specs=[pl.BlockS...]
  transfers between devices with their start and end apart: 13 -> 13, of which waited for: 6 -> 6; matrix products, arithmetic and copies ran while one was open for 3% -> 3% of each run, Pallas kernels for 30% -> 29%
where the time goes in v2:
time: 167 us; the launch traced here: 165 us
  Pallas kernels  58.4 us (35%)
  waiting for transfers between devices  43.4 us (26%)
  starting transfers between devices  24.3 us (15%)
  blocking collectives  18.4 us (11%)
  between operations  13.6 us (8%)
  local copies, waits for them, and re-layouts  3.85 us (2%)
  other arithmetic  3.02 us (2%)
    pallas_call x1, Pallas kernels, factor(): pl.pallas_call(factor_kernel, in_specs=[pl.BlockSpec(memory_space=pltpu.S...  34.4 us
    all_to_all x1, blocking collectives, per_device(): lax.all_to_all(jnp.broadcast_to(part, (rows, quarter, BLOCK)), 'prow', 0, 0)  18.4 us
    all_gather x1, waiting for transfers between devices, per_device(): window = lax.all_gather(strip.reshape(HALF, BLOCK), 'pcol', axis=0)  17.4 us
    ppermute x4, starting transfers between devices, per_device(): lax.ppermute(blocked[g * quarter:(g + 1) * quarter, :BLOCK], ('prow', 'pc...  12.8 us
    pallas_call x1, Pallas kernels, apply(): pl.pallas_call(apply_kernel, in_specs=[pl.BlockSpec(memory_space=pltpu.SM...  12.6 us
    ppermute x3, waiting for transfers between devices, per_device(): lax.ppermute(own, 'prow', [(a * SIDE + x, b * SIDE + x) for a, b in move...  12.1 us
    pallas_call x1, Pallas kernels, update(): pl.pallas_call(update_kernel, grid=(WIDTH // CHUNK,), in_specs=[pl.BlockS...  11.3 us
    ppermute x3, waiting for transfers between devices, per_device(): lax.ppermute(pair, 'prow', [(r // SIDE * SIDE + (r + d) % SIDE, r) for r...  10.2 us
  transfers between devices with their start and end apart: 13, of which 6 were waited for; matrix products, arithmetic and copies ran while one was open for 3% of the time, Pallas kernels for 29%

profile of v2, /device:TPU:1, one launch (start us, length us, event | category | flops | bytes accessed | tf_op | source)
XLA Modules:
  0.0 164.9 jit_solution(15500252575632660996)
XLA Ops:
  6.5 0.8 fusion
  7.3 0.7 collective-permute-start.1
  8.0 6.4 %collective-permute-start.2 = (f32[32,128]{1,0:T(8,128)S(1)}, f32[32,128]{1,0:T(8,128)S(1)}, u32[]{:S(2)}, u32[]{:S(2)}) collective-permute-start(f32[32,128]{1,0:T(8,128)S(1)} %get-tuple-element.21), channel_id=1, source_target_pairs={{0,16},{1,17},{2,18},{3,19},{4,20},{5,21},{6,22},{7,23},{16,80},{1... | collective-permute-start | bytes 49160 | tf_op jit(solution)/shard_map/ppermute | solution.py:325
  14.4 4.4 %collective-permute-start.3 = (f32[32,128]{1,0:T(8,128)S(1)}, f32[32,128]{1,0:T(8,128)S(1)}, u32[]{:S(2)}, u32[]{:S(2)}) collective-permute-start(f32[32,128]{1,0:T(8,128)S(1)} %get-tuple-element.23), channel_id=1, source_target_pairs={{0,32},{1,33},{2,34},{3,35},{4,36},{5,37},{6,38},{7,39},{16,96},{1... | collective-permute-start | bytes 49160 | tf_op jit(solution)/shard_map/ppermute | solution.py:325
  18.8 1.3 collective-permute-start.4
  20.2 0.8 collective-permute-done.4
  21.0 18.4 %all_to_all.5 = f32[16,32,128]{2,1,0:T(8,128)} all-to-all(f32[16,32,128]{2,1,0:T(8,128)S(1)} %broadcast_in_dim.3), channel_id=1, replica_groups=mesh['prow'=16,'pcol'=16] {'prow'}, dimensions={0} | all-to-all | bytes 524288 | tf_op jit(solution)/shard_map/all_to_all | solution.py:328
  39.4 0.0 all-gather.6.cloned.1.call-start
  39.5 1.1 slice.27
  40.5 2.5 %collective-permute-start.5 = (f32[128,1024]{1,0:T(8,128)S(1)}, f32[128,1024]{1,0:T(8,128)S(1)}, u32[]{:S(2)}, u32[]{:S(2)}) collective-permute-start(f32[128,1024]{1,0:T(8,128)S(1)} %slice.27), channel_id=1, source_target_pairs={{0,192},{16,208},{32,224},{48,240},{64,128},{80,144},{96,160},{112... | collective-permute-start | bytes 1572872 | tf_op jit(solution)/shard_map/ppermute | solution.py:335
  43.1 1.0 slice.22
  44.0 2.9 %collective-permute-start = (f32[512,128]{1,0:T(8,128)S(1)}, f32[512,128]{1,0:T(8,128)S(1)}, u32[]{:S(2)}, u32[]{:S(2)}) collective-permute-start(f32[512,128]{1,0:T(8,128)S(1)} %slice.22), channel_id=1, source_target_pairs={{0,14},{1,15},{2,12},{3,13},{4,10},{5,11},{6,8},{7,9},{16,30},{17,... | collective-permute-start | bytes 786440 | tf_op jit(solution)/shard_map/ppermute | solution.py:327
  47.0 1.9 %collective-permute-start.6 = (f32[128,1024]{1,0:T(8,128)S(1)}, f32[128,1024]{1,0:T(8,128)S(1)}, u32[]{:S(2)}, u32[]{:S(2)}) collective-permute-start(f32[128,1024]{1,0:T(8,128)S(1)} %slice.27), channel_id=1, source_target_pairs={{0,64},{16,80},{32,96},{48,112},{64,0},{80,16},{96,32},{112,48},{1... | collective-permute-start | bytes 1572872 | tf_op jit(solution)/shard_map/ppermute | solution.py:335
  48.9 1.3 collective-permute-start.7
  50.3 2.8 %collective-permute-done = f32[512,128]{1,0:T(8,128)S(1)} collective-permute-done((f32[512,128]{1,0:T(8,128)S(1)}, f32[512,128]{1,0:T(8,128)S(1)}, u32[]{:S(2)}, u32[]{:S(2)}) %collective-permute-start) | collective-permute-done | bytes 262176 | tf_op jit(solution)/shard_map/ppermute | solution.py:327
  53.1 1.7 %slice_select_fusion = f32[512,128]{1,0:T(8,128)} fusion(f32[512,128]{1,0:T(8,128)S(1)} %collective-permute-done, f32[1024,1024]{1,0:T(8,128)} %a_ref.1, pred[]{:T(512)S(6)} %lt.6), kind=kLoop, calls=%fused_computation.1 | loop fusion | flops 65536 | bytes 786433 | tf_op jit(solution)/shard_map/jit(_where)/select_n | solution.py:330
  54.8 1.1 broadcast_select_fusion.1
  55.9 2.9 %collective-permute-done.6 = f32[128,1024]{1,0:T(8,128)S(1)} collective-permute-done((f32[128,1024]{1,0:T(8,128)S(1)}, f32[128,1024]{1,0:T(8,128)S(1)}, u32[]{:S(2)}, u32[]{:S(2)}) %collective-permute-start.6) | collective-permute-done | bytes 524320 | tf_op jit(solution)/shard_map/ppermute | solution.py:335
  58.8 9.2 %collective-permute-done.7 = f32[128,1024]{1,0:T(8,128)S(1)} collective-permute-done((f32[128,1024]{1,0:T(8,128)S(1)}, f32[128,1024]{1,0:T(8,128)S(1)}, u32[]{:S(2)}, u32[]{:S(2)}) %collective-permute-start.7) | collective-permute-done | bytes 524320 | tf_op jit(solution)/shard_map/ppermute | solution.py:335
  68.0 0.1 broadcast_select_fusion
  68.0 0.1 pad_maximum_fusion.refs_0_
  68.2 17.4 %all-gather.4.cloned.1.call-done.w_ref = f32[16,512,128]{2,1,0:T(8,128)} async-done(((f32[1,512,128]{2,1,0:T(8,128)}), f32[16,512,128]{2,1,0:T(8,128)}) %all-gather.4.cloned.1.call-update) | async-done | bytes 4194320 | tf_op jit(solution)/shard_map/all_gather | solution.py:329
  85.6 0.1 pad_add_fusion.place_ref
  85.7 0.6 collective-permute-start.10
  86.3 2.1 %collective-permute-start.8 = (f32[256,1024]{1,0:T(8,128)S(1)}, f32[256,1024]{1,0:T(8,128)S(1)}, u32[]{:S(2)}, u32[]{:S(2)}) collective-permute-start(f32[256,1024]{1,0:T(8,128)S(1)} %pad_maximum_fusion.refs_0_), channel_id=1, source_target_pairs={{16,0},{32,16},{48,32},{0,48},{80,64},{96,80},{112,96},{64,112},{1... | collective-permute-start | bytes 3145736 | tf_op jit(solution)/shard_map/ppermute | solution.py:344
  88.4 0.0 collective-permute-start.9
  88.4 34.4 %factor.1 = (bf16[1024,1024]{1,0:T(8,128)(2,1)S(1)}, bf16[1024,1024]{1,0:T(8,128)(2,1)S(1)}, f32[128,128]{1,0:T(8,128)S(1)}) custom-call(s32[2]{0:T(128)S(1)} %pad_add_fusion.place_ref, f32[16,512,128]{2,1,0:T(8,128)} %all-gather.4.cloned.1.call-done.w_ref), custom_call_target="tpu_custom_call" | custom-call | flops 40000000000 | bytes 8388608 | tf_op jit(solution)/shard_map/factor/pallas_call | solution.py:196
  122.9 10.2 %collective-permute-done.9.refs_2_ = f32[256,1024]{1,0:T(8,128)S(1)} collective-permute-done((f32[256,1024]{1,0:T(8,128)S(1)}, f32[256,1024]{1,0:T(8,128)S(1)}, u32[]{:S(2)}, u32[]{:S(2)}) %collective-permute-start.9) | collective-permute-done | bytes 1048608 | tf_op jit(solution)/shard_map/ppermute | solution.py:344
  133.1 1.0 copy-done.3
  134.1 12.6 %apply.1 = (bf16[1024,1024]{1,0:T(8,128)(2,1)}, bf16[1024,1024]{1,0:T(8,128)(2,1)}, f32[128,128]{1,0:T(8,128)}) custom-call(s32[2]{0:T(128)S(1)} %pad_add_fusion.place_ref, bf16[1024,1024]{1,0:T(8,128)(2,1)S(1)} %get-tuple-element.15.mh, bf16[1024,1024]{1,0:T(8,128)(2,1)S(1)} %get-tuple-element.16.ml, f32[128,128]{1,0:T(8,128)S(1)} %get-tuple-element.17.corner_ref, ...), custom_call_target="tpu_custom_call" | custom-call | flops 10000000000 | bytes 8388608 | tf_op jit(solution)/shard_map/apply/pallas_call | solution.py:259
  146.7 0.0 all-gather.6.cloned.1.call-done
  146.7 11.3 %update.1 = f32[1024,1024]{1,0:T(8,128)} custom-call(s32[2]{0:T(128)S(1)} %pad_add_fusion.place_ref, f32[1024,1024]{1,0:T(8,128)} %a_ref.1, f32[16,512,128]{2,1,0:T(8,128)} %bitcast.4, bf16[1024,1024]{1,0:T(8,128)(2,1)} %get-tuple-element.18.yh_ref, bf16[1024,1024]{1,0:T(8,128)(2,1)} %get-tuple-element.19.yl_ref, f32[128,128]{1,0:T(8,128)} %get-tuple-element.20.corner_ref), custom_call_target="tpu_custom_call" | custom-call | tf_op jit(solution)/shard_map/update/pallas_call | solution.py:295
  (18 shorter events, 0.1 us)
Async XLA Ops:
  6.5 79.1 %all-gather.4.cloned.1.call-start = ((), (), s32[]{:S(2)}) async-start(), calls=%async_computation.1 | async-start | bytes 4456448 | tf_op jit(solution)/shard_map/all_gather | solution.py:329
  7.3 12.8 %collective-permute-start.1 = (f32[32,128]{1,0:T(8,128)S(1)}, f32[32,128]{1,0:T(8,128)S(1)}, u32[]{:S(2)}, u32[]{:S(2)}) collective-permute-start(f32[32,128]{1,0:T(8,128)S(1)} %get-tuple-element.24), channel_id=1, source_target_pairs={{0,0},{1,1},{2,2},{3,3},{4,4},{5,5},{6,6},{7,7},{16,64},{17,65},{1... | collective-permute-start | bytes 49160 | tf_op jit(solution)/shard_map/ppermute | solution.py:325
  8.0 12.2 %collective-permute-start.2 = (f32[32,128]{1,0:T(8,128)S(1)}, f32[32,128]{1,0:T(8,128)S(1)}, u32[]{:S(2)}, u32[]{:S(2)}) collective-permute-start(f32[32,128]{1,0:T(8,128)S(1)} %get-tuple-element.21), channel_id=1, source_target_pairs={{0,16},{1,17},{2,18},{3,19},{4,20},{5,21},{6,22},{7,23},{16,80},{1... | collective-permute-start | bytes 49160 | tf_op jit(solution)/shard_map/ppermute | solution.py:325
  14.4 5.7 %collective-permute-start.3 = (f32[32,128]{1,0:T(8,128)S(1)}, f32[32,128]{1,0:T(8,128)S(1)}, u32[]{:S(2)}, u32[]{:S(2)}) collective-permute-start(f32[32,128]{1,0:T(8,128)S(1)} %get-tuple-element.23), channel_id=1, source_target_pairs={{0,32},{1,33},{2,34},{3,35},{4,36},{5,37},{6,38},{7,39},{16,96},{1... | collective-permute-start | bytes 49160 | tf_op jit(solution)/shard_map/ppermute | solution.py:325
  18.8 2.1 %collective-permute-start.4 = (f32[32,128]{1,0:T(8,128)S(1)}, f32[32,128]{1,0:T(8,128)S(1)}, u32[]{:S(2)}, u32[]{:S(2)}) collective-permute-start(f32[32,128]{1,0:T(8,128)S(1)} %get-tuple-element.22), channel_id=1, source_target_pairs={{0,48},{1,49},{2,50},{3,51},{4,52},{5,53},{6,54},{7,55},{16,112},{... | collective-permute-start | bytes 49160 | tf_op jit(solution)/shard_map/ppermute | solution.py:325
  39.4 107.3 %all-gather.6.cloned.1.call-start = ((), (), s32[]{:S(2)}) async-start(), calls=%async_computation.2 | async-start | bytes 4456448 | tf_op jit(solution)/shard_map/all_gather | solution.py:341
  40.5 14.2 %collective-permute-start.5 = (f32[128,1024]{1,0:T(8,128)S(1)}, f32[128,1024]{1,0:T(8,128)S(1)}, u32[]{:S(2)}, u32[]{:S(2)}) collective-permute-start(f32[128,1024]{1,0:T(8,128)S(1)} %slice.27), channel_id=1, source_target_pairs={{0,192},{16,208},{32,224},{48,240},{64,128},{80,144},{96,160},{112... | collective-permute-start | bytes 1572872 | tf_op jit(solution)/shard_map/ppermute | solution.py:335
  44.0 9.0 %collective-permute-start = (f32[512,128]{1,0:T(8,128)S(1)}, f32[512,128]{1,0:T(8,128)S(1)}, u32[]{:S(2)}, u32[]{:S(2)}) collective-permute-start(f32[512,128]{1,0:T(8,128)S(1)} %slice.22), channel_id=1, source_target_pairs={{0,14},{1,15},{2,12},{3,13},{4,10},{5,11},{6,8},{7,9},{16,30},{17,... | collective-permute-start | bytes 786440 | tf_op jit(solution)/shard_map/ppermute | solution.py:327
  47.0 11.8 %collective-permute-start.6 = (f32[128,1024]{1,0:T(8,128)S(1)}, f32[128,1024]{1,0:T(8,128)S(1)}, u32[]{:S(2)}, u32[]{:S(2)}) collective-permute-start(f32[128,1024]{1,0:T(8,128)S(1)} %slice.27), channel_id=1, source_target_pairs={{0,64},{16,80},{32,96},{48,112},{64,0},{80,16},{96,32},{112,48},{1... | collective-permute-start | bytes 1572872 | tf_op jit(solution)/shard_map/ppermute | solution.py:335
  48.9 19.1 %collective-permute-start.7 = (f32[128,1024]{1,0:T(8,128)S(1)}, f32[128,1024]{1,0:T(8,128)S(1)}, u32[]{:S(2)}, u32[]{:S(2)}) collective-permute-start(f32[128,1024]{1,0:T(8,128)S(1)} %slice.27), channel_id=1, source_target_pairs={{0,128},{16,144},{32,160},{48,176},{64,192},{80,208},{96,224},{112... | collective-permute-start | bytes 1572872 | tf_op jit(solution)/shard_map/ppermute | solution.py:335
  68.2 54.7 %copy-start = (f32[256,1024]{1,0:T(8,128)}, f32[256,1024]{1,0:T(8,128)S(1)}, u32[]{:S(2)}) copy-start(f32[256,1024]{1,0:T(8,128)S(1)} %pad_maximum_fusion.refs_0_) | copy-start | bytes 3145732
  85.7 37.2 %collective-permute-start.10 = (f32[256,1024]{1,0:T(8,128)S(1)}, f32[256,1024]{1,0:T(8,128)S(1)}, u32[]{:S(2)}, u32[]{:S(2)}) collective-permute-start(f32[256,1024]{1,0:T(8,128)S(1)} %pad_maximum_fusion.refs_0_), channel_id=1, source_target_pairs={{48,0},{0,16},{16,32},{32,48},{112,64},{64,80},{80,96},{96,112},{1... | collective-permute-start | bytes 3145736 | tf_op jit(solution)/shard_map/ppermute | solution.py:344
  86.3 36.6 %collective-permute-start.8 = (f32[256,1024]{1,0:T(8,128)S(1)}, f32[256,1024]{1,0:T(8,128)S(1)}, u32[]{:S(2)}, u32[]{:S(2)}) collective-permute-start(f32[256,1024]{1,0:T(8,128)S(1)} %pad_maximum_fusion.refs_0_), channel_id=1, source_target_pairs={{16,0},{32,16},{48,32},{0,48},{80,64},{96,80},{112,96},{64,112},{1... | collective-permute-start | bytes 3145736 | tf_op jit(solution)/shard_map/ppermute | solution.py:344
  88.4 44.7 %collective-permute-start.9 = (f32[256,1024]{1,0:T(8,128)S(1)}, f32[256,1024]{1,0:T(8,128)S(1)}, u32[]{:S(2)}, u32[]{:S(2)}) collective-permute-start(f32[256,1024]{1,0:T(8,128)S(1)} %pad_maximum_fusion.refs_0_), channel_id=1, source_target_pairs={{32,0},{48,16},{0,32},{16,48},{96,64},{112,80},{64,96},{80,112},{1... | collective-permute-start | bytes 3145736 | tf_op jit(solution)/shard_map/ppermute | solution.py:344
  122.9 10.2 %copy-start.1 = (f32[256,1024]{1,0:T(8,128)}, f32[256,1024]{1,0:T(8,128)S(1)}, u32[]{:S(2)}) copy-start(f32[256,1024]{1,0:T(8,128)S(1)} %collective-permute-done.10.refs_3_) | copy-start | bytes 3145732
  122.9 10.2 %copy-start.2 = (f32[256,1024]{1,0:T(8,128)}, f32[256,1024]{1,0:T(8,128)S(1)}, u32[]{:S(2)}) copy-start(f32[256,1024]{1,0:T(8,128)S(1)} %collective-permute-done.8.refs_1_) | copy-start | bytes 3145732
  133.1 1.0 copy-start.3
Sparse Core Ops, SparseCore 0:
  39.5 46.0 all-gather.3
  87.4 37.1 all-gather.5

commit v3 on v2

--- a/solution.py
+++ b/solution.py
@@ -42,6 +42,16 @@
 
 def other_half(k):
     return 14 - k + 2 * (k % 2)
+
+
+def window_place(i, k):
+    if i < 3:
+        return k, i
+    if i == 3:
+        return (other_half(k), 2) if k < 4 else (other_half(k - 4), 1)
+    if k < 4:
+        return None
+    return (other_half(k - 4), 0) if i == 7 else (other_half(k), i - 4)
 
 
 def spread(row):
@@ -116,10 +126,13 @@
     x_ref, d_ref, work_ref, inv_ref, left_ref, right_ref, rest_ref, sems,
 ):
     copies = []
-    for j in range(STEPS):
-        for h, slot in enumerate((j, other_half(j))):
-            dst = x_ref.at[h * HALF : (h + 1) * HALF, j * BLOCK : (j + 1) * BLOCK]
-            copies.append(pltpu.make_async_copy(w_ref.at[slot], dst, sems.at[slot]))
+    for i in range(STEPS):
+        for k in range(STEPS):
+            if window_place(i, k):
+                slot, third = window_place(i, k)
+                src = w_ref.at[slot, third * BLOCK : (third + 1) * BLOCK]
+                dst = x_ref.at[i * BLOCK : (i + 1) * BLOCK, k * BLOCK : (k + 1) * BLOCK]
+                copies.append(pltpu.make_async_copy(src, dst, sems.at[len(copies)]))
     for copy in copies:
         copy.start()
     copies[0].wait()
@@ -210,7 +223,7 @@
             pltpu.VMEM((WIDTH, 2 * BLOCK), bf16),
             pltpu.VMEM((2 * BLOCK, WIDTH), bf16),
             pltpu.VMEM((BLOCK, WIDTH), bf16),
-            pltpu.SemaphoreType.DMA((2 * STEPS,)),
+            pltpu.SemaphoreType.DMA((3 * STEPS * 2,)),
         ],
         compiler_params=pltpu.CompilerParams(vmem_limit_bytes=24 * 2**20),
         cost_estimate=pl.CostEstimate(flops=40_000_000_000, bytes_accessed=2**23, transcendentals=0),
@@ -316,17 +329,23 @@
     span = range(STEPS)
     in_hbm = lambda a: pltpu.with_memory_space_constraint(a, pltpu.HBM)
 
-    quarter = BLOCK // 4
+    piece = 3 * BLOCK // rows
+    third = jnp.where(row < 3, row, jnp.where(row == 3, jnp.where(col < 4, 2, 1), jnp.where(row == 7, 0, row - 4)))
+    padded = jnp.pad(blocked[:BLOCK, :BLOCK], ((16, 16), (0, 0)))
     parts = []
-    for g in range(4):
-        pairs = [
-            (i * cols + k, (4 * (i % 4) + g) * cols + (k if i < 4 else other_half(k))) for i in span for k in span
-        ]
-        parts.append(lax.ppermute(blocked[g * quarter : (g + 1) * quarter, :BLOCK], ("prow", "pcol"), pairs))
-    part = (parts[0] + parts[1]) + (parts[2] + parts[3])
+    for g in range(6):
+        pairs = []
+        for i in span:
+            for k in span:
+                if window_place(i, k):
+                    to, b = window_place(i, k)
+                    pairs.append((i * cols + k, (5 * b + g) * cols + to))
+        part = lax.dynamic_slice(padded, (16 + piece * g - 8 * jnp.clip(third, 0, 2), 0), (piece, BLOCK))
+        parts.append(lax.ppermute(part, ("prow", "pcol"), pairs))
+    part = functools.reduce(jnp.add, parts)
     lower = lax.ppermute(blocked[HALF:, :BLOCK], "pcol", [(k, other_half(k)) for k in span])
-    strip = lax.all_to_all(jnp.broadcast_to(part, (rows, quarter, BLOCK)), "prow", 0, 0)
-    window = lax.all_gather(strip.reshape(HALF, BLOCK), "pcol", axis=0)
+    strip = lax.all_to_all(jnp.broadcast_to(part, (rows, piece, BLOCK)), "prow", 0, 0)
+    window = lax.all_gather(strip.reshape(3 * BLOCK, BLOCK), "pcol", axis=0)
     payload = jnp.where(col < STEPS, blocked[:HALF, :BLOCK], lower)
 
     own = blocked[:BLOCK]

time: 167 us -> 172 us (1.030)
  starting transfers between devices: 24.3 us -> 38.3 us
  blocking collectives: 18.4 us -> 11.2 us
    ppermute x4 -> x6, starting transfers between devices: 12.8 us -> 20.7 us  [per_device(): parts.append(lax.ppermute(part, ('prow', 'pcol'), pairs))]
    all_to_all x1, blocking collectives: 18.4 us -> 11.2 us  [per_device(): lax.all_to_all(jnp.broadcast_to(part, (rows, piece, BLOCK)), 'prow', 0, 0)]
    ppermute x1, starting transfers between devices: 2.94 us -> 9.16 us  [per_device(): lax.ppermute(blocked[HALF:, :BLOCK], 'pcol', [(k, other_half(k)) for k in...]
    ppermute x3, waiting for transfers between devices: 10.2 us -> 13.2 us  [per_device(): lax.ppermute(pair, 'prow', [(r // SIDE * SIDE + (r + d) % SIDE, r) for r...]
    ppermute x1, waiting for transfers between devices: 2.82 us -> 0.35 us  [per_device(): lax.ppermute(blocked[HALF:, :BLOCK], 'pcol', [(k, other_half(k)) for k in...]
    all_gather x1, waiting for transfers between devices: 17.4 us -> 15 us  [per_device(): window = lax.all_gather(strip.reshape(3 * BLOCK, BLOCK), 'pcol', axis=0)]
  transfers between devices with their start and end apart: 13 -> 15, of which waited for: 6 -> 6; matrix products, arithmetic and copies ran while one was open for 3% -> 3% of each run, Pallas kernels for 29% -> 28%
where the time goes in v3:
time: 172 us; the launch traced here: 171 us
  Pallas kernels  58.6 us (34%)
  waiting for transfers between devices  42.8 us (25%)
  starting transfers between devices  38.3 us (22%)
  between operations  13.6 us (8%)
  blocking collectives  11.2 us (7%)
  local copies, waits for them, and re-layouts  3.94 us (2%)
  other arithmetic  3.02 us (2%)
    pallas_call x1, Pallas kernels, factor(): pl.pallas_call(factor_kernel, in_specs=[pl.BlockSpec(memory_space=pltpu.S...  34.6 us
    ppermute x6, starting transfers between devices, per_device(): parts.append(lax.ppermute(part, ('prow', 'pcol'), pairs))  20.7 us
    all_gather x1, waiting for transfers between devices, per_device(): window = lax.all_gather(strip.reshape(3 * BLOCK, BLOCK), 'pcol', axis=0)  15 us
    ppermute x3, waiting for transfers between devices, per_device(): lax.ppermute(own, 'prow', [(a * SIDE + x, b * SIDE + x) for a, b in move...  13.3 us
    ppermute x3, waiting for transfers between devices, per_device(): lax.ppermute(pair, 'prow', [(r // SIDE * SIDE + (r + d) % SIDE, r) for r...  13.2 us
    pallas_call x1, Pallas kernels, apply(): pl.pallas_call(apply_kernel, in_specs=[pl.BlockSpec(memory_space=pltpu.SM...  12.6 us
    pallas_call x1, Pallas kernels, update(): pl.pallas_call(update_kernel, grid=(WIDTH // CHUNK,), in_specs=[pl.BlockS...  11.3 us
    all_to_all x1, blocking collectives, per_device(): lax.all_to_all(jnp.broadcast_to(part, (rows, piece, BLOCK)), 'prow', 0, 0)  11.2 us
  transfers between devices with their start and end apart: 15, of which 6 were waited for; matrix products, arithmetic and copies ran while one was open for 3% of the time, Pallas kernels for 28%

profile of v3, /device:TPU:1, one launch (start us, length us, event | category | flops | bytes accessed | tf_op | source)
XLA Modules:
  0.0 171.5 jit_solution(18403904118639757080)
XLA Ops:
  6.5 0.8 slice.14
  7.4 0.7 collective-permute-start.1
  8.1 6.5 %collective-permute-start.2 = (f32[24,128]{1,0:T(8,128)S(1)}, f32[24,128]{1,0:T(8,128)S(1)}, u32[]{:S(2)}, u32[]{:S(2)}) collective-permute-start(f32[24,128]{1,0:T(8,128)S(1)} %get-tuple-element.21), channel_id=1, source_target_pairs={{0,16},{1,17},{2,18},{3,19},{4,20},{5,21},{6,22},{7,23},{16,96},{1... | collective-permute-start | bytes 36872 | tf_op jit(solution)/shard_map/ppermute | solution.py:344
  14.6 4.4 %collective-permute-start.3 = (f32[24,128]{1,0:T(8,128)S(1)}, f32[24,128]{1,0:T(8,128)S(1)}, u32[]{:S(2)}, u32[]{:S(2)}) collective-permute-start(f32[24,128]{1,0:T(8,128)S(1)} %get-tuple-element.22), channel_id=1, source_target_pairs={{0,32},{1,33},{2,34},{3,35},{4,36},{5,37},{6,38},{7,39},{16,112},{... | collective-permute-start | bytes 36872 | tf_op jit(solution)/shard_map/ppermute | solution.py:344
  19.0 6.6 %collective-permute-start.4 = (f32[24,128]{1,0:T(8,128)S(1)}, f32[24,128]{1,0:T(8,128)S(1)}, u32[]{:S(2)}, u32[]{:S(2)}) collective-permute-start(f32[24,128]{1,0:T(8,128)S(1)} %get-tuple-element.23), channel_id=1, source_target_pairs={{0,48},{1,49},{2,50},{3,51},{4,52},{5,53},{6,54},{7,55},{16,128},{... | collective-permute-start | bytes 36872 | tf_op jit(solution)/shard_map/ppermute | solution.py:344
  25.6 1.3 collective-permute-start.5
  26.9 1.3 collective-permute-start.6
  28.3 0.8 collective-permute-done.6
  29.1 11.2 %all_to_all.5 = f32[16,24,128]{2,1,0:T(8,128)} all-to-all(f32[16,24,128]{2,1,0:T(8,128)S(1)} %broadcast_in_dim.3), channel_id=1, replica_groups=mesh['prow'=16,'pcol'=16] {'prow'}, dimensions={0} | all-to-all | bytes 393216 | tf_op jit(solution)/shard_map/all_to_all | solution.py:347
  40.3 1.1 slice.15
  41.4 2.4 %collective-permute-start.7 = (f32[128,1024]{1,0:T(8,128)S(1)}, f32[128,1024]{1,0:T(8,128)S(1)}, u32[]{:S(2)}, u32[]{:S(2)}) collective-permute-start(f32[128,1024]{1,0:T(8,128)S(1)} %slice.15), channel_id=1, source_target_pairs={{0,192},{16,208},{32,224},{48,240},{64,128},{80,144},{96,160},{112... | collective-permute-start | bytes 1572872 | tf_op jit(solution)/shard_map/ppermute | solution.py:354
  43.8 1.0 slice.13
  44.8 9.2 %collective-permute-start = (f32[512,128]{1,0:T(8,128)S(1)}, f32[512,128]{1,0:T(8,128)S(1)}, u32[]{:S(2)}, u32[]{:S(2)}) collective-permute-start(f32[512,128]{1,0:T(8,128)S(1)} %slice.13), channel_id=1, source_target_pairs={{0,14},{1,15},{2,12},{3,13},{4,10},{5,11},{6,8},{7,9},{16,30},{17,... | collective-permute-start | bytes 786440 | tf_op jit(solution)/shard_map/ppermute | solution.py:346
  54.0 1.9 %collective-permute-start.8 = (f32[128,1024]{1,0:T(8,128)S(1)}, f32[128,1024]{1,0:T(8,128)S(1)}, u32[]{:S(2)}, u32[]{:S(2)}) collective-permute-start(f32[128,1024]{1,0:T(8,128)S(1)} %slice.15), channel_id=1, source_target_pairs={{0,64},{16,80},{32,96},{48,112},{64,0},{80,16},{96,32},{112,48},{1... | collective-permute-start | bytes 1572872 | tf_op jit(solution)/shard_map/ppermute | solution.py:354
  55.9 1.3 collective-permute-start.9
  57.2 0.4 collective-permute-done
  57.6 1.7 slice_select_fusion
  59.3 1.1 broadcast_select_fusion.1
  60.4 4.1 %collective-permute-done.8 = f32[128,1024]{1,0:T(8,128)S(1)} collective-permute-done((f32[128,1024]{1,0:T(8,128)S(1)}, f32[128,1024]{1,0:T(8,128)S(1)}, u32[]{:S(2)}, u32[]{:S(2)}) %collective-permute-start.8) | collective-permute-done | bytes 524320 | tf_op jit(solution)/shard_map/ppermute | solution.py:354
  64.5 9.2 %collective-permute-done.9 = f32[128,1024]{1,0:T(8,128)S(1)} collective-permute-done((f32[128,1024]{1,0:T(8,128)S(1)}, f32[128,1024]{1,0:T(8,128)S(1)}, u32[]{:S(2)}, u32[]{:S(2)}) %collective-permute-start.9) | collective-permute-done | bytes 524320 | tf_op jit(solution)/shard_map/ppermute | solution.py:354
  73.7 0.1 broadcast_select_fusion
  73.8 0.1 pad_maximum_fusion.refs_0_
  73.9 15.0 %all-gather.4.cloned.1.call-done.w_ref = f32[16,384,128]{2,1,0:T(8,128)} async-done(((f32[1,384,128]{2,1,0:T(8,128)}), f32[16,384,128]{2,1,0:T(8,128)}) %all-gather.4.cloned.1.call-update) | async-done | bytes 3145744 | tf_op jit(solution)/shard_map/all_gather | solution.py:348
  88.9 0.1 pad_add_fusion.place_ref
  89.0 1.6 collective-permute-start.10
  90.6 0.7 collective-permute-start.11
  91.3 0.4 collective-permute-start.12
  91.7 34.6 %factor.1 = (bf16[1024,1024]{1,0:T(8,128)(2,1)S(1)}, bf16[1024,1024]{1,0:T(8,128)(2,1)S(1)}, f32[128,128]{1,0:T(8,128)S(1)}) custom-call(s32[2]{0:T(128)S(1)} %pad_add_fusion.place_ref, f32[16,384,128]{2,1,0:T(8,128)} %all-gather.4.cloned.1.call-done.w_ref), custom_call_target="tpu_custom_call" | custom-call | flops 40000000000 | bytes 8388608 | tf_op jit(solution)/shard_map/factor/pallas_call | solution.py:209
  126.4 13.2 %collective-permute-done.12.refs_3_ = f32[256,1024]{1,0:T(8,128)S(1)} collective-permute-done((f32[256,1024]{1,0:T(8,128)S(1)}, f32[256,1024]{1,0:T(8,128)S(1)}, u32[]{:S(2)}, u32[]{:S(2)}) %collective-permute-start.12) | collective-permute-done | bytes 1048608 | tf_op jit(solution)/shard_map/ppermute | solution.py:363
  139.6 1.0 copy-done.3
  140.6 12.6 %apply.1 = (bf16[1024,1024]{1,0:T(8,128)(2,1)}, bf16[1024,1024]{1,0:T(8,128)(2,1)}, f32[128,128]{1,0:T(8,128)}) custom-call(s32[2]{0:T(128)S(1)} %pad_add_fusion.place_ref, bf16[1024,1024]{1,0:T(8,128)(2,1)S(1)} %get-tuple-element.15.mh, bf16[1024,1024]{1,0:T(8,128)(2,1)S(1)} %get-tuple-element.16.ml, f32[128,128]{1,0:T(8,128)S(1)} %get-tuple-element.17.corner_ref, ...), custom_call_target="tpu_custom_call" | custom-call | flops 10000000000 | bytes 8388608 | tf_op jit(solution)/shard_map/apply/pallas_call | solution.py:272
  153.3 11.3 %update.1 = f32[1024,1024]{1,0:T(8,128)} custom-call(s32[2]{0:T(128)S(1)} %pad_add_fusion.place_ref, f32[1024,1024]{1,0:T(8,128)} %a_ref.1, f32[16,512,128]{2,1,0:T(8,128)} %bitcast.4, bf16[1024,1024]{1,0:T(8,128)(2,1)} %get-tuple-element.18.yh_ref, bf16[1024,1024]{1,0:T(8,128)(2,1)} %get-tuple-element.19.yl_ref, f32[128,128]{1,0:T(8,128)} %get-tuple-element.20.corner_ref), custom_call_target="tpu_custom_call" | custom-call | tf_op jit(solution)/shard_map/update/pallas_call | solution.py:308
  (23 shorter events, 0.2 us)
Async XLA Ops:
  6.5 82.4 %all-gather.4.cloned.1.call-start = ((), (), s32[]{:S(2)}) async-start(), calls=%async_computation.1 | async-start | bytes 3342336 | tf_op jit(solution)/shard_map/all_gather | solution.py:348
  7.4 19.5 %collective-permute-start.1 = (f32[24,128]{1,0:T(8,128)S(1)}, f32[24,128]{1,0:T(8,128)S(1)}, u32[]{:S(2)}, u32[]{:S(2)}) collective-permute-start(f32[24,128]{1,0:T(8,128)S(1)} %get-tuple-element.26), channel_id=1, source_target_pairs={{0,0},{1,1},{2,2},{3,3},{4,4},{5,5},{6,6},{7,7},{16,80},{17,81},{1... | collective-permute-start | bytes 36872 | tf_op jit(solution)/shard_map/ppermute | solution.py:344
  8.1 20.1 %collective-permute-start.2 = (f32[24,128]{1,0:T(8,128)S(1)}, f32[24,128]{1,0:T(8,128)S(1)}, u32[]{:S(2)}, u32[]{:S(2)}) collective-permute-start(f32[24,128]{1,0:T(8,128)S(1)} %get-tuple-element.21), channel_id=1, source_target_pairs={{0,16},{1,17},{2,18},{3,19},{4,20},{5,21},{6,22},{7,23},{16,96},{1... | collective-permute-start | bytes 36872 | tf_op jit(solution)/shard_map/ppermute | solution.py:344
  14.6 13.7 %collective-permute-start.3 = (f32[24,128]{1,0:T(8,128)S(1)}, f32[24,128]{1,0:T(8,128)S(1)}, u32[]{:S(2)}, u32[]{:S(2)}) collective-permute-start(f32[24,128]{1,0:T(8,128)S(1)} %get-tuple-element.22), channel_id=1, source_target_pairs={{0,32},{1,33},{2,34},{3,35},{4,36},{5,37},{6,38},{7,39},{16,112},{... | collective-permute-start | bytes 36872 | tf_op jit(solution)/shard_map/ppermute | solution.py:344
  19.0 9.2 %collective-permute-start.4 = (f32[24,128]{1,0:T(8,128)S(1)}, f32[24,128]{1,0:T(8,128)S(1)}, u32[]{:S(2)}, u32[]{:S(2)}) collective-permute-start(f32[24,128]{1,0:T(8,128)S(1)} %get-tuple-element.23), channel_id=1, source_target_pairs={{0,48},{1,49},{2,50},{3,51},{4,52},{5,53},{6,54},{7,55},{16,128},{... | collective-permute-start | bytes 36872 | tf_op jit(solution)/shard_map/ppermute | solution.py:344
  25.6 2.6 %collective-permute-start.5 = (f32[24,128]{1,0:T(8,128)S(1)}, f32[24,128]{1,0:T(8,128)S(1)}, u32[]{:S(2)}, u32[]{:S(2)}) collective-permute-start(f32[24,128]{1,0:T(8,128)S(1)} %get-tuple-element.24), channel_id=1, source_target_pairs={{0,64},{1,65},{2,66},{3,67},{4,68},{5,69},{6,70},{7,71},{16,144},{... | collective-permute-start | bytes 36872 | tf_op jit(solution)/shard_map/ppermute | solution.py:344
  26.9 2.1 %collective-permute-start.6 = (f32[24,128]{1,0:T(8,128)S(1)}, f32[24,128]{1,0:T(8,128)S(1)}, u32[]{:S(2)}, u32[]{:S(2)}) collective-permute-start(f32[24,128]{1,0:T(8,128)S(1)} %get-tuple-element.25), channel_id=1, source_target_pairs={{0,80},{1,81},{2,82},{3,83},{4,84},{5,85},{6,86},{7,87},{16,160},{... | collective-permute-start | bytes 36872 | tf_op jit(solution)/shard_map/ppermute | solution.py:344
  40.2 113.0 %all-gather.6.cloned.1.call-start = ((), (), s32[]{:S(2)}) async-start(), calls=%async_computation.2 | async-start | bytes 4456448 | tf_op jit(solution)/shard_map/all_gather | solution.py:360
  41.4 17.9 %collective-permute-start.7 = (f32[128,1024]{1,0:T(8,128)S(1)}, f32[128,1024]{1,0:T(8,128)S(1)}, u32[]{:S(2)}, u32[]{:S(2)}) collective-permute-start(f32[128,1024]{1,0:T(8,128)S(1)} %slice.15), channel_id=1, source_target_pairs={{0,192},{16,208},{32,224},{48,240},{64,128},{80,144},{96,160},{112... | collective-permute-start | bytes 1572872 | tf_op jit(solution)/shard_map/ppermute | solution.py:354
  44.8 12.8 %collective-permute-start = (f32[512,128]{1,0:T(8,128)S(1)}, f32[512,128]{1,0:T(8,128)S(1)}, u32[]{:S(2)}, u32[]{:S(2)}) collective-permute-start(f32[512,128]{1,0:T(8,128)S(1)} %slice.13), channel_id=1, source_target_pairs={{0,14},{1,15},{2,12},{3,13},{4,10},{5,11},{6,8},{7,9},{16,30},{17,... | collective-permute-start | bytes 786440 | tf_op jit(solution)/shard_map/ppermute | solution.py:346
  54.0 10.5 %collective-permute-start.8 = (f32[128,1024]{1,0:T(8,128)S(1)}, f32[128,1024]{1,0:T(8,128)S(1)}, u32[]{:S(2)}, u32[]{:S(2)}) collective-permute-start(f32[128,1024]{1,0:T(8,128)S(1)} %slice.15), channel_id=1, source_target_pairs={{0,64},{16,80},{32,96},{48,112},{64,0},{80,16},{96,32},{112,48},{1... | collective-permute-start | bytes 1572872 | tf_op jit(solution)/shard_map/ppermute | solution.py:354
  55.9 17.8 %collective-permute-start.9 = (f32[128,1024]{1,0:T(8,128)S(1)}, f32[128,1024]{1,0:T(8,128)S(1)}, u32[]{:S(2)}, u32[]{:S(2)}) collective-permute-start(f32[128,1024]{1,0:T(8,128)S(1)} %slice.15), channel_id=1, source_target_pairs={{0,128},{16,144},{32,160},{48,176},{64,192},{80,208},{96,224},{112... | collective-permute-start | bytes 1572872 | tf_op jit(solution)/shard_map/ppermute | solution.py:354
  73.9 52.5 %copy-start = (f32[256,1024]{1,0:T(8,128)}, f32[256,1024]{1,0:T(8,128)S(1)}, u32[]{:S(2)}) copy-start(f32[256,1024]{1,0:T(8,128)S(1)} %pad_maximum_fusion.refs_0_) | copy-start | bytes 3145732
  89.0 37.4 %collective-permute-start.10 = (f32[256,1024]{1,0:T(8,128)S(1)}, f32[256,1024]{1,0:T(8,128)S(1)}, u32[]{:S(2)}, u32[]{:S(2)}) collective-permute-start(f32[256,1024]{1,0:T(8,128)S(1)} %pad_maximum_fusion.refs_0_), channel_id=1, source_target_pairs={{16,0},{32,16},{48,32},{0,48},{80,64},{96,80},{112,96},{64,112},{1... | collective-permute-start | bytes 3145736 | tf_op jit(solution)/shard_map/ppermute | solution.py:363
  90.6 35.8 %collective-permute-start.11 = (f32[256,1024]{1,0:T(8,128)S(1)}, f32[256,1024]{1,0:T(8,128)S(1)}, u32[]{:S(2)}, u32[]{:S(2)}) collective-permute-start(f32[256,1024]{1,0:T(8,128)S(1)} %pad_maximum_fusion.refs_0_), channel_id=1, source_target_pairs={{32,0},{48,16},{0,32},{16,48},{96,64},{112,80},{64,96},{80,112},{1... | collective-permute-start | bytes 3145736 | tf_op jit(solution)/shard_map/ppermute | solution.py:363
  91.3 48.3 %collective-permute-start.12 = (f32[256,1024]{1,0:T(8,128)S(1)}, f32[256,1024]{1,0:T(8,128)S(1)}, u32[]{:S(2)}, u32[]{:S(2)}) collective-permute-start(f32[256,1024]{1,0:T(8,128)S(1)} %pad_maximum_fusion.refs_0_), channel_id=1, source_target_pairs={{48,0},{0,16},{16,32},{32,48},{112,64},{64,80},{80,96},{96,112},{1... | collective-permute-start | bytes 3145736 | tf_op jit(solution)/shard_map/ppermute | solution.py:363
  126.4 13.3 %copy-start.1 = (f32[256,1024]{1,0:T(8,128)}, f32[256,1024]{1,0:T(8,128)S(1)}, u32[]{:S(2)}) copy-start(f32[256,1024]{1,0:T(8,128)S(1)} %collective-permute-done.10.refs_1_) | copy-start | bytes 3145732
  126.4 13.2 %copy-start.2 = (f32[256,1024]{1,0:T(8,128)}, f32[256,1024]{1,0:T(8,128)S(1)}, u32[]{:S(2)}) copy-start(f32[256,1024]{1,0:T(8,128)S(1)} %collective-permute-done.11.refs_2_) | copy-start | bytes 3145732
  139.6 1.0 copy-start.3
Sparse Core Ops, SparseCore 0:
  40.4 48.5 all-gather.3
  90.7 38.3 all-gather.5

commit v4 on v2

--- a/solution.py
+++ b/solution.py
@@ -115,14 +115,19 @@
     place_ref, w_ref, mh_ref, ml_ref, corner_ref,
     x_ref, d_ref, work_ref, inv_ref, left_ref, right_ref, rest_ref, sems,
 ):
-    copies = []
-    for j in range(STEPS):
-        for h, slot in enumerate((j, other_half(j))):
-            dst = x_ref.at[h * HALF : (h + 1) * HALF, j * BLOCK : (j + 1) * BLOCK]
-            copies.append(pltpu.make_async_copy(w_ref.at[slot], dst, sems.at[slot]))
-    for copy in copies:
+    quarters = x_ref.reshape(2, SIDE, 2, 2, BLOCK // 4, WIDTH)
+    first, later = [], []
+    for slot in range(2 * STEPS):
+        b, k = (0, slot) if slot < STEPS else (1, other_half(slot))
+        for side in range(SIDE):
+            a, y = (0, side) if side < 2 else (1, SIDE - 1 - side)
+            dst = quarters.at[y, :, b, a, :, k * BLOCK : (k + 1) * BLOCK]
+            copy = pltpu.make_async_copy(w_ref.at[slot, side], dst, sems.at[slot * SIDE + side])
+            (first if y == 0 and k == 0 else later).append(copy)
+    for copy in first + later:
         copy.start()
-    copies[0].wait()
+    for copy in first:
+        copy.wait()
     r = lax.broadcasted_iota(jnp.int32, (BLOCK, BLOCK), 0)
     c = lax.broadcasted_iota(jnp.int32, (BLOCK, BLOCK), 1)
     work_ref[:, :BLOCK] = x_ref[:BLOCK, :BLOCK]
@@ -176,7 +181,7 @@
         return 0
 
     factor_block([])
-    for copy in copies[1:]:
+    for copy in later:
         copy.wait()
     prepare(0)
     lax.fori_loop(1, STEPS, step, 0)
@@ -210,7 +215,7 @@
             pltpu.VMEM((WIDTH, 2 * BLOCK), bf16),
             pltpu.VMEM((2 * BLOCK, WIDTH), bf16),
             pltpu.VMEM((BLOCK, WIDTH), bf16),
-            pltpu.SemaphoreType.DMA((2 * STEPS,)),
+            pltpu.SemaphoreType.DMA((2 * STEPS * SIDE,)),
         ],
         compiler_params=pltpu.CompilerParams(vmem_limit_bytes=24 * 2**20),
         cost_estimate=pl.CostEstimate(flops=40_000_000_000, bytes_accessed=2**23, transcendentals=0),
@@ -317,16 +322,22 @@
     in_hbm = lambda a: pltpu.with_memory_space_constraint(a, pltpu.HBM)
 
     quarter = BLOCK // 4
+    corner = blocked[:BLOCK, :BLOCK]
     parts = []
-    for g in range(4):
-        pairs = [
-            (i * cols + k, (4 * (i % 4) + g) * cols + (k if i < 4 else other_half(k))) for i in span for k in span
-        ]
-        parts.append(lax.ppermute(blocked[g * quarter : (g + 1) * quarter, :BLOCK], ("prow", "pcol"), pairs))
-    part = (parts[0] + parts[1]) + (parts[2] + parts[3])
+    for b, a in ((0, 1), (1, 0), (1, 1)):
+        pairs = []
+        for i in span:
+            to_row = (SIDE - 1 - i // SIDE) * SIDE + i % SIDE if a else i
+            for k in span:
+                pairs.append((i * cols + k, to_row * cols + (other_half(k) if b else k)))
+        at = (2 * b + a) * quarter
+        parts.append(lax.ppermute(corner[at : at + quarter], ("prow", "pcol"), pairs))
+    stays = (row < STEPS) & (col < STEPS)
+    part = jnp.where(stays, corner[:quarter], parts[0] + parts[1] + parts[2])
     lower = lax.ppermute(blocked[HALF:, :BLOCK], "pcol", [(k, other_half(k)) for k in span])
     strip = lax.all_to_all(jnp.broadcast_to(part, (rows, quarter, BLOCK)), "prow", 0, 0)
     window = lax.all_gather(strip.reshape(HALF, BLOCK), "pcol", axis=0)
+    window = window.reshape(cols, SIDE, SIDE, quarter, BLOCK)
     payload = jnp.where(col < STEPS, blocked[:HALF, :BLOCK], lower)
 
     own = blocked[:BLOCK]

time: 167 us -> 165 us (0.988)
  blocking collectives: 18.4 us -> 11.7 us
  starting transfers between devices: 24.3 us -> 27.1 us
  waiting for transfers between devices: 43.4 us -> 45.7 us
    all_to_all x1, blocking collectives: 18.4 us -> 11.7 us  [per_device(): lax.all_to_all(jnp.broadcast_to(part, (rows, quarter, BLOCK)), 'prow', 0, 0)]
    ppermute x1, starting transfers between devices: 2.94 us -> 6.85 us  [per_device(): lax.ppermute(blocked[HALF:, :BLOCK], 'pcol', [(k, other_half(k)) for k in...]
    ppermute x3, waiting for transfers between devices: 10.2 us -> 12.4 us  [per_device(): lax.ppermute(pair, 'prow', [(r // SIDE * SIDE + (r + d) % SIDE, r) for r...]
    ppermute x4 -> x3, starting transfers between devices: 12.8 us -> 12.1 us  [per_device(): parts.append(lax.ppermute(corner[at:at + quarter], ('prow', 'pcol'), pairs))]
  transfers between devices with their start and end apart: 13 -> 12, of which waited for: 6 -> 6; matrix products, arithmetic and copies ran while one was open for 3% -> 3% of each run, Pallas kernels for 29% -> 29%
where the time goes in v4:
time: 165 us
  Pallas kernels  58.8 us (36%)
  waiting for transfers between devices  45.7 us (28%)
  starting transfers between devices  27.1 us (16%)
  between operations  13.6 us (8%)
  blocking collectives  11.7 us (7%)
  local copies, waits for them, and re-layouts  3.81 us (2%)
  other arithmetic  3.74 us (2%)
    pallas_call x1, Pallas kernels, factor(): pl.pallas_call(factor_kernel, in_specs=[pl.BlockSpec(memory_space=pltpu.S...  34.9 us
    all_gather x1, waiting for transfers between devices, per_device(): window = lax.all_gather(strip.reshape(HALF, BLOCK), 'pcol', axis=0)  17.6 us
    pallas_call x1, Pallas kernels, apply(): pl.pallas_call(apply_kernel, in_specs=[pl.BlockSpec(memory_space=pltpu.SM...  12.6 us
    ppermute x3, waiting for transfers between devices, per_device(): lax.ppermute(own, 'prow', [(a * SIDE + x, b * SIDE + x) for a, b in move...  12.5 us
    ppermute x3, waiting for transfers between devices, per_device(): lax.ppermute(pair, 'prow', [(r // SIDE * SIDE + (r + d) % SIDE, r) for r...  12.4 us
    ppermute x3, starting transfers between devices, per_device(): parts.append(lax.ppermute(corner[at:at + quarter], ('prow', 'pcol'), pairs))  12.1 us
    all_to_all x1, blocking collectives, per_device(): lax.all_to_all(jnp.broadcast_to(part, (rows, quarter, BLOCK)), 'prow', 0, 0)  11.7 us
    pallas_call x1, Pallas kernels, update(): pl.pallas_call(update_kernel, grid=(WIDTH // CHUNK,), in_specs=[pl.BlockS...  11.3 us
  transfers between devices with their start and end apart: 12, of which 6 were waited for; matrix products, arithmetic and copies ran while one was open for 3% of the time, Pallas kernels for 29%

profile of v4, /device:TPU:1, one launch (start us, length us, event | category | flops | bytes accessed | tf_op | source)
XLA Modules:
  0.0 164.5 jit_solution(7102981749563697162)
XLA Ops:
  6.5 0.8 fusion
  7.3 5.4 %collective-permute-start.1 = (f32[32,128]{1,0:T(8,128)S(1)}, f32[32,128]{1,0:T(8,128)S(1)}, u32[]{:S(2)}, u32[]{:S(2)}) collective-permute-start(f32[32,128]{1,0:T(8,128)S(1)} %get-tuple-element.23), channel_id=1, source_target_pairs={{0,192},{1,193},{2,194},{3,195},{4,196},{5,197},{6,198},{7,199},{1... | collective-permute-start | bytes 49160 | tf_op jit(solution)/shard_map/ppermute | solution.py:334
  12.7 3.5 %collective-permute-start.2 = (f32[32,128]{1,0:T(8,128)S(1)}, f32[32,128]{1,0:T(8,128)S(1)}, u32[]{:S(2)}, u32[]{:S(2)}) collective-permute-start(f32[32,128]{1,0:T(8,128)S(1)} %get-tuple-element.21), channel_id=1, source_target_pairs={{0,14},{1,15},{2,12},{3,13},{4,10},{5,11},{6,8},{7,9},{16,30},{17,... | collective-permute-start | bytes 49160 | tf_op jit(solution)/shard_map/ppermute | solution.py:334
  16.3 3.1 %collective-permute-start.3 = (f32[32,128]{1,0:T(8,128)S(1)}, f32[32,128]{1,0:T(8,128)S(1)}, u32[]{:S(2)}, u32[]{:S(2)}) collective-permute-start(f32[32,128]{1,0:T(8,128)S(1)} %get-tuple-element.22), channel_id=1, source_target_pairs={{0,206},{1,207},{2,204},{3,205},{4,202},{5,203},{6,200},{7,201},{1... | collective-permute-start | bytes 49160 | tf_op jit(solution)/shard_map/ppermute | solution.py:334
  19.4 0.8 collective-permute-done.3
  20.2 0.7 add_select_fusion
  21.0 11.7 %all_to_all.5 = f32[16,32,128]{2,1,0:T(8,128)} all-to-all(f32[16,32,128]{2,1,0:T(8,128)S(1)} %broadcast_in_dim.3), channel_id=1, replica_groups=mesh['prow'=16,'pcol'=16] {'prow'}, dimensions={0} | all-to-all | bytes 524288 | tf_op jit(solution)/shard_map/all_to_all | solution.py:338
  32.7 0.0 all-gather.4.cloned.1.call-update
  32.7 0.0 all-gather.6.cloned.1.call-start
  32.7 1.1 slice.32
  33.8 2.5 %collective-permute-start.4 = (f32[128,1024]{1,0:T(8,128)S(1)}, f32[128,1024]{1,0:T(8,128)S(1)}, u32[]{:S(2)}, u32[]{:S(2)}) collective-permute-start(f32[128,1024]{1,0:T(8,128)S(1)} %slice.32), channel_id=1, source_target_pairs={{0,192},{16,208},{32,224},{48,240},{64,128},{80,144},{96,160},{112... | collective-permute-start | bytes 1572872 | tf_op jit(solution)/shard_map/ppermute | solution.py:346
  36.3 1.0 slice.27
  37.3 6.8 %collective-permute-start = (f32[512,128]{1,0:T(8,128)S(1)}, f32[512,128]{1,0:T(8,128)S(1)}, u32[]{:S(2)}, u32[]{:S(2)}) collective-permute-start(f32[512,128]{1,0:T(8,128)S(1)} %slice.27), channel_id=1, source_target_pairs={{0,14},{1,15},{2,12},{3,13},{4,10},{5,11},{6,8},{7,9},{16,30},{17,... | collective-permute-start | bytes 786440 | tf_op jit(solution)/shard_map/ppermute | solution.py:337
  44.2 1.9 %collective-permute-start.5 = (f32[128,1024]{1,0:T(8,128)S(1)}, f32[128,1024]{1,0:T(8,128)S(1)}, u32[]{:S(2)}, u32[]{:S(2)}) collective-permute-start(f32[128,1024]{1,0:T(8,128)S(1)} %slice.32), channel_id=1, source_target_pairs={{0,64},{16,80},{32,96},{48,112},{64,0},{80,16},{96,32},{112,48},{1... | collective-permute-start | bytes 1572872 | tf_op jit(solution)/shard_map/ppermute | solution.py:346
  46.1 1.3 collective-permute-start.6
  47.4 2.4 %collective-permute-done = f32[512,128]{1,0:T(8,128)S(1)} collective-permute-done((f32[512,128]{1,0:T(8,128)S(1)}, f32[512,128]{1,0:T(8,128)S(1)}, u32[]{:S(2)}, u32[]{:S(2)}) %collective-permute-start) | collective-permute-done | bytes 262176 | tf_op jit(solution)/shard_map/ppermute | solution.py:337
  49.8 1.7 %slice_select_fusion = f32[512,128]{1,0:T(8,128)} fusion(f32[512,128]{1,0:T(8,128)S(1)} %collective-permute-done, f32[1024,1024]{1,0:T(8,128)} %a_ref.1, pred[]{:T(512)S(6)} %lt.8), kind=kLoop, calls=%fused_computation.1 | loop fusion | flops 65536 | bytes 786433 | tf_op jit(solution)/shard_map/jit(_where)/select_n | solution.py:341
  51.5 1.1 broadcast_select_fusion.1
  52.6 3.3 %collective-permute-done.5 = f32[128,1024]{1,0:T(8,128)S(1)} collective-permute-done((f32[128,1024]{1,0:T(8,128)S(1)}, f32[128,1024]{1,0:T(8,128)S(1)}, u32[]{:S(2)}, u32[]{:S(2)}) %collective-permute-start.5) | collective-permute-done | bytes 524320 | tf_op jit(solution)/shard_map/ppermute | solution.py:346
  55.8 9.2 %collective-permute-done.6 = f32[128,1024]{1,0:T(8,128)S(1)} collective-permute-done((f32[128,1024]{1,0:T(8,128)S(1)}, f32[128,1024]{1,0:T(8,128)S(1)}, u32[]{:S(2)}, u32[]{:S(2)}) %collective-permute-start.6) | collective-permute-done | bytes 524320 | tf_op jit(solution)/shard_map/ppermute | solution.py:346
  65.1 0.1 broadcast_select_fusion
  65.1 0.1 pad_maximum_fusion.refs_0_
  65.3 17.6 %all-gather.4.cloned.1.call-done = f32[16,512,128]{2,1,0:T(8,128)} async-done(((f32[1,512,128]{2,1,0:T(8,128)}), f32[16,512,128]{2,1,0:T(8,128)}) %all-gather.4.cloned.1.call-update) | async-done | bytes 4194320 | tf_op jit(solution)/shard_map/all_gather | solution.py:339
  82.9 0.1 pad_add_fusion.place_ref
  83.0 0.7 collective-permute-start.7
  83.7 1.7 %collective-permute-start.8 = (f32[256,1024]{1,0:T(8,128)S(1)}, f32[256,1024]{1,0:T(8,128)S(1)}, u32[]{:S(2)}, u32[]{:S(2)}) collective-permute-start(f32[256,1024]{1,0:T(8,128)S(1)} %pad_maximum_fusion.refs_0_), channel_id=1, source_target_pairs={{32,0},{48,16},{0,32},{16,48},{96,64},{112,80},{64,96},{80,112},{1... | collective-permute-start | bytes 3145736 | tf_op jit(solution)/shard_map/ppermute | solution.py:355
  85.4 34.9 %factor.1 = (bf16[1024,1024]{1,0:T(8,128)(2,1)S(1)}, bf16[1024,1024]{1,0:T(8,128)(2,1)S(1)}, f32[128,128]{1,0:T(8,128)S(1)}) custom-call(s32[2]{0:T(128)S(1)} %pad_add_fusion.place_ref, f32[16,4,4,32,128]{4,3,2,1,0:T(8,128)} %bitcast.7), custom_call_target="tpu_custom_call" | custom-call | flops 40000000000 | bytes 8388608 | tf_op jit(solution)/shard_map/factor/pallas_call | solution.py:201
  120.3 12.4 %collective-permute-done.9.refs_3_ = f32[256,1024]{1,0:T(8,128)S(1)} collective-permute-done((f32[256,1024]{1,0:T(8,128)S(1)}, f32[256,1024]{1,0:T(8,128)S(1)}, u32[]{:S(2)}, u32[]{:S(2)}) %collective-permute-start.9) | collective-permute-done | bytes 1048608 | tf_op jit(solution)/shard_map/ppermute | solution.py:355
  132.7 1.0 copy-done.3
  133.7 12.6 %apply.1 = (bf16[1024,1024]{1,0:T(8,128)(2,1)}, bf16[1024,1024]{1,0:T(8,128)(2,1)}, f32[128,128]{1,0:T(8,128)}) custom-call(s32[2]{0:T(128)S(1)} %pad_add_fusion.place_ref, bf16[1024,1024]{1,0:T(8,128)(2,1)S(1)} %get-tuple-element.15.mh, bf16[1024,1024]{1,0:T(8,128)(2,1)S(1)} %get-tuple-element.16.ml, f32[128,128]{1,0:T(8,128)S(1)} %get-tuple-element.17.corner_ref, ...), custom_call_target="tpu_custom_call" | custom-call | flops 10000000000 | bytes 8388608 | tf_op jit(solution)/shard_map/apply/pallas_call | solution.py:264
  146.3 0.0 all-gather.6.cloned.1.call-done
  146.4 11.3 %update.1 = f32[1024,1024]{1,0:T(8,128)} custom-call(s32[2]{0:T(128)S(1)} %pad_add_fusion.place_ref, f32[1024,1024]{1,0:T(8,128)} %a_ref.1, f32[16,512,128]{2,1,0:T(8,128)} %bitcast.5, bf16[1024,1024]{1,0:T(8,128)(2,1)} %get-tuple-element.18.yh_ref, bf16[1024,1024]{1,0:T(8,128)(2,1)} %get-tuple-element.19.yl_ref, f32[128,128]{1,0:T(8,128)} %get-tuple-element.20.corner_ref), custom_call_target="tpu_custom_call" | custom-call | tf_op jit(solution)/shard_map/update/pallas_call | solution.py:300
  (16 shorter events, 0.1 us)
Async XLA Ops:
  6.5 76.3 %all-gather.4.cloned.1.call-start = ((), (), s32[]{:S(2)}) async-start(), calls=%async_computation.1 | async-start | bytes 4456448 | tf_op jit(solution)/shard_map/all_gather | solution.py:339
  7.3 12.1 %collective-permute-start.1 = (f32[32,128]{1,0:T(8,128)S(1)}, f32[32,128]{1,0:T(8,128)S(1)}, u32[]{:S(2)}, u32[]{:S(2)}) collective-permute-start(f32[32,128]{1,0:T(8,128)S(1)} %get-tuple-element.23), channel_id=1, source_target_pairs={{0,192},{1,193},{2,194},{3,195},{4,196},{5,197},{6,198},{7,199},{1... | collective-permute-start | bytes 49160 | tf_op jit(solution)/shard_map/ppermute | solution.py:334
  12.7 6.7 %collective-permute-start.2 = (f32[32,128]{1,0:T(8,128)S(1)}, f32[32,128]{1,0:T(8,128)S(1)}, u32[]{:S(2)}, u32[]{:S(2)}) collective-permute-start(f32[32,128]{1,0:T(8,128)S(1)} %get-tuple-element.21), channel_id=1, source_target_pairs={{0,14},{1,15},{2,12},{3,13},{4,10},{5,11},{6,8},{7,9},{16,30},{17,... | collective-permute-start | bytes 49160 | tf_op jit(solution)/shard_map/ppermute | solution.py:334
  16.3 4.0 %collective-permute-start.3 = (f32[32,128]{1,0:T(8,128)S(1)}, f32[32,128]{1,0:T(8,128)S(1)}, u32[]{:S(2)}, u32[]{:S(2)}) collective-permute-start(f32[32,128]{1,0:T(8,128)S(1)} %get-tuple-element.22), channel_id=1, source_target_pairs={{0,206},{1,207},{2,204},{3,205},{4,202},{5,203},{6,200},{7,201},{1... | collective-permute-start | bytes 49160 | tf_op jit(solution)/shard_map/ppermute | solution.py:334
  32.7 113.7 %all-gather.6.cloned.1.call-start = ((), (), s32[]{:S(2)}) async-start(), calls=%async_computation.2 | async-start | bytes 4456448 | tf_op jit(solution)/shard_map/all_gather | solution.py:352
  33.8 17.7 %collective-permute-start.4 = (f32[128,1024]{1,0:T(8,128)S(1)}, f32[128,1024]{1,0:T(8,128)S(1)}, u32[]{:S(2)}, u32[]{:S(2)}) collective-permute-start(f32[128,1024]{1,0:T(8,128)S(1)} %slice.32), channel_id=1, source_target_pairs={{0,192},{16,208},{32,224},{48,240},{64,128},{80,144},{96,160},{112... | collective-permute-start | bytes 1572872 | tf_op jit(solution)/shard_map/ppermute | solution.py:346
  37.3 12.5 %collective-permute-start = (f32[512,128]{1,0:T(8,128)S(1)}, f32[512,128]{1,0:T(8,128)S(1)}, u32[]{:S(2)}, u32[]{:S(2)}) collective-permute-start(f32[512,128]{1,0:T(8,128)S(1)} %slice.27), channel_id=1, source_target_pairs={{0,14},{1,15},{2,12},{3,13},{4,10},{5,11},{6,8},{7,9},{16,30},{17,... | collective-permute-start | bytes 786440 | tf_op jit(solution)/shard_map/ppermute | solution.py:337
  44.2 11.7 %collective-permute-start.5 = (f32[128,1024]{1,0:T(8,128)S(1)}, f32[128,1024]{1,0:T(8,128)S(1)}, u32[]{:S(2)}, u32[]{:S(2)}) collective-permute-start(f32[128,1024]{1,0:T(8,128)S(1)} %slice.32), channel_id=1, source_target_pairs={{0,64},{16,80},{32,96},{48,112},{64,0},{80,16},{96,32},{112,48},{1... | collective-permute-start | bytes 1572872 | tf_op jit(solution)/shard_map/ppermute | solution.py:346
  46.1 19.0 %collective-permute-start.6 = (f32[128,1024]{1,0:T(8,128)S(1)}, f32[128,1024]{1,0:T(8,128)S(1)}, u32[]{:S(2)}, u32[]{:S(2)}) collective-permute-start(f32[128,1024]{1,0:T(8,128)S(1)} %slice.32), channel_id=1, source_target_pairs={{0,128},{16,144},{32,160},{48,176},{64,192},{80,208},{96,224},{112... | collective-permute-start | bytes 1572872 | tf_op jit(solution)/shard_map/ppermute | solution.py:346
  65.2 55.0 %copy-start = (f32[256,1024]{1,0:T(8,128)}, f32[256,1024]{1,0:T(8,128)S(1)}, u32[]{:S(2)}) copy-start(f32[256,1024]{1,0:T(8,128)S(1)} %pad_maximum_fusion.refs_0_) | copy-start | bytes 3145732
  83.0 37.3 %collective-permute-start.7 = (f32[256,1024]{1,0:T(8,128)S(1)}, f32[256,1024]{1,0:T(8,128)S(1)}, u32[]{:S(2)}, u32[]{:S(2)}) collective-permute-start(f32[256,1024]{1,0:T(8,128)S(1)} %pad_maximum_fusion.refs_0_), channel_id=1, source_target_pairs={{16,0},{32,16},{48,32},{0,48},{80,64},{96,80},{112,96},{64,112},{1... | collective-permute-start | bytes 3145736 | tf_op jit(solution)/shard_map/ppermute | solution.py:355
  83.7 36.6 %collective-permute-start.8 = (f32[256,1024]{1,0:T(8,128)S(1)}, f32[256,1024]{1,0:T(8,128)S(1)}, u32[]{:S(2)}, u32[]{:S(2)}) collective-permute-start(f32[256,1024]{1,0:T(8,128)S(1)} %pad_maximum_fusion.refs_0_), channel_id=1, source_target_pairs={{32,0},{48,16},{0,32},{16,48},{96,64},{112,80},{64,96},{80,112},{1... | collective-permute-start | bytes 3145736 | tf_op jit(solution)/shard_map/ppermute | solution.py:355
  85.4 47.4 %collective-permute-start.9 = (f32[256,1024]{1,0:T(8,128)S(1)}, f32[256,1024]{1,0:T(8,128)S(1)}, u32[]{:S(2)}, u32[]{:S(2)}) collective-permute-start(f32[256,1024]{1,0:T(8,128)S(1)} %pad_maximum_fusion.refs_0_), channel_id=1, source_target_pairs={{48,0},{0,16},{16,32},{32,48},{112,64},{64,80},{80,96},{96,112},{1... | collective-permute-start | bytes 3145736 | tf_op jit(solution)/shard_map/ppermute | solution.py:355
  120.3 12.4 %copy-start.1 = (f32[256,1024]{1,0:T(8,128)}, f32[256,1024]{1,0:T(8,128)S(1)}, u32[]{:S(2)}) copy-start(f32[256,1024]{1,0:T(8,128)S(1)} %collective-permute-done.7.refs_1_) | copy-start | bytes 3145732
  120.3 12.4 %copy-start.2 = (f32[256,1024]{1,0:T(8,128)}, f32[256,1024]{1,0:T(8,128)S(1)}, u32[]{:S(2)}) copy-start(f32[256,1024]{1,0:T(8,128)S(1)} %collective-permute-done.8.refs_2_) | copy-start | bytes 3145732
  132.7 1.0 copy-start.3
Sparse Core Ops, SparseCore 0:
  32.8 50.0 all-gather.3
  84.7 37.1 all-gather.5

commit v5 on v4

--- a/solution.py
+++ b/solution.py
@@ -172,10 +172,10 @@
         u = dot_split_128(split(inverse), split(x_ref[here, after]))
         work_ref[:, :BLOCK] = x_ref[after, after] - dot_split_128(split(jnp.transpose(u)), split(u))
 
-    def step(k, _):
+    def step(k, _, lowest=1):
         others = [functools.partial(finish_row, k - 1, b) for b in range(STEPS)]
         others += [functools.partial(clear, k - 1)]
-        others += [functools.partial(trail, m, n) for n in range(STEPS // 2) for m in range(STEPS)]
+        others += [functools.partial(trail, m, n) for n in range(STEPS // 2) for m in range(lowest, STEPS)]
         factor_block(others)
         prepare(k)
         return 0
@@ -184,7 +184,8 @@
     for copy in later:
         copy.wait()
     prepare(0)
-    lax.fori_loop(1, STEPS, step, 0)
+    lax.fori_loop(1, STEPS // 2, step, 0)
+    lax.fori_loop(STEPS // 2, STEPS, functools.partial(step, lowest=STEPS // 2), 0)
     end = slice(WIDTH - BLOCK, WIDTH)
     x_ref[end, :] = dot_split_128(split(inv_ref[...]), split(x_ref[end, :]))
     x_ref[end, end] = inv_ref[...]
@@ -277,13 +278,40 @@
     )(place, mh, ml, corner, *across)
 
 
-def update_kernel(place_ref, a_ref, u_ref, yh_ref, yl_ref, corner_ref, out_ref):
+def update_kernel(place_ref, a_ref, u_ref, corner_ref, yh_hbm, yl_hbm, out_ref, yh, yl, sems):
     row, col, step = place_ref[0], place_ref[1], pl.program_id(0)
+    blocks = [slice(k, k + CHUNK) for k in range(0, WIDTH, CHUNK)]
+    arriving = [
+        [pltpu.make_async_copy(src.at[at], dst.at[at], sems.at[m, n]) for m, (src, dst) in enumerate(((yh_hbm, yh), (yl_hbm, yl)))]
+        for n, at in enumerate(blocks)
+    ]
+
+    @pl.when(step == 0)
+    def _():
+        for copies in arriving:
+            for copy in copies:
+                copy.start()
+
     slots = [jnp.where(step < HALF // CHUNK, j, other_half(j) - STEPS) for j in range(STEPS)]
-    u = split(jnp.concatenate([u_ref[s] for s in slots], 1))
-    product = dot_split(u, (yh_ref[...], yl_ref[...]))
-    out_ref[:, :BLOCK] = jnp.where(col < STEPS, product[:, :BLOCK], a_ref[:, :BLOCK] - product[:, :BLOCK])
-    out_ref[:, BLOCK:] = a_ref[:, BLOCK:] - product[:, BLOCK:]
+    uh, ul = split(jnp.concatenate([u_ref[s] for s in slots], 1))
+
+    def finish(product):
+        out_ref[:, :BLOCK] = jnp.where(col < STEPS, product[:, :BLOCK], a_ref[:, :BLOCK] - product[:, :BLOCK])
+        out_ref[:, BLOCK:] = a_ref[:, BLOCK:] - product[:, BLOCK:]
+
+    @pl.when(step == 0)
+    def _():
+        total = None
+        for copies, at in zip(arriving, blocks):
+            for copy in copies:
+                copy.wait()
+            part = dot_split((uh[:, at], ul[:, at]), (yh[at], yl[at]))
+            total = part if total is None else total + part
+        finish(total)
+
+    @pl.when(step > 0)
+    def _():
+        finish(dot_split((uh, ul), (yh[...], yl[...])))
 
     @pl.when((step == 0) & (row < STEPS))
     def _():
@@ -304,15 +332,20 @@
             pl.BlockSpec(memory_space=pltpu.SMEM),
             pl.BlockSpec((CHUNK, WIDTH), lambda i: (i, 0)),
             pl.BlockSpec((STEPS, CHUNK, BLOCK), lambda i: (i // per_half, i % per_half, 0)),
-            whole(WIDTH, WIDTH),
-            whole(WIDTH, WIDTH),
             whole(BLOCK, BLOCK),
+            pl.BlockSpec(memory_space=pltpu.HBM),
+            pl.BlockSpec(memory_space=pltpu.HBM),
         ],
         out_specs=pl.BlockSpec((CHUNK, WIDTH), lambda i: (i, 0)),
         out_shape=jax.ShapeDtypeStruct((WIDTH, WIDTH), f32),
+        scratch_shapes=[
+            pltpu.VMEM((WIDTH, WIDTH), bf16),
+            pltpu.VMEM((WIDTH, WIDTH), bf16),
+            pltpu.SemaphoreType.DMA((2, WIDTH // CHUNK)),
+        ],
         compiler_params=pltpu.CompilerParams(vmem_limit_bytes=28 * 2**20),
         name="update",
-    )(place, blocked, gathered, yh, yl, corner)
+    )(place, blocked, gathered, corner, yh, yl)
 
 
 def per_device(blocked):
@@ -324,7 +357,7 @@
     quarter = BLOCK // 4
     corner = blocked[:BLOCK, :BLOCK]
     parts = []
-    for b, a in ((0, 1), (1, 0), (1, 1)):
+    for b, a in ((1, 1), (1, 0), (0, 1)):
         pairs = []
         for i in span:
             to_row = (SIDE - 1 - i // SIDE) * SIDE + i % SIDE if a else i
@@ -356,7 +389,7 @@
 
     place = jnp.stack([row, col])
     mh, ml, corner = factor(place, in_hbm(window))
-    applied = apply(place, mh, ml, corner, [in_hbm(v) for v in across])
+    applied = apply(place, mh, ml, corner, across)
     return update(place, *(in_hbm(v) for v in (blocked, panels, *applied)))
 
 

time: 165 us -> 163 us (0.988)
  starting transfers between devices: 27.1 us -> 23.2 us
  blocking collectives: 11.7 us -> 14.2 us
  waiting for transfers between devices: 45.7 us -> 47.5 us
    ppermute x1, starting transfers between devices: 6.85 us -> 1.72 us  [per_device(): lax.ppermute(blocked[HALF:, :BLOCK], 'pcol', [(k, other_half(k)) for k in...]
    all_to_all x1, blocking collectives: 11.7 us -> 14.2 us  [per_device(): lax.all_to_all(jnp.broadcast_to(part, (rows, quarter, BLOCK)), 'prow', 0, 0)]
    ppermute x3, waiting for transfers between devices: 12.4 us -> 14.1 us  [per_device(): lax.ppermute(pair, 'prow', [(r // SIDE * SIDE + (r + d) % SIDE, r) for r...]
  transfers between devices with their start and end apart: 12 -> 12, of which waited for: 6 -> 6; matrix products, arithmetic and copies ran while one was open for 3% -> 3% of each run, Pallas kernels for 29% -> 28%
where the time goes in v5:
time: 163 us; the launch traced here: 162 us
  Pallas kernels  57.2 us (35%)
  waiting for transfers between devices  47.5 us (29%)
  starting transfers between devices  23.2 us (14%)
  blocking collectives  14.2 us (9%)
  between operations  13.6 us (8%)
  other arithmetic  3.75 us (2%)
  local copies, waits for them, and re-layouts  2.83 us (2%)
    pallas_call x1, Pallas kernels, factor(): pl.pallas_call(factor_kernel, in_specs=[pl.BlockSpec(memory_space=pltpu.S...  33.5 us
    all_gather x1, waiting for transfers between devices, per_device(): window = lax.all_gather(strip.reshape(HALF, BLOCK), 'pcol', axis=0)  17.7 us
    all_to_all x1, blocking collectives, per_device(): lax.all_to_all(jnp.broadcast_to(part, (rows, quarter, BLOCK)), 'prow', 0, 0)  14.2 us
    ppermute x3, waiting for transfers between devices, per_device(): lax.ppermute(pair, 'prow', [(r // SIDE * SIDE + (r + d) % SIDE, r) for r...  14.1 us
    ppermute x3, starting transfers between devices, per_device(): parts.append(lax.ppermute(corner[at:at + quarter], ('prow', 'pcol'), pairs))  13.3 us
    ppermute x3, waiting for transfers between devices, per_device(): lax.ppermute(own, 'prow', [(a * SIDE + x, b * SIDE + x) for a, b in move...  12.6 us
    pallas_call x1, Pallas kernels, update(): pl.pallas_call(update_kernel, grid=(WIDTH // CHUNK,), in_specs=[pl.BlockS...  12.3 us
    pallas_call x1, Pallas kernels, apply(): pl.pallas_call(apply_kernel, in_specs=[pl.BlockSpec(memory_space=pltpu.SM...  11.4 us
  transfers between devices with their start and end apart: 12, of which 6 were waited for; matrix products, arithmetic and copies ran while one was open for 3% of the time, Pallas kernels for 28%

profile of v5, /device:TPU:1, one launch (start us, length us, event | category | flops | bytes accessed | tf_op | source)
XLA Modules:
  0.0 162.2 jit_solution(1677874666101096796)
XLA Ops:
  6.5 0.8 fusion
  7.3 10.7 %collective-permute-start.1 = (f32[32,128]{1,0:T(8,128)S(1)}, f32[32,128]{1,0:T(8,128)S(1)}, u32[]{:S(2)}, u32[]{:S(2)}) collective-permute-start(f32[32,128]{1,0:T(8,128)S(1)} %get-tuple-element.23), channel_id=1, source_target_pairs={{0,206},{1,207},{2,204},{3,205},{4,202},{5,203},{6,200},{7,201},{1... | collective-permute-start | bytes 49160 | tf_op jit(solution)/shard_map/ppermute | solution.py:367
  18.0 1.3 collective-permute-start.2
  19.3 1.3 collective-permute-start.3
  20.7 0.8 collective-permute-done.3
  21.5 0.7 add_select_fusion
  22.2 14.2 %all_to_all.5 = f32[16,32,128]{2,1,0:T(8,128)} all-to-all(f32[16,32,128]{2,1,0:T(8,128)S(1)} %broadcast_in_dim.3), channel_id=1, replica_groups=mesh['prow'=16,'pcol'=16] {'prow'}, dimensions={0} | all-to-all | bytes 524288 | tf_op jit(solution)/shard_map/all_to_all | solution.py:371
  36.5 0.0 all-gather.4.cloned.1.call-update
  36.5 0.0 all-gather.6.cloned.1.call-start
  36.5 1.1 slice.32
  37.6 2.5 %collective-permute-start.4 = (f32[128,1024]{1,0:T(8,128)S(1)}, f32[128,1024]{1,0:T(8,128)S(1)}, u32[]{:S(2)}, u32[]{:S(2)}) collective-permute-start(f32[128,1024]{1,0:T(8,128)S(1)} %slice.32), channel_id=1, source_target_pairs={{0,192},{16,208},{32,224},{48,240},{64,128},{80,144},{96,160},{112... | collective-permute-start | bytes 1572872 | tf_op jit(solution)/shard_map/ppermute | solution.py:379
  40.1 1.0 slice.27
  41.1 1.7 %collective-permute-start = (f32[512,128]{1,0:T(8,128)S(1)}, f32[512,128]{1,0:T(8,128)S(1)}, u32[]{:S(2)}, u32[]{:S(2)}) collective-permute-start(f32[512,128]{1,0:T(8,128)S(1)} %slice.27), channel_id=1, source_target_pairs={{0,14},{1,15},{2,12},{3,13},{4,10},{5,11},{6,8},{7,9},{16,30},{17,... | collective-permute-start | bytes 786440 | tf_op jit(solution)/shard_map/ppermute | solution.py:370
  42.8 1.9 %collective-permute-start.5 = (f32[128,1024]{1,0:T(8,128)S(1)}, f32[128,1024]{1,0:T(8,128)S(1)}, u32[]{:S(2)}, u32[]{:S(2)}) collective-permute-start(f32[128,1024]{1,0:T(8,128)S(1)} %slice.32), channel_id=1, source_target_pairs={{0,64},{16,80},{32,96},{48,112},{64,0},{80,16},{96,32},{112,48},{1... | collective-permute-start | bytes 1572872 | tf_op jit(solution)/shard_map/ppermute | solution.py:379
  44.8 1.3 collective-permute-start.6
  46.1 2.2 %collective-permute-done = f32[512,128]{1,0:T(8,128)S(1)} collective-permute-done((f32[512,128]{1,0:T(8,128)S(1)}, f32[512,128]{1,0:T(8,128)S(1)}, u32[]{:S(2)}, u32[]{:S(2)}) %collective-permute-start) | collective-permute-done | bytes 262176 | tf_op jit(solution)/shard_map/ppermute | solution.py:370
  48.3 1.7 %slice_select_fusion = f32[512,128]{1,0:T(8,128)} fusion(f32[512,128]{1,0:T(8,128)S(1)} %collective-permute-done, f32[1024,1024]{1,0:T(8,128)} %a_ref.1, pred[]{:T(512)S(6)} %lt.8), kind=kLoop, calls=%fused_computation.1 | loop fusion | flops 65536 | bytes 786433 | tf_op jit(solution)/shard_map/jit(_where)/select_n | solution.py:374
  50.0 1.1 broadcast_select_fusion.1
  51.1 3.4 %collective-permute-done.5 = f32[128,1024]{1,0:T(8,128)S(1)} collective-permute-done((f32[128,1024]{1,0:T(8,128)S(1)}, f32[128,1024]{1,0:T(8,128)S(1)}, u32[]{:S(2)}, u32[]{:S(2)}) %collective-permute-start.5) | collective-permute-done | bytes 524320 | tf_op jit(solution)/shard_map/ppermute | solution.py:379
  54.5 9.2 %collective-permute-done.6 = f32[128,1024]{1,0:T(8,128)S(1)} collective-permute-done((f32[128,1024]{1,0:T(8,128)S(1)}, f32[128,1024]{1,0:T(8,128)S(1)}, u32[]{:S(2)}, u32[]{:S(2)}) %collective-permute-start.6) | collective-permute-done | bytes 524320 | tf_op jit(solution)/shard_map/ppermute | solution.py:379
  63.7 0.1 broadcast_select_fusion
  63.8 0.1 pad_maximum_fusion.refs_0_
  63.9 17.7 %all-gather.4.cloned.1.call-done = f32[16,512,128]{2,1,0:T(8,128)} async-done(((f32[1,512,128]{2,1,0:T(8,128)}), f32[16,512,128]{2,1,0:T(8,128)}) %all-gather.4.cloned.1.call-update) | async-done | bytes 4194320 | tf_op jit(solution)/shard_map/all_gather | solution.py:372
  81.6 0.0 all-gather.6.cloned.1.call-update
  81.7 0.1 pad_add_fusion.place_ref
  81.7 0.9 collective-permute-start.7
  82.6 1.5 collective-permute-start.8
  84.1 33.5 %factor.1 = (bf16[1024,1024]{1,0:T(8,128)(2,1)S(1)}, bf16[1024,1024]{1,0:T(8,128)(2,1)S(1)}, f32[128,128]{1,0:T(8,128)S(1)}) custom-call(s32[2]{0:T(128)S(1)} %pad_add_fusion.place_ref, f32[16,4,4,32,128]{4,3,2,1,0:T(8,128)} %bitcast.7), custom_call_target="tpu_custom_call" | custom-call | flops 40000000000 | bytes 8388608 | tf_op jit(solution)/shard_map/factor/pallas_call | solution.py:202
  117.6 14.1 %collective-permute-done.9.refs_3_ = f32[256,1024]{1,0:T(8,128)S(1)} collective-permute-done((f32[256,1024]{1,0:T(8,128)S(1)}, f32[256,1024]{1,0:T(8,128)S(1)}, u32[]{:S(2)}, u32[]{:S(2)}) %collective-permute-start.9) | collective-permute-done | bytes 1048608 | tf_op jit(solution)/shard_map/ppermute | solution.py:388
  131.7 11.4 %apply.1 = (bf16[1024,1024]{1,0:T(8,128)(2,1)}, bf16[1024,1024]{1,0:T(8,128)(2,1)}, f32[128,128]{1,0:T(8,128)}) custom-call(s32[2]{0:T(128)S(1)} %pad_add_fusion.place_ref, bf16[1024,1024]{1,0:T(8,128)(2,1)S(1)} %get-tuple-element.15.mh, bf16[1024,1024]{1,0:T(8,128)(2,1)S(1)} %get-tuple-element.16.ml, f32[128,128]{1,0:T(8,128)S(1)} %get-tuple-element.17.corner_ref, ...), custom_call_target="tpu_custom_call" | custom-call | flops 10000000000 | bytes 8388608 | tf_op jit(solution)/shard_map/apply/pallas_call | solution.py:265
  143.1 0.0 all-gather.6.cloned.1.call-done
  143.1 12.3 %update.1 = f32[1024,1024]{1,0:T(8,128)} custom-call(s32[2]{0:T(128)S(1)} %pad_add_fusion.place_ref, f32[1024,1024]{1,0:T(8,128)} %a_ref.1, f32[16,512,128]{2,1,0:T(8,128)} %bitcast.5, f32[128,128]{1,0:T(8,128)} %get-tuple-element.18.corner_ref, bf16[1024,1024]{1,0:T(8,128)(2,1)} %get-tuple-element.19.yh_hbm, bf16[1024,1024]{1,0:T(8,128)(2,1)} %get-tuple-element.20.yl_hbm), custom_call_target="tpu_custom_call" | custom-call | tf_op jit(solution)/shard_map/update/pallas_call | solution.py:328
  (8 shorter events, 0.0 us)
Async XLA Ops:
  6.5 75.1 %all-gather.4.cloned.1.call-start = ((), (), s32[]{:S(2)}) async-start(), calls=%async_computation.1 | async-start | bytes 4456448 | tf_op jit(solution)/shard_map/all_gather | solution.py:372
  7.3 13.4 %collective-permute-start.1 = (f32[32,128]{1,0:T(8,128)S(1)}, f32[32,128]{1,0:T(8,128)S(1)}, u32[]{:S(2)}, u32[]{:S(2)}) collective-permute-start(f32[32,128]{1,0:T(8,128)S(1)} %get-tuple-element.23), channel_id=1, source_target_pairs={{0,206},{1,207},{2,204},{3,205},{4,202},{5,203},{6,200},{7,201},{1... | collective-permute-start | bytes 49160 | tf_op jit(solution)/shard_map/ppermute | solution.py:367
  18.0 2.6 %collective-permute-start.2 = (f32[32,128]{1,0:T(8,128)S(1)}, f32[32,128]{1,0:T(8,128)S(1)}, u32[]{:S(2)}, u32[]{:S(2)}) collective-permute-start(f32[32,128]{1,0:T(8,128)S(1)} %get-tuple-element.21), channel_id=1, source_target_pairs={{0,14},{1,15},{2,12},{3,13},{4,10},{5,11},{6,8},{7,9},{16,30},{17,... | collective-permute-start | bytes 49160 | tf_op jit(solution)/shard_map/ppermute | solution.py:367
  19.3 2.1 %collective-permute-start.3 = (f32[32,128]{1,0:T(8,128)S(1)}, f32[32,128]{1,0:T(8,128)S(1)}, u32[]{:S(2)}, u32[]{:S(2)}) collective-permute-start(f32[32,128]{1,0:T(8,128)S(1)} %get-tuple-element.22), channel_id=1, source_target_pairs={{0,192},{1,193},{2,194},{3,195},{4,196},{5,197},{6,198},{7,199},{1... | collective-permute-start | bytes 49160 | tf_op jit(solution)/shard_map/ppermute | solution.py:367
  36.5 106.6 %all-gather.6.cloned.1.call-start = ((), (), s32[]{:S(2)}) async-start(), calls=%async_computation.2 | async-start | bytes 4456448 | tf_op jit(solution)/shard_map/all_gather | solution.py:385
  37.6 12.4 %collective-permute-start.4 = (f32[128,1024]{1,0:T(8,128)S(1)}, f32[128,1024]{1,0:T(8,128)S(1)}, u32[]{:S(2)}, u32[]{:S(2)}) collective-permute-start(f32[128,1024]{1,0:T(8,128)S(1)} %slice.32), channel_id=1, source_target_pairs={{0,192},{16,208},{32,224},{48,240},{64,128},{80,144},{96,160},{112... | collective-permute-start | bytes 1572872 | tf_op jit(solution)/shard_map/ppermute | solution.py:379
  41.1 7.2 %collective-permute-start = (f32[512,128]{1,0:T(8,128)S(1)}, f32[512,128]{1,0:T(8,128)S(1)}, u32[]{:S(2)}, u32[]{:S(2)}) collective-permute-start(f32[512,128]{1,0:T(8,128)S(1)} %slice.27), channel_id=1, source_target_pairs={{0,14},{1,15},{2,12},{3,13},{4,10},{5,11},{6,8},{7,9},{16,30},{17,... | collective-permute-start | bytes 786440 | tf_op jit(solution)/shard_map/ppermute | solution.py:370
  42.8 11.7 %collective-permute-start.5 = (f32[128,1024]{1,0:T(8,128)S(1)}, f32[128,1024]{1,0:T(8,128)S(1)}, u32[]{:S(2)}, u32[]{:S(2)}) collective-permute-start(f32[128,1024]{1,0:T(8,128)S(1)} %slice.32), channel_id=1, source_target_pairs={{0,64},{16,80},{32,96},{48,112},{64,0},{80,16},{96,32},{112,48},{1... | collective-permute-start | bytes 1572872 | tf_op jit(solution)/shard_map/ppermute | solution.py:379
  44.8 18.9 %collective-permute-start.6 = (f32[128,1024]{1,0:T(8,128)S(1)}, f32[128,1024]{1,0:T(8,128)S(1)}, u32[]{:S(2)}, u32[]{:S(2)}) collective-permute-start(f32[128,1024]{1,0:T(8,128)S(1)} %slice.32), channel_id=1, source_target_pairs={{0,128},{16,144},{32,160},{48,176},{64,192},{80,208},{96,224},{112... | collective-permute-start | bytes 1572872 | tf_op jit(solution)/shard_map/ppermute | solution.py:379
  81.7 35.9 %collective-permute-start.7 = (f32[256,1024]{1,0:T(8,128)S(1)}, f32[256,1024]{1,0:T(8,128)S(1)}, u32[]{:S(2)}, u32[]{:S(2)}) collective-permute-start(f32[256,1024]{1,0:T(8,128)S(1)} %pad_maximum_fusion.refs_0_), channel_id=1, source_target_pairs={{16,0},{32,16},{48,32},{0,48},{80,64},{96,80},{112,96},{64,112},{1... | collective-permute-start | bytes 3145736 | tf_op jit(solution)/shard_map/ppermute | solution.py:388
  82.6 35.0 %collective-permute-start.8 = (f32[256,1024]{1,0:T(8,128)S(1)}, f32[256,1024]{1,0:T(8,128)S(1)}, u32[]{:S(2)}, u32[]{:S(2)}) collective-permute-start(f32[256,1024]{1,0:T(8,128)S(1)} %pad_maximum_fusion.refs_0_), channel_id=1, source_target_pairs={{32,0},{48,16},{0,32},{16,48},{96,64},{112,80},{64,96},{80,112},{1... | collective-permute-start | bytes 3145736 | tf_op jit(solution)/shard_map/ppermute | solution.py:388
  84.1 47.6 %collective-permute-start.9 = (f32[256,1024]{1,0:T(8,128)S(1)}, f32[256,1024]{1,0:T(8,128)S(1)}, u32[]{:S(2)}, u32[]{:S(2)}) collective-permute-start(f32[256,1024]{1,0:T(8,128)S(1)} %pad_maximum_fusion.refs_0_), channel_id=1, source_target_pairs={{48,0},{0,16},{16,32},{32,48},{112,64},{64,80},{80,96},{96,112},{1... | collective-permute-start | bytes 3145736 | tf_op jit(solution)/shard_map/ppermute | solution.py:388
Sparse Core Ops, SparseCore 0:
  36.6 44.9 all-gather.3
  83.5 37.2 all-gather.5

commit v6 on v4

--- a/solution.py
+++ b/solution.py
@@ -13,6 +13,7 @@
 WIDTH = STEPS * BLOCK
 HALF = WIDTH // 2
 SIDE = 4
+ARRIVING = 2 * SIDE
 NB = 32
 GROUP = 16
 CHUNK = 256
@@ -172,10 +173,10 @@
         u = dot_split_128(split(inverse), split(x_ref[here, after]))
         work_ref[:, :BLOCK] = x_ref[after, after] - dot_split_128(split(jnp.transpose(u)), split(u))
 
-    def step(k, _):
+    def step(k, _, lowest=1):
         others = [functools.partial(finish_row, k - 1, b) for b in range(STEPS)]
         others += [functools.partial(clear, k - 1)]
-        others += [functools.partial(trail, m, n) for n in range(STEPS // 2) for m in range(STEPS)]
+        others += [functools.partial(trail, m, n) for n in range(STEPS // 2) for m in range(lowest, STEPS)]
         factor_block(others)
         prepare(k)
         return 0
@@ -184,7 +185,8 @@
     for copy in later:
         copy.wait()
     prepare(0)
-    lax.fori_loop(1, STEPS, step, 0)
+    lax.fori_loop(1, STEPS // 2, step, 0)
+    lax.fori_loop(STEPS // 2, STEPS, functools.partial(step, lowest=STEPS // 2), 0)
     end = slice(WIDTH - BLOCK, WIDTH)
     x_ref[end, :] = dot_split_128(split(inv_ref[...]), split(x_ref[end, :]))
     x_ref[end, end] = inv_ref[...]
@@ -224,24 +226,41 @@
 
 
 def apply_kernel(place_ref, mh, ml, corner_ref, *refs):
-    v_hbm, outs, (vh, vl, v_ref, sems) = refs[:SIDE], refs[SIDE : SIDE + 3], refs[SIDE + 3 :]
+    v_hbm, outs, (vh, vl, pair_ref, four_ref, sems) = refs[:ARRIVING], refs[ARRIVING : ARRIVING + 3], refs[ARRIVING + 3 :]
     count = iter(range(sems.shape[0]))
     copy = lambda src, dst: pltpu.make_async_copy(src, dst, sems.at[next(count)])
-    arriving = [copy(v, v_ref.at[d]) for d, v in enumerate(v_hbm)]
+    arriving = [copy(v, pair_ref.at[d]) for d, v in enumerate(v_hbm[:SIDE])]
     for c in arriving:
         c.start()
     row, col = place_ref[0], place_ref[1]
+    near = [copy(v, four_ref.at[e]) for e, v in enumerate(v_hbm[SIDE : SIDE + 2])]
+    far = [pltpu.make_async_copy(v, four_ref.at[e], sems.at[SIDE + e]) for e, v in enumerate(v_hbm[SIDE + 2 :])]
+    arriving += near
+
+    @pl.when(row < 2 * SIDE)
+    def _():
+        for c in near:
+            c.start()
+
+    @pl.when(row >= 2 * SIDE)
+    def _():
+        for c in far:
+            c.start()
+
     other = pl.ds(pl.multiple_of(jnp.minimum(col, STEPS - 1) * BLOCK, BLOCK), BLOCK)
     sent = [copy(corner_ref, outs[2])]
     sent[0].start()
     my_y, my_x = row // SIDE, row % SIDE
     swapped = jnp.where((my_y == 1) | (my_y == 2), 1, 0)
-    for d in range(SIDE):
-        arriving[d].wait()
-        for e in range(2):
+    half = BLOCK // 2
+    for n, c in enumerate(arriving):
+        c.wait()
+        for m in range(2 if n < SIDE else SIDE):
+            d, e = (n, m) if n < SIDE else (m, n - SIDE)
+            v_ref = pair_ref.at[d] if n < SIDE else four_ref.at[e]
             block = SIDE * (e + swapped - 2 * e * swapped) + (my_x + d) % SIDE
-            at = pl.ds(pl.multiple_of(block * BLOCK, BLOCK), BLOCK)
-            vh[at], vl[at] = split(v_ref[d, e * BLOCK : (e + 1) * BLOCK])
+            at = pl.ds(pl.multiple_of(block * BLOCK + half * (n >= SIDE), half), half)
+            vh[at], vl[at] = split(v_ref[m * half : (m + 1) * half])
     for k in reversed(range(0, WIDTH, CHUNK)):
         at, upto = slice(k, k + CHUNK), slice(0, k + CHUNK)
         vh[at], vl[at] = split(dot_split((mh[at, upto], ml[at, upto]), (vh[upto], vl[upto])))
@@ -263,13 +282,14 @@
     square = pltpu.VMEM((WIDTH, WIDTH), bf16)
     return pl.pallas_call(
         apply_kernel,
-        in_specs=[pl.BlockSpec(memory_space=pltpu.SMEM), vmem, vmem, vmem] + [hbm] * SIDE,
+        in_specs=[pl.BlockSpec(memory_space=pltpu.SMEM), vmem, vmem, vmem] + [hbm] * ARRIVING,
         out_specs=(hbm,) * 3,
         out_shape=(pltpu.HBM((WIDTH, WIDTH), bf16), pltpu.HBM((WIDTH, WIDTH), bf16), pltpu.HBM((BLOCK, BLOCK), f32)),
         scratch_shapes=[square, square]
         + [
-            pltpu.VMEM((SIDE, 2 * BLOCK, WIDTH), f32),
-            pltpu.SemaphoreType.DMA((SIDE + 1 + 2 * (WIDTH // CHUNK),)),
+            pltpu.VMEM((SIDE, BLOCK, WIDTH), f32),
+            pltpu.VMEM((2, 2 * BLOCK, WIDTH), f32),
+            pltpu.SemaphoreType.DMA((ARRIVING + 1 + 2 * (WIDTH // CHUNK),)),
         ],
         compiler_params=pltpu.CompilerParams(vmem_limit_bytes=20 * 2**20),
         cost_estimate=pl.CostEstimate(flops=10_000_000_000, bytes_accessed=2**23, transcendentals=0),
@@ -324,7 +344,7 @@
     quarter = BLOCK // 4
     corner = blocked[:BLOCK, :BLOCK]
     parts = []
-    for b, a in ((0, 1), (1, 0), (1, 1)):
+    for b, a in ((1, 1), (1, 0), (0, 1)):
         pairs = []
         for i in span:
             to_row = (SIDE - 1 - i // SIDE) * SIDE + i % SIDE if a else i
@@ -340,23 +360,34 @@
     window = window.reshape(cols, SIDE, SIDE, quarter, BLOCK)
     payload = jnp.where(col < STEPS, blocked[:HALF, :BLOCK], lower)
 
-    own = blocked[:BLOCK]
+    upper, under = blocked[: BLOCK // 2], blocked[BLOCK // 2 : BLOCK]
+    source = row < 2 * SIDE
     moves = ([(0, 1), (1, 0)], [(0, 3), (1, 2)], [(0, 2), (1, 3)])
-    got = [
-        lax.ppermute(own, "prow", [(a * SIDE + x, b * SIDE + x) for a, b in move for x in range(SIDE)])
-        for move in moves
-    ]
-    source = row < 2 * SIDE
-    pair = jnp.concatenate([jnp.where(source, own, got[1]), jnp.where(source, got[0], got[2])], 0)
-    payload, window, _ = lax.optimization_barrier((payload, window, pair))
+
+    def along_y(piece):
+        got = []
+        for move in moves:
+            pairs = [(a * SIDE + x, b * SIDE + x) for a, b in move for x in range(SIDE)]
+            got.append(lax.ppermute(piece, "prow", pairs))
+        return [piece] + got
+
+    def along_x(piece, sides):
+        got = [piece]
+        for d in range(1, SIDE):
+            pairs = [(y * SIDE + (x + d) % SIDE, y * SIDE + x) for y in range(sides) for x in range(SIDE)]
+            got.append(lax.ppermute(piece, "prow", pairs))
+        return got
+
+    here, first, second, third = along_y(upper)
+    pair = jnp.concatenate([jnp.where(source, here, second), jnp.where(source, first, third)], 0)
+    four = jnp.concatenate(along_x(under, 2), 0)
+    payload, window, _, _ = lax.optimization_barrier((payload, window, pair, four))
     panels = lax.all_gather(payload, "pcol", axis=0)
-    across = [pair]
-    for d in range(1, SIDE):
-        across.append(lax.ppermute(pair, "prow", [(r // SIDE * SIDE + (r + d) % SIDE, r) for r in range(rows)]))
+    across = along_x(pair, SIDE) + along_y(four)
 
     place = jnp.stack([row, col])
     mh, ml, corner = factor(place, in_hbm(window))
-    applied = apply(place, mh, ml, corner, [in_hbm(v) for v in across])
+    applied = apply(place, mh, ml, corner, across)
     return update(place, *(in_hbm(v) for v in (blocked, panels, *applied)))
 
 

time: 165 us -> 174 us (1.055)
  the two profiles are of different devices: /device:TPU:1 before, /device:TPU:38 now
where the time goes in v6:
time: 174 us; the launch traced here: 173 us
  starting transfers between devices  58 us (33%)
  Pallas kernels  56.2 us (32%)
  waiting for transfers between devices  24.6 us (14%)
  blocking collectives  13.9 us (8%)
  between operations  13.7 us (8%)
  other arithmetic  3.79 us (2%)
  local copies, waits for them, and re-layouts  2.72 us (2%)
    pallas_call x1, Pallas kernels, factor(): pl.pallas_call(factor_kernel, in_specs=[pl.BlockSpec(memory_space=pltpu.S...  33.5 us
    ppermute x6, starting transfers between devices, along_y(): got.append(lax.ppermute(piece, 'prow', pairs))  25.8 us
    ppermute x6, starting transfers between devices, along_x(): got.append(lax.ppermute(piece, 'prow', pairs))  15.6 us
    all_to_all x1, blocking collectives, per_device(): lax.all_to_all(jnp.broadcast_to(part, (rows, quarter, BLOCK)), 'prow', 0, 0)  13.9 us
    all_gather x1, waiting for transfers between devices, per_device(): window = lax.all_gather(strip.reshape(HALF, BLOCK), 'pcol', axis=0)  13.5 us
    ppermute x3, starting transfers between devices, per_device(): parts.append(lax.ppermute(corner[at:at + quarter], ('prow', 'pcol'), pairs))  12.8 us
    pallas_call x1, Pallas kernels, apply(): pl.pallas_call(apply_kernel, in_specs=[pl.BlockSpec(memory_space=pltpu.SM...  11.4 us
    pallas_call x1, Pallas kernels, update(): pl.pallas_call(update_kernel, grid=(WIDTH // CHUNK,), in_specs=[pl.BlockS...  11.3 us
  transfers between devices with their start and end apart: 18, of which 6 were waited for; matrix products, arithmetic and copies ran while one was open for 3% of the time, Pallas kernels for 26%

profile of v6, /device:TPU:38, one launch (start us, length us, event | category | flops | bytes accessed | tf_op | source)
XLA Modules:
  0.0 173.0 jit_solution(14520764403401316292)
XLA Ops:
  6.5 0.8 fusion.1
  7.3 10.2 %collective-permute-start.1 = (f32[32,128]{1,0:T(8,128)S(1)}, f32[32,128]{1,0:T(8,128)S(1)}, u32[]{:S(2)}, u32[]{:S(2)}) collective-permute-start(f32[32,128]{1,0:T(8,128)S(1)} %get-tuple-element.25), channel_id=1, source_target_pairs={{0,206},{1,207},{2,204},{3,205},{4,202},{5,203},{6,200},{7,201},{1... | collective-permute-start | bytes 49160 | tf_op jit(solution)/shard_map/ppermute | solution.py:354
  17.5 1.3 collective-permute-start.2
  18.8 1.3 collective-permute-start.3
  20.2 1.3 collective-permute-done.3
  21.5 0.7 add_select_fusion
  22.3 13.9 %all_to_all.5 = f32[16,32,128]{2,1,0:T(8,128)} all-to-all(f32[16,32,128]{2,1,0:T(8,128)S(1)} %broadcast_in_dim.3), channel_id=1, replica_groups=mesh['prow'=16,'pcol'=16] {'prow'}, dimensions={0} | all-to-all | bytes 524288 | tf_op jit(solution)/shard_map/all_to_all | solution.py:358
  36.3 1.0 slice.35
  37.3 3.0 %collective-permute-start.4 = (f32[64,1024]{1,0:T(8,128)S(1)}, f32[64,1024]{1,0:T(8,128)S(1)}, u32[]{:S(2)}, u32[]{:S(2)}) collective-permute-start(f32[64,1024]{1,0:T(8,128)S(1)} %slice.35), channel_id=1, source_target_pairs={{0,192},{16,208},{32,224},{48,240},{64,128},{80,144},{96,160},{112... | collective-permute-start | bytes 786440 | tf_op jit(solution)/shard_map/ppermute | solution.py:371
  40.3 2.1 %collective-permute-start.5 = (f32[64,1024]{1,0:T(8,128)S(1)}, f32[64,1024]{1,0:T(8,128)S(1)}, u32[]{:S(2)}, u32[]{:S(2)}) collective-permute-start(f32[64,1024]{1,0:T(8,128)S(1)} %slice.35), channel_id=1, source_target_pairs={{0,64},{16,80},{32,96},{48,112},{64,0},{80,16},{96,32},{112,48},{1... | collective-permute-start | bytes 786440 | tf_op jit(solution)/shard_map/ppermute | solution.py:371
  42.4 1.3 collective-permute-start.6
  43.7 1.0 slice.30
  44.7 3.8 %collective-permute-start = (f32[512,128]{1,0:T(8,128)S(1)}, f32[512,128]{1,0:T(8,128)S(1)}, u32[]{:S(2)}, u32[]{:S(2)}) collective-permute-start(f32[512,128]{1,0:T(8,128)S(1)} %slice.30), channel_id=1, source_target_pairs={{0,14},{1,15},{2,12},{3,13},{4,10},{5,11},{6,8},{7,9},{16,30},{17,... | collective-permute-start | bytes 786440 | tf_op jit(solution)/shard_map/ppermute | solution.py:357
  48.5 1.1 fusion
  49.7 2.6 %collective-permute-start.7 = (f32[64,1024]{1,0:T(8,128)S(1)}, f32[64,1024]{1,0:T(8,128)S(1)}, u32[]{:S(2)}, u32[]{:S(2)}) collective-permute-start(f32[64,1024]{1,0:T(8,128)S(1)} %get-tuple-element.21), channel_id=1, source_target_pairs={{16,0},{32,16},{48,32},{0,48},{80,64},{96,80},{112,96},{64,112},{1... | collective-permute-start | bytes 786440 | tf_op jit(solution)/shard_map/ppermute | solution.py:378
  52.3 4.7 %collective-permute-start.8 = (f32[64,1024]{1,0:T(8,128)S(1)}, f32[64,1024]{1,0:T(8,128)S(1)}, u32[]{:S(2)}, u32[]{:S(2)}) collective-permute-start(f32[64,1024]{1,0:T(8,128)S(1)} %get-tuple-element.21), channel_id=1, source_target_pairs={{32,0},{48,16},{0,32},{16,48},{96,64},{112,80},{64,96},{80,112},{3... | collective-permute-start | bytes 786440 | tf_op jit(solution)/shard_map/ppermute | solution.py:378
  57.0 3.0 %collective-permute-start.9 = (f32[64,1024]{1,0:T(8,128)S(1)}, f32[64,1024]{1,0:T(8,128)S(1)}, u32[]{:S(2)}, u32[]{:S(2)}) collective-permute-start(f32[64,1024]{1,0:T(8,128)S(1)} %get-tuple-element.21), channel_id=1, source_target_pairs={{48,0},{0,16},{16,32},{32,48},{112,64},{64,80},{80,96},{96,112},{4... | collective-permute-start | bytes 786440 | tf_op jit(solution)/shard_map/ppermute | solution.py:378
  60.2 1.7 slice_select_fusion
  61.9 1.7 %collective-permute-done.8 = f32[64,1024]{1,0:T(8,128)S(1)} collective-permute-done((f32[64,1024]{1,0:T(8,128)S(1)}, f32[64,1024]{1,0:T(8,128)S(1)}, u32[]{:S(2)}, u32[]{:S(2)}) %collective-permute-start.8) | collective-permute-done | bytes 262176 | tf_op jit(solution)/shard_map/ppermute | solution.py:378
  63.6 2.5 %collective-permute-done.9 = f32[64,1024]{1,0:T(8,128)S(1)} collective-permute-done((f32[64,1024]{1,0:T(8,128)S(1)}, f32[64,1024]{1,0:T(8,128)S(1)}, u32[]{:S(2)}, u32[]{:S(2)}) %collective-permute-start.9) | collective-permute-done | bytes 262176 | tf_op jit(solution)/shard_map/ppermute | solution.py:378
  66.1 0.1 pad_maximum_fusion.refs_4_
  66.2 13.5 %all-gather.4.cloned.1.call-done = f32[16,512,128]{2,1,0:T(8,128)} async-done(((f32[1,512,128]{2,1,0:T(8,128)}), f32[16,512,128]{2,1,0:T(8,128)}) %all-gather.4.cloned.1.call-update) | async-done | bytes 4194320 | tf_op jit(solution)/shard_map/all_gather | solution.py:359
  79.8 1.3 collective-permute-start.10
  81.2 2.4 %collective-permute-start.11 = (f32[128,1024]{1,0:T(8,128)S(1)}, f32[128,1024]{1,0:T(8,128)S(1)}, u32[]{:S(2)}, u32[]{:S(2)}) collective-permute-start(f32[128,1024]{1,0:T(8,128)S(1)} %pad_maximum_fusion.1.refs_0_), channel_id=1, source_target_pairs={{32,0},{48,16},{0,32},{16,48},{96,64},{112,80},{64,96},{80,112},{1... | collective-permute-start | bytes 1572872 | tf_op jit(solution)/shard_map/ppermute | solution.py:378
  83.6 1.4 collective-permute-start.12
  85.1 3.7 %collective-permute-start.13 = (f32[256,1024]{1,0:T(8,128)S(1)}, f32[256,1024]{1,0:T(8,128)S(1)}, u32[]{:S(2)}, u32[]{:S(2)}) collective-permute-start(f32[256,1024]{1,0:T(8,128)S(1)} %pad_maximum_fusion.refs_4_), channel_id=1, source_target_pairs={{0,64},{16,80},{32,96},{48,112},{64,0},{80,16},{96,32},{112,48},{1... | collective-permute-start | bytes 3145736 | tf_op jit(solution)/shard_map/ppermute | solution.py:371
  88.7 1.4 collective-permute-start.14
  90.1 5.3 %collective-permute-done.10.refs_1_ = f32[128,1024]{1,0:T(8,128)S(1)} collective-permute-done((f32[128,1024]{1,0:T(8,128)S(1)}, f32[128,1024]{1,0:T(8,128)S(1)}, u32[]{:S(2)}, u32[]{:S(2)}) %collective-permute-start.10) | collective-permute-done | bytes 524320 | tf_op jit(solution)/shard_map/ppermute | solution.py:378
  95.4 14.4 %collective-permute-start.15 = (f32[256,1024]{1,0:T(8,128)S(1)}, f32[256,1024]{1,0:T(8,128)S(1)}, u32[]{:S(2)}, u32[]{:S(2)}) collective-permute-start(f32[256,1024]{1,0:T(8,128)S(1)} %pad_maximum_fusion.refs_4_), channel_id=1, source_target_pairs={{0,128},{16,144},{32,160},{48,176},{64,192},{80,208},{96,224},{112... | collective-permute-start | bytes 3145736 | tf_op jit(solution)/shard_map/ppermute | solution.py:371
  109.8 33.5 %factor.1 = (bf16[1024,1024]{1,0:T(8,128)(2,1)S(1)}, bf16[1024,1024]{1,0:T(8,128)(2,1)S(1)}, f32[128,128]{1,0:T(8,128)S(1)}) custom-call(s32[2]{0:T(128)S(1)} %pad_add_fusion.place_ref, f32[16,4,4,32,128]{4,3,2,1,0:T(8,128)} %bitcast.7), custom_call_target="tpu_custom_call" | custom-call | flops 40000000000 | bytes 8388608 | tf_op jit(solution)/shard_map/factor/pallas_call | solution.py:203
  143.3 11.4 %apply.1 = (bf16[1024,1024]{1,0:T(8,128)(2,1)}, bf16[1024,1024]{1,0:T(8,128)(2,1)}, f32[128,128]{1,0:T(8,128)}) custom-call(s32[2]{0:T(128)S(1)} %pad_add_fusion.place_ref, bf16[1024,1024]{1,0:T(8,128)(2,1)S(1)} %get-tuple-element.15.mh, bf16[1024,1024]{1,0:T(8,128)(2,1)S(1)} %get-tuple-element.16.ml, f32[128,128]{1,0:T(8,128)S(1)} %get-tuple-element.17.corner_ref, ...), custom_call_target="tpu_custom_call" | custom-call | flops 10000000000 | bytes 8388608 | tf_op jit(solution)/shard_map/apply/pallas_call | solution.py:283
  154.8 11.3 %update.1 = f32[1024,1024]{1,0:T(8,128)} custom-call(s32[2]{0:T(128)S(1)} %pad_add_fusion.place_ref, f32[1024,1024]{1,0:T(8,128)} %a_ref.1, f32[16,512,128]{2,1,0:T(8,128)} %bitcast.5, bf16[1024,1024]{1,0:T(8,128)(2,1)} %get-tuple-element.18.yh_ref, bf16[1024,1024]{1,0:T(8,128)(2,1)} %get-tuple-element.19.yl_ref, f32[128,128]{1,0:T(8,128)} %get-tuple-element.20.corner_ref), custom_call_target="tpu_custom_call" | custom-call | tf_op jit(solution)/shard_map/update/pallas_call | solution.py:320
  (21 shorter events, 0.4 us)
Async XLA Ops:
  6.5 73.2 %all-gather.4.cloned.1.call-start = ((), (), s32[]{:S(2)}) async-start(), calls=%async_computation.1 | async-start | bytes 4456448 | tf_op jit(solution)/shard_map/all_gather | solution.py:359
  7.3 12.8 %collective-permute-start.1 = (f32[32,128]{1,0:T(8,128)S(1)}, f32[32,128]{1,0:T(8,128)S(1)}, u32[]{:S(2)}, u32[]{:S(2)}) collective-permute-start(f32[32,128]{1,0:T(8,128)S(1)} %get-tuple-element.25), channel_id=1, source_target_pairs={{0,206},{1,207},{2,204},{3,205},{4,202},{5,203},{6,200},{7,201},{1... | collective-permute-start | bytes 49160 | tf_op jit(solution)/shard_map/ppermute | solution.py:354
  17.5 2.7 %collective-permute-start.2 = (f32[32,128]{1,0:T(8,128)S(1)}, f32[32,128]{1,0:T(8,128)S(1)}, u32[]{:S(2)}, u32[]{:S(2)}) collective-permute-start(f32[32,128]{1,0:T(8,128)S(1)} %get-tuple-element.23), channel_id=1, source_target_pairs={{0,14},{1,15},{2,12},{3,13},{4,10},{5,11},{6,8},{7,9},{16,30},{17,... | collective-permute-start | bytes 49160 | tf_op jit(solution)/shard_map/ppermute | solution.py:354
  18.8 2.7 %collective-permute-start.3 = (f32[32,128]{1,0:T(8,128)S(1)}, f32[32,128]{1,0:T(8,128)S(1)}, u32[]{:S(2)}, u32[]{:S(2)}) collective-permute-start(f32[32,128]{1,0:T(8,128)S(1)} %get-tuple-element.24), channel_id=1, source_target_pairs={{0,192},{1,193},{2,194},{3,195},{4,196},{5,197},{6,198},{7,199},{1... | collective-permute-start | bytes 49160 | tf_op jit(solution)/shard_map/ppermute | solution.py:354
  36.2 118.5 %all-gather.6.cloned.1.call-start = ((), (), s32[]{:S(2)}) async-start(), calls=%async_computation.2 | async-start | bytes 4456448 | tf_op jit(solution)/shard_map/all_gather | solution.py:385
  37.3 11.3 %collective-permute-start.4 = (f32[64,1024]{1,0:T(8,128)S(1)}, f32[64,1024]{1,0:T(8,128)S(1)}, u32[]{:S(2)}, u32[]{:S(2)}) collective-permute-start(f32[64,1024]{1,0:T(8,128)S(1)} %slice.35), channel_id=1, source_target_pairs={{0,192},{16,208},{32,224},{48,240},{64,128},{80,144},{96,160},{112... | collective-permute-start | bytes 786440 | tf_op jit(solution)/shard_map/ppermute | solution.py:371
  40.3 16.7 %collective-permute-start.5 = (f32[64,1024]{1,0:T(8,128)S(1)}, f32[64,1024]{1,0:T(8,128)S(1)}, u32[]{:S(2)}, u32[]{:S(2)}) collective-permute-start(f32[64,1024]{1,0:T(8,128)S(1)} %slice.35), channel_id=1, source_target_pairs={{0,64},{16,80},{32,96},{48,112},{64,0},{80,16},{96,32},{112,48},{1... | collective-permute-start | bytes 786440 | tf_op jit(solution)/shard_map/ppermute | solution.py:371
  42.4 17.7 %collective-permute-start.6 = (f32[64,1024]{1,0:T(8,128)S(1)}, f32[64,1024]{1,0:T(8,128)S(1)}, u32[]{:S(2)}, u32[]{:S(2)}) collective-permute-start(f32[64,1024]{1,0:T(8,128)S(1)} %slice.35), channel_id=1, source_target_pairs={{0,128},{16,144},{32,160},{48,176},{64,192},{80,208},{96,224},{112... | collective-permute-start | bytes 786440 | tf_op jit(solution)/shard_map/ppermute | solution.py:371
  44.7 15.5 %collective-permute-start = (f32[512,128]{1,0:T(8,128)S(1)}, f32[512,128]{1,0:T(8,128)S(1)}, u32[]{:S(2)}, u32[]{:S(2)}) collective-permute-start(f32[512,128]{1,0:T(8,128)S(1)} %slice.30), channel_id=1, source_target_pairs={{0,14},{1,15},{2,12},{3,13},{4,10},{5,11},{6,8},{7,9},{16,30},{17,... | collective-permute-start | bytes 786440 | tf_op jit(solution)/shard_map/ppermute | solution.py:357
  49.7 12.2 %collective-permute-start.7 = (f32[64,1024]{1,0:T(8,128)S(1)}, f32[64,1024]{1,0:T(8,128)S(1)}, u32[]{:S(2)}, u32[]{:S(2)}) collective-permute-start(f32[64,1024]{1,0:T(8,128)S(1)} %get-tuple-element.21), channel_id=1, source_target_pairs={{16,0},{32,16},{48,32},{0,48},{80,64},{96,80},{112,96},{64,112},{1... | collective-permute-start | bytes 786440 | tf_op jit(solution)/shard_map/ppermute | solution.py:378
  52.3 11.3 %collective-permute-start.8 = (f32[64,1024]{1,0:T(8,128)S(1)}, f32[64,1024]{1,0:T(8,128)S(1)}, u32[]{:S(2)}, u32[]{:S(2)}) collective-permute-start(f32[64,1024]{1,0:T(8,128)S(1)} %get-tuple-element.21), channel_id=1, source_target_pairs={{32,0},{48,16},{0,32},{16,48},{96,64},{112,80},{64,96},{80,112},{3... | collective-permute-start | bytes 786440 | tf_op jit(solution)/shard_map/ppermute | solution.py:378
  57.0 9.1 %collective-permute-start.9 = (f32[64,1024]{1,0:T(8,128)S(1)}, f32[64,1024]{1,0:T(8,128)S(1)}, u32[]{:S(2)}, u32[]{:S(2)}) collective-permute-start(f32[64,1024]{1,0:T(8,128)S(1)} %get-tuple-element.21), channel_id=1, source_target_pairs={{48,0},{0,16},{16,32},{32,48},{112,64},{64,80},{80,96},{96,112},{4... | collective-permute-start | bytes 786440 | tf_op jit(solution)/shard_map/ppermute | solution.py:378
  79.8 15.6 %collective-permute-start.10 = (f32[128,1024]{1,0:T(8,128)S(1)}, f32[128,1024]{1,0:T(8,128)S(1)}, u32[]{:S(2)}, u32[]{:S(2)}) collective-permute-start(f32[128,1024]{1,0:T(8,128)S(1)} %pad_maximum_fusion.1.refs_0_), channel_id=1, source_target_pairs={{16,0},{32,16},{48,32},{0,48},{80,64},{96,80},{112,96},{64,112},{1... | collective-permute-start | bytes 1572872 | tf_op jit(solution)/shard_map/ppermute | solution.py:378
  81.2 62.1 %collective-permute-start.11 = (f32[128,1024]{1,0:T(8,128)S(1)}, f32[128,1024]{1,0:T(8,128)S(1)}, u32[]{:S(2)}, u32[]{:S(2)}) collective-permute-start(f32[128,1024]{1,0:T(8,128)S(1)} %pad_maximum_fusion.1.refs_0_), channel_id=1, source_target_pairs={{32,0},{48,16},{0,32},{16,48},{96,64},{112,80},{64,96},{80,112},{1... | collective-permute-start | bytes 1572872 | tf_op jit(solution)/shard_map/ppermute | solution.py:378
  83.6 59.7 %collective-permute-start.12 = (f32[128,1024]{1,0:T(8,128)S(1)}, f32[128,1024]{1,0:T(8,128)S(1)}, u32[]{:S(2)}, u32[]{:S(2)}) collective-permute-start(f32[128,1024]{1,0:T(8,128)S(1)} %pad_maximum_fusion.1.refs_0_), channel_id=1, source_target_pairs={{48,0},{0,16},{16,32},{32,48},{112,64},{64,80},{80,96},{96,112},{1... | collective-permute-start | bytes 1572872 | tf_op jit(solution)/shard_map/ppermute | solution.py:378
  85.1 58.3 %collective-permute-start.13 = (f32[256,1024]{1,0:T(8,128)S(1)}, f32[256,1024]{1,0:T(8,128)S(1)}, u32[]{:S(2)}, u32[]{:S(2)}) collective-permute-start(f32[256,1024]{1,0:T(8,128)S(1)} %pad_maximum_fusion.refs_4_), channel_id=1, source_target_pairs={{0,64},{16,80},{32,96},{48,112},{64,0},{80,16},{96,32},{112,48},{1... | collective-permute-start | bytes 3145736 | tf_op jit(solution)/shard_map/ppermute | solution.py:371
  88.7 54.6 %collective-permute-start.14 = (f32[256,1024]{1,0:T(8,128)S(1)}, f32[256,1024]{1,0:T(8,128)S(1)}, u32[]{:S(2)}, u32[]{:S(2)}) collective-permute-start(f32[256,1024]{1,0:T(8,128)S(1)} %pad_maximum_fusion.refs_4_), channel_id=1, source_target_pairs={{0,192},{16,208},{32,224},{48,240},{64,128},{80,144},{96,160},{112... | collective-permute-start | bytes 3145736 | tf_op jit(solution)/shard_map/ppermute | solution.py:371
  95.4 47.9 %collective-permute-start.15 = (f32[256,1024]{1,0:T(8,128)S(1)}, f32[256,1024]{1,0:T(8,128)S(1)}, u32[]{:S(2)}, u32[]{:S(2)}) collective-permute-start(f32[256,1024]{1,0:T(8,128)S(1)} %pad_maximum_fusion.refs_4_), channel_id=1, source_target_pairs={{0,128},{16,144},{32,160},{48,176},{64,192},{80,208},{96,224},{112... | collective-permute-start | bytes 3145736 | tf_op jit(solution)/shard_map/ppermute | solution.py:371
Sparse Core Ops, SparseCore 0:
  36.4 43.3 all-gather.3
  81.6 40.8 all-gather.5

commit v7 on v4

--- a/solution.py
+++ b/solution.py
@@ -172,10 +172,10 @@
         u = dot_split_128(split(inverse), split(x_ref[here, after]))
         work_ref[:, :BLOCK] = x_ref[after, after] - dot_split_128(split(jnp.transpose(u)), split(u))
 
-    def step(k, _):
+    def step(k, _, lowest=1):
         others = [functools.partial(finish_row, k - 1, b) for b in range(STEPS)]
         others += [functools.partial(clear, k - 1)]
-        others += [functools.partial(trail, m, n) for n in range(STEPS // 2) for m in range(STEPS)]
+        others += [functools.partial(trail, m, n) for n in range(STEPS // 2) for m in range(lowest, STEPS)]
         factor_block(others)
         prepare(k)
         return 0
@@ -184,7 +184,8 @@
     for copy in later:
         copy.wait()
     prepare(0)
-    lax.fori_loop(1, STEPS, step, 0)
+    lax.fori_loop(1, STEPS // 2, step, 0)
+    lax.fori_loop(STEPS // 2, STEPS, functools.partial(step, lowest=STEPS // 2), 0)
     end = slice(WIDTH - BLOCK, WIDTH)
     x_ref[end, :] = dot_split_128(split(inv_ref[...]), split(x_ref[end, :]))
     x_ref[end, end] = inv_ref[...]
@@ -324,7 +325,7 @@
     quarter = BLOCK // 4
     corner = blocked[:BLOCK, :BLOCK]
     parts = []
-    for b, a in ((0, 1), (1, 0), (1, 1)):
+    for b, a in ((1, 1), (1, 0), (0, 1)):
         pairs = []
         for i in span:
             to_row = (SIDE - 1 - i // SIDE) * SIDE + i % SIDE if a else i
@@ -356,7 +357,7 @@
 
     place = jnp.stack([row, col])
     mh, ml, corner = factor(place, in_hbm(window))
-    applied = apply(place, mh, ml, corner, [in_hbm(v) for v in across])
+    applied = apply(place, mh, ml, corner, across)
     return update(place, *(in_hbm(v) for v in (blocked, panels, *applied)))
 
 

time: 165 us -> 162 us (0.982)
  starting transfers between devices: 27.1 us -> 23.2 us
  Pallas kernels: 58.8 us -> 56.2 us
  blocking collectives: 11.7 us -> 14.2 us
  waiting for transfers between devices: 45.7 us -> 47.5 us
    ppermute x1, starting transfers between devices: 6.85 us -> 1.72 us  [per_device(): lax.ppermute(blocked[HALF:, :BLOCK], 'pcol', [(k, other_half(k)) for k in...]
    all_to_all x1, blocking collectives: 11.7 us -> 14.2 us  [per_device(): lax.all_to_all(jnp.broadcast_to(part, (rows, quarter, BLOCK)), 'prow', 0, 0)]
    ppermute x3, waiting for transfers between devices: 12.4 us -> 14.1 us  [per_device(): lax.ppermute(pair, 'prow', [(r // SIDE * SIDE + (r + d) % SIDE, r) for r...]
  transfers between devices with their start and end apart: 12 -> 12, of which waited for: 6 -> 6; matrix products, arithmetic and copies ran while one was open for 3% -> 3% of each run, Pallas kernels for 29% -> 28%
where the time goes in v7:
time: 162 us; the launch traced here: 161 us
  Pallas kernels  56.2 us (35%)
  waiting for transfers between devices  47.5 us (29%)
  starting transfers between devices  23.2 us (14%)
  blocking collectives  14.2 us (9%)
  between operations  13.6 us (8%)
  other arithmetic  3.75 us (2%)
  local copies, waits for them, and re-layouts  2.83 us (2%)
    pallas_call x1, Pallas kernels, factor(): pl.pallas_call(factor_kernel, in_specs=[pl.BlockSpec(memory_space=pltpu.S...  33.5 us
    all_gather x1, waiting for transfers between devices, per_device(): window = lax.all_gather(strip.reshape(HALF, BLOCK), 'pcol', axis=0)  17.7 us
    all_to_all x1, blocking collectives, per_device(): lax.all_to_all(jnp.broadcast_to(part, (rows, quarter, BLOCK)), 'prow', 0, 0)  14.2 us
    ppermute x3, waiting for transfers between devices, per_device(): lax.ppermute(pair, 'prow', [(r // SIDE * SIDE + (r + d) % SIDE, r) for r...  14.1 us
    ppermute x3, starting transfers between devices, per_device(): parts.append(lax.ppermute(corner[at:at + quarter], ('prow', 'pcol'), pairs))  13.3 us
    ppermute x3, waiting for transfers between devices, per_device(): lax.ppermute(own, 'prow', [(a * SIDE + x, b * SIDE + x) for a, b in move...  12.6 us
    pallas_call x1, Pallas kernels, apply(): pl.pallas_call(apply_kernel, in_specs=[pl.BlockSpec(memory_space=pltpu.SM...  11.4 us
    pallas_call x1, Pallas kernels, update(): pl.pallas_call(update_kernel, grid=(WIDTH // CHUNK,), in_specs=[pl.BlockS...  11.3 us
  transfers between devices with their start and end apart: 12, of which 6 were waited for; matrix products, arithmetic and copies ran while one was open for 3% of the time, Pallas kernels for 28%

profile of v7, /device:TPU:1, one launch (start us, length us, event | category | flops | bytes accessed | tf_op | source)
XLA Modules:
  0.0 161.3 jit_solution(10818032693058129638)
XLA Ops:
  6.5 0.8 fusion
  7.3 10.7 %collective-permute-start.1 = (f32[32,128]{1,0:T(8,128)S(1)}, f32[32,128]{1,0:T(8,128)S(1)}, u32[]{:S(2)}, u32[]{:S(2)}) collective-permute-start(f32[32,128]{1,0:T(8,128)S(1)} %get-tuple-element.23), channel_id=1, source_target_pairs={{0,206},{1,207},{2,204},{3,205},{4,202},{5,203},{6,200},{7,201},{1... | collective-permute-start | bytes 49160 | tf_op jit(solution)/shard_map/ppermute | solution.py:335
  18.0 1.3 collective-permute-start.2
  19.3 1.3 collective-permute-start.3
  20.7 0.8 collective-permute-done.3
  21.5 0.7 add_select_fusion
  22.2 14.2 %all_to_all.5 = f32[16,32,128]{2,1,0:T(8,128)} all-to-all(f32[16,32,128]{2,1,0:T(8,128)S(1)} %broadcast_in_dim.3), channel_id=1, replica_groups=mesh['prow'=16,'pcol'=16] {'prow'}, dimensions={0} | all-to-all | bytes 524288 | tf_op jit(solution)/shard_map/all_to_all | solution.py:339
  36.5 0.0 all-gather.4.cloned.1.call-update
  36.5 0.0 all-gather.6.cloned.1.call-start
  36.5 1.1 slice.32
  37.6 2.5 %collective-permute-start.4 = (f32[128,1024]{1,0:T(8,128)S(1)}, f32[128,1024]{1,0:T(8,128)S(1)}, u32[]{:S(2)}, u32[]{:S(2)}) collective-permute-start(f32[128,1024]{1,0:T(8,128)S(1)} %slice.32), channel_id=1, source_target_pairs={{0,192},{16,208},{32,224},{48,240},{64,128},{80,144},{96,160},{112... | collective-permute-start | bytes 1572872 | tf_op jit(solution)/shard_map/ppermute | solution.py:347
  40.1 1.0 slice.27
  41.1 1.7 %collective-permute-start = (f32[512,128]{1,0:T(8,128)S(1)}, f32[512,128]{1,0:T(8,128)S(1)}, u32[]{:S(2)}, u32[]{:S(2)}) collective-permute-start(f32[512,128]{1,0:T(8,128)S(1)} %slice.27), channel_id=1, source_target_pairs={{0,14},{1,15},{2,12},{3,13},{4,10},{5,11},{6,8},{7,9},{16,30},{17,... | collective-permute-start | bytes 786440 | tf_op jit(solution)/shard_map/ppermute | solution.py:338
  42.8 1.9 %collective-permute-start.5 = (f32[128,1024]{1,0:T(8,128)S(1)}, f32[128,1024]{1,0:T(8,128)S(1)}, u32[]{:S(2)}, u32[]{:S(2)}) collective-permute-start(f32[128,1024]{1,0:T(8,128)S(1)} %slice.32), channel_id=1, source_target_pairs={{0,64},{16,80},{32,96},{48,112},{64,0},{80,16},{96,32},{112,48},{1... | collective-permute-start | bytes 1572872 | tf_op jit(solution)/shard_map/ppermute | solution.py:347
  44.8 1.3 collective-permute-start.6
  46.1 2.2 %collective-permute-done = f32[512,128]{1,0:T(8,128)S(1)} collective-permute-done((f32[512,128]{1,0:T(8,128)S(1)}, f32[512,128]{1,0:T(8,128)S(1)}, u32[]{:S(2)}, u32[]{:S(2)}) %collective-permute-start) | collective-permute-done | bytes 262176 | tf_op jit(solution)/shard_map/ppermute | solution.py:338
  48.3 1.7 %slice_select_fusion = f32[512,128]{1,0:T(8,128)} fusion(f32[512,128]{1,0:T(8,128)S(1)} %collective-permute-done, f32[1024,1024]{1,0:T(8,128)} %a_ref.1, pred[]{:T(512)S(6)} %lt.8), kind=kLoop, calls=%fused_computation.1 | loop fusion | flops 65536 | bytes 786433 | tf_op jit(solution)/shard_map/jit(_where)/select_n | solution.py:342
  50.0 1.1 broadcast_select_fusion.1
  51.1 3.4 %collective-permute-done.5 = f32[128,1024]{1,0:T(8,128)S(1)} collective-permute-done((f32[128,1024]{1,0:T(8,128)S(1)}, f32[128,1024]{1,0:T(8,128)S(1)}, u32[]{:S(2)}, u32[]{:S(2)}) %collective-permute-start.5) | collective-permute-done | bytes 524320 | tf_op jit(solution)/shard_map/ppermute | solution.py:347
  54.5 9.2 %collective-permute-done.6 = f32[128,1024]{1,0:T(8,128)S(1)} collective-permute-done((f32[128,1024]{1,0:T(8,128)S(1)}, f32[128,1024]{1,0:T(8,128)S(1)}, u32[]{:S(2)}, u32[]{:S(2)}) %collective-permute-start.6) | collective-permute-done | bytes 524320 | tf_op jit(solution)/shard_map/ppermute | solution.py:347
  63.7 0.1 broadcast_select_fusion
  63.8 0.1 pad_maximum_fusion.refs_0_
  63.9 17.7 %all-gather.4.cloned.1.call-done = f32[16,512,128]{2,1,0:T(8,128)} async-done(((f32[1,512,128]{2,1,0:T(8,128)}), f32[16,512,128]{2,1,0:T(8,128)}) %all-gather.4.cloned.1.call-update) | async-done | bytes 4194320 | tf_op jit(solution)/shard_map/all_gather | solution.py:340
  81.6 0.0 all-gather.6.cloned.1.call-update
  81.7 0.1 pad_add_fusion.place_ref
  81.7 0.9 collective-permute-start.7
  82.6 1.5 collective-permute-start.8
  84.1 33.5 %factor.1 = (bf16[1024,1024]{1,0:T(8,128)(2,1)S(1)}, bf16[1024,1024]{1,0:T(8,128)(2,1)S(1)}, f32[128,128]{1,0:T(8,128)S(1)}) custom-call(s32[2]{0:T(128)S(1)} %pad_add_fusion.place_ref, f32[16,4,4,32,128]{4,3,2,1,0:T(8,128)} %bitcast.7), custom_call_target="tpu_custom_call" | custom-call | flops 40000000000 | bytes 8388608 | tf_op jit(solution)/shard_map/factor/pallas_call | solution.py:202
  117.6 14.1 %collective-permute-done.9.refs_3_ = f32[256,1024]{1,0:T(8,128)S(1)} collective-permute-done((f32[256,1024]{1,0:T(8,128)S(1)}, f32[256,1024]{1,0:T(8,128)S(1)}, u32[]{:S(2)}, u32[]{:S(2)}) %collective-permute-start.9) | collective-permute-done | bytes 1048608 | tf_op jit(solution)/shard_map/ppermute | solution.py:356
  131.7 11.4 %apply.1 = (bf16[1024,1024]{1,0:T(8,128)(2,1)}, bf16[1024,1024]{1,0:T(8,128)(2,1)}, f32[128,128]{1,0:T(8,128)}) custom-call(s32[2]{0:T(128)S(1)} %pad_add_fusion.place_ref, bf16[1024,1024]{1,0:T(8,128)(2,1)S(1)} %get-tuple-element.15.mh, bf16[1024,1024]{1,0:T(8,128)(2,1)S(1)} %get-tuple-element.16.ml, f32[128,128]{1,0:T(8,128)S(1)} %get-tuple-element.17.corner_ref, ...), custom_call_target="tpu_custom_call" | custom-call | flops 10000000000 | bytes 8388608 | tf_op jit(solution)/shard_map/apply/pallas_call | solution.py:265
  143.1 0.0 all-gather.6.cloned.1.call-done
  143.1 11.3 %update.1 = f32[1024,1024]{1,0:T(8,128)} custom-call(s32[2]{0:T(128)S(1)} %pad_add_fusion.place_ref, f32[1024,1024]{1,0:T(8,128)} %a_ref.1, f32[16,512,128]{2,1,0:T(8,128)} %bitcast.5, bf16[1024,1024]{1,0:T(8,128)(2,1)} %get-tuple-element.18.yh_ref, bf16[1024,1024]{1,0:T(8,128)(2,1)} %get-tuple-element.19.yl_ref, f32[128,128]{1,0:T(8,128)} %get-tuple-element.20.corner_ref), custom_call_target="tpu_custom_call" | custom-call | tf_op jit(solution)/shard_map/update/pallas_call | solution.py:301
  (8 shorter events, 0.0 us)
Async XLA Ops:
  6.5 75.1 %all-gather.4.cloned.1.call-start = ((), (), s32[]{:S(2)}) async-start(), calls=%async_computation.1 | async-start | bytes 4456448 | tf_op jit(solution)/shard_map/all_gather | solution.py:340
  7.3 13.4 %collective-permute-start.1 = (f32[32,128]{1,0:T(8,128)S(1)}, f32[32,128]{1,0:T(8,128)S(1)}, u32[]{:S(2)}, u32[]{:S(2)}) collective-permute-start(f32[32,128]{1,0:T(8,128)S(1)} %get-tuple-element.23), channel_id=1, source_target_pairs={{0,206},{1,207},{2,204},{3,205},{4,202},{5,203},{6,200},{7,201},{1... | collective-permute-start | bytes 49160 | tf_op jit(solution)/shard_map/ppermute | solution.py:335
  18.0 2.6 %collective-permute-start.2 = (f32[32,128]{1,0:T(8,128)S(1)}, f32[32,128]{1,0:T(8,128)S(1)}, u32[]{:S(2)}, u32[]{:S(2)}) collective-permute-start(f32[32,128]{1,0:T(8,128)S(1)} %get-tuple-element.21), channel_id=1, source_target_pairs={{0,14},{1,15},{2,12},{3,13},{4,10},{5,11},{6,8},{7,9},{16,30},{17,... | collective-permute-start | bytes 49160 | tf_op jit(solution)/shard_map/ppermute | solution.py:335
  19.3 2.1 %collective-permute-start.3 = (f32[32,128]{1,0:T(8,128)S(1)}, f32[32,128]{1,0:T(8,128)S(1)}, u32[]{:S(2)}, u32[]{:S(2)}) collective-permute-start(f32[32,128]{1,0:T(8,128)S(1)} %get-tuple-element.22), channel_id=1, source_target_pairs={{0,192},{1,193},{2,194},{3,195},{4,196},{5,197},{6,198},{7,199},{1... | collective-permute-start | bytes 49160 | tf_op jit(solution)/shard_map/ppermute | solution.py:335
  36.5 106.6 %all-gather.6.cloned.1.call-start = ((), (), s32[]{:S(2)}) async-start(), calls=%async_computation.2 | async-start | bytes 4456448 | tf_op jit(solution)/shard_map/all_gather | solution.py:353
  37.6 12.4 %collective-permute-start.4 = (f32[128,1024]{1,0:T(8,128)S(1)}, f32[128,1024]{1,0:T(8,128)S(1)}, u32[]{:S(2)}, u32[]{:S(2)}) collective-permute-start(f32[128,1024]{1,0:T(8,128)S(1)} %slice.32), channel_id=1, source_target_pairs={{0,192},{16,208},{32,224},{48,240},{64,128},{80,144},{96,160},{112... | collective-permute-start | bytes 1572872 | tf_op jit(solution)/shard_map/ppermute | solution.py:347
  41.1 7.2 %collective-permute-start = (f32[512,128]{1,0:T(8,128)S(1)}, f32[512,128]{1,0:T(8,128)S(1)}, u32[]{:S(2)}, u32[]{:S(2)}) collective-permute-start(f32[512,128]{1,0:T(8,128)S(1)} %slice.27), channel_id=1, source_target_pairs={{0,14},{1,15},{2,12},{3,13},{4,10},{5,11},{6,8},{7,9},{16,30},{17,... | collective-permute-start | bytes 786440 | tf_op jit(solution)/shard_map/ppermute | solution.py:338
  42.8 11.7 %collective-permute-start.5 = (f32[128,1024]{1,0:T(8,128)S(1)}, f32[128,1024]{1,0:T(8,128)S(1)}, u32[]{:S(2)}, u32[]{:S(2)}) collective-permute-start(f32[128,1024]{1,0:T(8,128)S(1)} %slice.32), channel_id=1, source_target_pairs={{0,64},{16,80},{32,96},{48,112},{64,0},{80,16},{96,32},{112,48},{1... | collective-permute-start | bytes 1572872 | tf_op jit(solution)/shard_map/ppermute | solution.py:347
  44.8 18.9 %collective-permute-start.6 = (f32[128,1024]{1,0:T(8,128)S(1)}, f32[128,1024]{1,0:T(8,128)S(1)}, u32[]{:S(2)}, u32[]{:S(2)}) collective-permute-start(f32[128,1024]{1,0:T(8,128)S(1)} %slice.32), channel_id=1, source_target_pairs={{0,128},{16,144},{32,160},{48,176},{64,192},{80,208},{96,224},{112... | collective-permute-start | bytes 1572872 | tf_op jit(solution)/shard_map/ppermute | solution.py:347
  81.7 35.9 %collective-permute-start.7 = (f32[256,1024]{1,0:T(8,128)S(1)}, f32[256,1024]{1,0:T(8,128)S(1)}, u32[]{:S(2)}, u32[]{:S(2)}) collective-permute-start(f32[256,1024]{1,0:T(8,128)S(1)} %pad_maximum_fusion.refs_0_), channel_id=1, source_target_pairs={{16,0},{32,16},{48,32},{0,48},{80,64},{96,80},{112,96},{64,112},{1... | collective-permute-start | bytes 3145736 | tf_op jit(solution)/shard_map/ppermute | solution.py:356
  82.6 35.0 %collective-permute-start.8 = (f32[256,1024]{1,0:T(8,128)S(1)}, f32[256,1024]{1,0:T(8,128)S(1)}, u32[]{:S(2)}, u32[]{:S(2)}) collective-permute-start(f32[256,1024]{1,0:T(8,128)S(1)} %pad_maximum_fusion.refs_0_), channel_id=1, source_target_pairs={{32,0},{48,16},{0,32},{16,48},{96,64},{112,80},{64,96},{80,112},{1... | collective-permute-start | bytes 3145736 | tf_op jit(solution)/shard_map/ppermute | solution.py:356
  84.1 47.6 %collective-permute-start.9 = (f32[256,1024]{1,0:T(8,128)S(1)}, f32[256,1024]{1,0:T(8,128)S(1)}, u32[]{:S(2)}, u32[]{:S(2)}) collective-permute-start(f32[256,1024]{1,0:T(8,128)S(1)} %pad_maximum_fusion.refs_0_), channel_id=1, source_target_pairs={{48,0},{0,16},{16,32},{32,48},{112,64},{64,80},{80,96},{96,112},{1... | collective-permute-start | bytes 3145736 | tf_op jit(solution)/shard_map/ppermute | solution.py:356
Sparse Core Ops, SparseCore 0:
  36.6 44.9 all-gather.3
  83.5 37.2 all-gather.5

commit v8 on v7

--- a/solution.py
+++ b/solution.py
@@ -343,10 +343,9 @@
 
     own = blocked[:BLOCK]
     moves = ([(0, 1), (1, 0)], [(0, 3), (1, 2)], [(0, 2), (1, 3)])
-    got = [
-        lax.ppermute(own, "prow", [(a * SIDE + x, b * SIDE + x) for a, b in move for x in range(SIDE)])
-        for move in moves
-    ]
+    got = []
+    for move in moves:
+        got.append(lax.ppermute(own, "prow", [(a * SIDE + x, b * SIDE + x) for a, b in move for x in range(SIDE)]))
     source = row < 2 * SIDE
     pair = jnp.concatenate([jnp.where(source, own, got[1]), jnp.where(source, got[0], got[2])], 0)
     payload, window, _ = lax.optimization_barrier((payload, window, pair))

time: 162 us -> 162 us (level)
  no operation moved by 1% of the time
where the time goes in v8:
time: 162 us; the launch traced here: 161 us
  Pallas kernels  56.2 us (35%)
  waiting for transfers between devices  47.5 us (29%)
  starting transfers between devices  23.2 us (14%)
  blocking collectives  14.2 us (9%)
  between operations  13.6 us (8%)
  other arithmetic  3.75 us (2%)
  local copies, waits for them, and re-layouts  2.83 us (2%)
    pallas_call x1, Pallas kernels, factor(): pl.pallas_call(factor_kernel, in_specs=[pl.BlockSpec(memory_space=pltpu.S...  33.5 us
    all_gather x1, waiting for transfers between devices, per_device(): window = lax.all_gather(strip.reshape(HALF, BLOCK), 'pcol', axis=0)  17.7 us
    all_to_all x1, blocking collectives, per_device(): lax.all_to_all(jnp.broadcast_to(part, (rows, quarter, BLOCK)), 'prow', 0, 0)  14.2 us
    ppermute x3, waiting for transfers between devices, per_device(): lax.ppermute(pair, 'prow', [(r // SIDE * SIDE + (r + d) % SIDE, r) for r...  14.1 us
    ppermute x3, starting transfers between devices, per_device(): parts.append(lax.ppermute(corner[at:at + quarter], ('prow', 'pcol'), pairs))  13.3 us
    ppermute x3, waiting for transfers between devices, per_device(): lax.ppermute(own, 'prow', [(a * SIDE + x, b * SIDE + x) for a, b in move...  12.6 us
    pallas_call x1, Pallas kernels, apply(): pl.pallas_call(apply_kernel, in_specs=[pl.BlockSpec(memory_space=pltpu.SM...  11.4 us
    pallas_call x1, Pallas kernels, update(): pl.pallas_call(update_kernel, grid=(WIDTH // CHUNK,), in_specs=[pl.BlockS...  11.3 us
  transfers between devices with their start and end apart: 12, of which 6 were waited for; matrix products, arithmetic and copies ran while one was open for 3% of the time, Pallas kernels for 28%

profile of v8, /device:TPU:1, one launch (start us, length us, event | category | flops | bytes accessed | tf_op | source)
XLA Modules:
  0.0 161.3 jit_solution(10818032693058129638)
XLA Ops:
  6.5 0.8 fusion
  7.3 10.7 %collective-permute-start.1 = (f32[32,128]{1,0:T(8,128)S(1)}, f32[32,128]{1,0:T(8,128)S(1)}, u32[]{:S(2)}, u32[]{:S(2)}) collective-permute-start(f32[32,128]{1,0:T(8,128)S(1)} %get-tuple-element.23), channel_id=1, source_target_pairs={{0,206},{1,207},{2,204},{3,205},{4,202},{5,203},{6,200},{7,201},{1... | collective-permute-start | bytes 49160 | tf_op jit(solution)/shard_map/ppermute | solution.py:335
  18.0 1.3 collective-permute-start.2
  19.3 1.3 collective-permute-start.3
  20.7 0.8 collective-permute-done.3
  21.5 0.7 add_select_fusion
  22.2 14.2 %all_to_all.5 = f32[16,32,128]{2,1,0:T(8,128)} all-to-all(f32[16,32,128]{2,1,0:T(8,128)S(1)} %broadcast_in_dim.3), channel_id=1, replica_groups=mesh['prow'=16,'pcol'=16] {'prow'}, dimensions={0} | all-to-all | bytes 524288 | tf_op jit(solution)/shard_map/all_to_all | solution.py:339
  36.5 0.0 all-gather.4.cloned.1.call-update
  36.5 0.0 all-gather.6.cloned.1.call-start
  36.5 1.1 slice.32
  37.6 2.5 %collective-permute-start.4 = (f32[128,1024]{1,0:T(8,128)S(1)}, f32[128,1024]{1,0:T(8,128)S(1)}, u32[]{:S(2)}, u32[]{:S(2)}) collective-permute-start(f32[128,1024]{1,0:T(8,128)S(1)} %slice.32), channel_id=1, source_target_pairs={{0,192},{16,208},{32,224},{48,240},{64,128},{80,144},{96,160},{112... | collective-permute-start | bytes 1572872 | tf_op jit(solution)/shard_map/ppermute | solution.py:348
  40.1 1.0 slice.27
  41.1 1.7 %collective-permute-start = (f32[512,128]{1,0:T(8,128)S(1)}, f32[512,128]{1,0:T(8,128)S(1)}, u32[]{:S(2)}, u32[]{:S(2)}) collective-permute-start(f32[512,128]{1,0:T(8,128)S(1)} %slice.27), channel_id=1, source_target_pairs={{0,14},{1,15},{2,12},{3,13},{4,10},{5,11},{6,8},{7,9},{16,30},{17,... | collective-permute-start | bytes 786440 | tf_op jit(solution)/shard_map/ppermute | solution.py:338
  42.8 1.9 %collective-permute-start.5 = (f32[128,1024]{1,0:T(8,128)S(1)}, f32[128,1024]{1,0:T(8,128)S(1)}, u32[]{:S(2)}, u32[]{:S(2)}) collective-permute-start(f32[128,1024]{1,0:T(8,128)S(1)} %slice.32), channel_id=1, source_target_pairs={{0,64},{16,80},{32,96},{48,112},{64,0},{80,16},{96,32},{112,48},{1... | collective-permute-start | bytes 1572872 | tf_op jit(solution)/shard_map/ppermute | solution.py:348
  44.8 1.3 collective-permute-start.6
  46.1 2.2 %collective-permute-done = f32[512,128]{1,0:T(8,128)S(1)} collective-permute-done((f32[512,128]{1,0:T(8,128)S(1)}, f32[512,128]{1,0:T(8,128)S(1)}, u32[]{:S(2)}, u32[]{:S(2)}) %collective-permute-start) | collective-permute-done | bytes 262176 | tf_op jit(solution)/shard_map/ppermute | solution.py:338
  48.3 1.7 %slice_select_fusion = f32[512,128]{1,0:T(8,128)} fusion(f32[512,128]{1,0:T(8,128)S(1)} %collective-permute-done, f32[1024,1024]{1,0:T(8,128)} %a_ref.1, pred[]{:T(512)S(6)} %lt.8), kind=kLoop, calls=%fused_computation.1 | loop fusion | flops 65536 | bytes 786433 | tf_op jit(solution)/shard_map/jit(_where)/select_n | solution.py:342
  50.0 1.1 broadcast_select_fusion.1
  51.1 3.4 %collective-permute-done.5 = f32[128,1024]{1,0:T(8,128)S(1)} collective-permute-done((f32[128,1024]{1,0:T(8,128)S(1)}, f32[128,1024]{1,0:T(8,128)S(1)}, u32[]{:S(2)}, u32[]{:S(2)}) %collective-permute-start.5) | collective-permute-done | bytes 524320 | tf_op jit(solution)/shard_map/ppermute | solution.py:348
  54.5 9.2 %collective-permute-done.6 = f32[128,1024]{1,0:T(8,128)S(1)} collective-permute-done((f32[128,1024]{1,0:T(8,128)S(1)}, f32[128,1024]{1,0:T(8,128)S(1)}, u32[]{:S(2)}, u32[]{:S(2)}) %collective-permute-start.6) | collective-permute-done | bytes 524320 | tf_op jit(solution)/shard_map/ppermute | solution.py:348
  63.7 0.1 broadcast_select_fusion
  63.8 0.1 pad_maximum_fusion.refs_0_
  63.9 17.7 %all-gather.4.cloned.1.call-done = f32[16,512,128]{2,1,0:T(8,128)} async-done(((f32[1,512,128]{2,1,0:T(8,128)}), f32[16,512,128]{2,1,0:T(8,128)}) %all-gather.4.cloned.1.call-update) | async-done | bytes 4194320 | tf_op jit(solution)/shard_map/all_gather | solution.py:340
  81.6 0.0 all-gather.6.cloned.1.call-update
  81.7 0.1 pad_add_fusion.place_ref
  81.7 0.9 collective-permute-start.7
  82.6 1.5 collective-permute-start.8
  84.1 33.5 %factor.1 = (bf16[1024,1024]{1,0:T(8,128)(2,1)S(1)}, bf16[1024,1024]{1,0:T(8,128)(2,1)S(1)}, f32[128,128]{1,0:T(8,128)S(1)}) custom-call(s32[2]{0:T(128)S(1)} %pad_add_fusion.place_ref, f32[16,4,4,32,128]{4,3,2,1,0:T(8,128)} %bitcast.7), custom_call_target="tpu_custom_call" | custom-call | flops 40000000000 | bytes 8388608 | tf_op jit(solution)/shard_map/factor/pallas_call | solution.py:202
  117.6 14.1 %collective-permute-done.9.refs_3_ = f32[256,1024]{1,0:T(8,128)S(1)} collective-permute-done((f32[256,1024]{1,0:T(8,128)S(1)}, f32[256,1024]{1,0:T(8,128)S(1)}, u32[]{:S(2)}, u32[]{:S(2)}) %collective-permute-start.9) | collective-permute-done | bytes 1048608 | tf_op jit(solution)/shard_map/ppermute | solution.py:355
  131.7 11.4 %apply.1 = (bf16[1024,1024]{1,0:T(8,128)(2,1)}, bf16[1024,1024]{1,0:T(8,128)(2,1)}, f32[128,128]{1,0:T(8,128)}) custom-call(s32[2]{0:T(128)S(1)} %pad_add_fusion.place_ref, bf16[1024,1024]{1,0:T(8,128)(2,1)S(1)} %get-tuple-element.15.mh, bf16[1024,1024]{1,0:T(8,128)(2,1)S(1)} %get-tuple-element.16.ml, f32[128,128]{1,0:T(8,128)S(1)} %get-tuple-element.17.corner_ref, ...), custom_call_target="tpu_custom_call" | custom-call | flops 10000000000 | bytes 8388608 | tf_op jit(solution)/shard_map/apply/pallas_call | solution.py:265
  143.1 0.0 all-gather.6.cloned.1.call-done
  143.1 11.3 %update.1 = f32[1024,1024]{1,0:T(8,128)} custom-call(s32[2]{0:T(128)S(1)} %pad_add_fusion.place_ref, f32[1024,1024]{1,0:T(8,128)} %a_ref.1, f32[16,512,128]{2,1,0:T(8,128)} %bitcast.5, bf16[1024,1024]{1,0:T(8,128)(2,1)} %get-tuple-element.18.yh_ref, bf16[1024,1024]{1,0:T(8,128)(2,1)} %get-tuple-element.19.yl_ref, f32[128,128]{1,0:T(8,128)} %get-tuple-element.20.corner_ref), custom_call_target="tpu_custom_call" | custom-call | tf_op jit(solution)/shard_map/update/pallas_call | solution.py:301
  (8 shorter events, 0.0 us)
Async XLA Ops:
  6.5 75.1 %all-gather.4.cloned.1.call-start = ((), (), s32[]{:S(2)}) async-start(), calls=%async_computation.1 | async-start | bytes 4456448 | tf_op jit(solution)/shard_map/all_gather | solution.py:340
  7.3 13.4 %collective-permute-start.1 = (f32[32,128]{1,0:T(8,128)S(1)}, f32[32,128]{1,0:T(8,128)S(1)}, u32[]{:S(2)}, u32[]{:S(2)}) collective-permute-start(f32[32,128]{1,0:T(8,128)S(1)} %get-tuple-element.23), channel_id=1, source_target_pairs={{0,206},{1,207},{2,204},{3,205},{4,202},{5,203},{6,200},{7,201},{1... | collective-permute-start | bytes 49160 | tf_op jit(solution)/shard_map/ppermute | solution.py:335
  18.0 2.6 %collective-permute-start.2 = (f32[32,128]{1,0:T(8,128)S(1)}, f32[32,128]{1,0:T(8,128)S(1)}, u32[]{:S(2)}, u32[]{:S(2)}) collective-permute-start(f32[32,128]{1,0:T(8,128)S(1)} %get-tuple-element.21), channel_id=1, source_target_pairs={{0,14},{1,15},{2,12},{3,13},{4,10},{5,11},{6,8},{7,9},{16,30},{17,... | collective-permute-start | bytes 49160 | tf_op jit(solution)/shard_map/ppermute | solution.py:335
  19.3 2.1 %collective-permute-start.3 = (f32[32,128]{1,0:T(8,128)S(1)}, f32[32,128]{1,0:T(8,128)S(1)}, u32[]{:S(2)}, u32[]{:S(2)}) collective-permute-start(f32[32,128]{1,0:T(8,128)S(1)} %get-tuple-element.22), channel_id=1, source_target_pairs={{0,192},{1,193},{2,194},{3,195},{4,196},{5,197},{6,198},{7,199},{1... | collective-permute-start | bytes 49160 | tf_op jit(solution)/shard_map/ppermute | solution.py:335
  36.5 106.6 %all-gather.6.cloned.1.call-start = ((), (), s32[]{:S(2)}) async-start(), calls=%async_computation.2 | async-start | bytes 4456448 | tf_op jit(solution)/shard_map/all_gather | solution.py:352
  37.6 12.4 %collective-permute-start.4 = (f32[128,1024]{1,0:T(8,128)S(1)}, f32[128,1024]{1,0:T(8,128)S(1)}, u32[]{:S(2)}, u32[]{:S(2)}) collective-permute-start(f32[128,1024]{1,0:T(8,128)S(1)} %slice.32), channel_id=1, source_target_pairs={{0,192},{16,208},{32,224},{48,240},{64,128},{80,144},{96,160},{112... | collective-permute-start | bytes 1572872 | tf_op jit(solution)/shard_map/ppermute | solution.py:348
  41.1 7.2 %collective-permute-start = (f32[512,128]{1,0:T(8,128)S(1)}, f32[512,128]{1,0:T(8,128)S(1)}, u32[]{:S(2)}, u32[]{:S(2)}) collective-permute-start(f32[512,128]{1,0:T(8,128)S(1)} %slice.27), channel_id=1, source_target_pairs={{0,14},{1,15},{2,12},{3,13},{4,10},{5,11},{6,8},{7,9},{16,30},{17,... | collective-permute-start | bytes 786440 | tf_op jit(solution)/shard_map/ppermute | solution.py:338
  42.8 11.7 %collective-permute-start.5 = (f32[128,1024]{1,0:T(8,128)S(1)}, f32[128,1024]{1,0:T(8,128)S(1)}, u32[]{:S(2)}, u32[]{:S(2)}) collective-permute-start(f32[128,1024]{1,0:T(8,128)S(1)} %slice.32), channel_id=1, source_target_pairs={{0,64},{16,80},{32,96},{48,112},{64,0},{80,16},{96,32},{112,48},{1... | collective-permute-start | bytes 1572872 | tf_op jit(solution)/shard_map/ppermute | solution.py:348
  44.8 18.9 %collective-permute-start.6 = (f32[128,1024]{1,0:T(8,128)S(1)}, f32[128,1024]{1,0:T(8,128)S(1)}, u32[]{:S(2)}, u32[]{:S(2)}) collective-permute-start(f32[128,1024]{1,0:T(8,128)S(1)} %slice.32), channel_id=1, source_target_pairs={{0,128},{16,144},{32,160},{48,176},{64,192},{80,208},{96,224},{112... | collective-permute-start | bytes 1572872 | tf_op jit(solution)/shard_map/ppermute | solution.py:348
  81.7 35.9 %collective-permute-start.7 = (f32[256,1024]{1,0:T(8,128)S(1)}, f32[256,1024]{1,0:T(8,128)S(1)}, u32[]{:S(2)}, u32[]{:S(2)}) collective-permute-start(f32[256,1024]{1,0:T(8,128)S(1)} %pad_maximum_fusion.refs_0_), channel_id=1, source_target_pairs={{16,0},{32,16},{48,32},{0,48},{80,64},{96,80},{112,96},{64,112},{1... | collective-permute-start | bytes 3145736 | tf_op jit(solution)/shard_map/ppermute | solution.py:355
  82.6 35.0 %collective-permute-start.8 = (f32[256,1024]{1,0:T(8,128)S(1)}, f32[256,1024]{1,0:T(8,128)S(1)}, u32[]{:S(2)}, u32[]{:S(2)}) collective-permute-start(f32[256,1024]{1,0:T(8,128)S(1)} %pad_maximum_fusion.refs_0_), channel_id=1, source_target_pairs={{32,0},{48,16},{0,32},{16,48},{96,64},{112,80},{64,96},{80,112},{1... | collective-permute-start | bytes 3145736 | tf_op jit(solution)/shard_map/ppermute | solution.py:355
  84.1 47.6 %collective-permute-start.9 = (f32[256,1024]{1,0:T(8,128)S(1)}, f32[256,1024]{1,0:T(8,128)S(1)}, u32[]{:S(2)}, u32[]{:S(2)}) collective-permute-start(f32[256,1024]{1,0:T(8,128)S(1)} %pad_maximum_fusion.refs_0_), channel_id=1, source_target_pairs={{48,0},{0,16},{16,32},{32,48},{112,64},{64,80},{80,96},{96,112},{1... | collective-permute-start | bytes 3145736 | tf_op jit(solution)/shard_map/ppermute | solution.py:355
Sparse Core Ops, SparseCore 0:
  36.6 44.9 all-gather.3
  83.5 37.2 all-gather.5
